TPU v7x, 32 devices: a whole 2x2x4 slice. The times are simulated.
32 devices in a mesh: groups: 2 (over y), seq: 4 (over z), head: 4 (over x, core).
Axes of the slice: x: 2, y: 2, z: 4, core: 2. Of those that a mesh axis runs over, the one named last changes fastest.
Arguments:
- tokens: bfloat16 [4096, 4096], P(('groups', 'seq')), parts along dimension 0, may hold values from -24 to 24
- proj_weight: bfloat16 [3, 4096, 2048], P(None, 'seq', 'head'), may hold values from -1 to 1
- cluster_ids: int32 [16, 4096, 1], P('head', ('groups', 'seq')), parts along dimension 1, may hold values from 0 to 255; in each aligned block of 512 rows (0 to 511, 512 to 1023, ..., all dimensions but the last counted through in order) at most 4 rows name the same one
- centroids: float32 [32, 256, 128], P(('groups', 'head'), 'seq'), parts along dimension 0, may hold values from -3 to 3
Outputs:
- context: bfloat16 [4096, 2048], P(('groups', 'seq'), 'head'), parts along dimension 0
- new_centroids: float32 [32, 256, 128], P(('groups', 'head'), 'seq'), parts along dimension 0
There are 2 independent parts, one for each index of `groups`. A program takes and returns all parts, laid end to end along the dimension named above; an argument that names none is the same for every part. Nothing has to cross between parts.
Inputs may be any that keep to these rules, and one draw needn't show every extreme that they name: `cluster_ids`: for each head, no cluster is named by more than 4 of the 512 tokens of one aligned block (one index of seq); some blocks reach 4.
All inputs are finite; a program needn't handle non-finite values.
Results may differ from a plain program's by a relative error of at most 0.018.
Values may be sent and summed in bfloat16 or wider, within the bound.
No kernel may reach another device: no remote copies, remote signals or barrier semaphores. Data moves between devices by JAX's collectives and lax.ppermute only.
A program may use at most 64 MiB of HBM per device.

v0:
```python
import jax
import jax.numpy as jnp
from jax import lax
from jax.experimental import pallas as pl
from jax.experimental.pallas import tpu as pltpu
from jax.sharding import PartitionSpec as P

SLOTS = 4
CORES = 2


def routed(tokens, proj_weight, cluster_ids, centroids):
    owners = lax.axis_size("seq")
    local_rows = tokens.shape[0]
    hs = centroids.shape[2]
    clusters = centroids.shape[1] * owners
    columns = proj_weight.shape[2]
    head_count = columns // hs
    owned = clusters // owners
    capacity = owners * SLOTS
    score_scale = hs ** (-0.5)
    projected = jnp.einsum(
        "td,pdc->ptc",
        tokens,
        lax.all_gather(proj_weight, "seq", axis=1, tiled=True),
        preferred_element_type=jnp.float32,
    ).astype(jnp.bfloat16)
    per_head = projected.reshape(3, local_rows, head_count, hs).transpose(2, 1, 0, 3)
    packed = per_head.reshape(head_count, local_rows, 3 * hs)
    member = cluster_ids[:, :, 0]
    labels = jnp.arange(clusters, dtype=jnp.int32)
    onehot = (member[:, :, None] == labels[None, None, :]).astype(jnp.bfloat16)
    ordinal_rows = jnp.arange(local_rows, dtype=jnp.int32)
    earlier = (ordinal_rows[None, :] < ordinal_rows[:, None]).astype(jnp.bfloat16)
    before = jnp.einsum("ts,hsc->htc", earlier, onehot, preferred_element_type=jnp.float32)
    ranking = jnp.take_along_axis(before, member[:, :, None], axis=2)[:, :, 0].astype(jnp.int32)
    placed = member * SLOTS + ranking
    head_index = jnp.arange(head_count, dtype=jnp.int32)[:, None]
    outbox = (
        jnp.zeros((head_count, clusters * SLOTS, 3 * hs), jnp.bfloat16)
        .at[head_index, placed]
        .set(packed)
    )
    outbox = outbox.reshape(head_count, owners, owned * SLOTS, 3 * hs)
    local_counts = jnp.sum(onehot, axis=1, dtype=jnp.float32)
    tallies = local_counts.astype(jnp.int32).reshape(head_count, owners, owned)
    blocks = lax.all_to_all(outbox, "seq", split_axis=1, concat_axis=1, tiled=True)
    arrived = lax.all_to_all(tallies, "seq", split_axis=1, concat_axis=1, tiled=True)
    arranged = (
        blocks.reshape(head_count, owners, owned, SLOTS, 3 * hs)
        .transpose(0, 2, 1, 3, 4)
        .reshape(head_count, owned, capacity, 3 * hs)
    )
    filled = jnp.arange(SLOTS, dtype=jnp.int32)[None, None, None, :] < arrived[:, :, :, None]
    filled = filled.transpose(0, 2, 1, 3).reshape(head_count, owned, capacity)
    queries = arranged[:, :, :, :hs]
    key_block = arranged[:, :, :, hs : 2 * hs]
    value_block = arranged[:, :, :, 2 * hs :]
    scores = (
        jnp.einsum("hcqd,hckd->hcqk", queries, key_block, preferred_element_type=jnp.float32)
        * score_scale
    )
    ordinal = jnp.arange(capacity, dtype=jnp.int32)
    causal = ordinal[None, None, None, :] <= ordinal[None, None, :, None]
    itself = ordinal[None, None, None, :] == ordinal[None, None, :, None]
    allowed = filled[:, :, None, :] & causal | itself
    scores = jnp.where(allowed, scores, -1e30)
    row_max = jnp.max(scores, axis=3, keepdims=True)
    raised = jnp.exp(scores - row_max)
    weights = (raised / jnp.sum(raised, axis=3, keepdims=True)).astype(jnp.bfloat16)
    attended = jnp.einsum(
        "hcqk,hckd->hcqd", weights, value_block, preferred_element_type=jnp.float32
    ).astype(jnp.bfloat16)
    attended = (
        attended.reshape(head_count, owned, owners, SLOTS, hs)
        .transpose(0, 2, 1, 3, 4)
        .reshape(head_count, owners, owned * SLOTS, hs)
    )
    returned = lax.all_to_all(attended, "seq", split_axis=1, concat_axis=1, tiled=True)
    key_sums = jnp.einsum(
        "hck,hckd->hcd", filled.astype(jnp.bfloat16), key_block, preferred_element_type=jnp.float32
    )
    counts = jnp.sum(filled, axis=2).astype(jnp.float32)
    gathered = returned.reshape(head_count, clusters * SLOTS, hs)
    mine = jax.vmap(lambda table, where: table[where])(gathered, placed)
    context = mine.transpose(1, 0, 2).reshape(local_rows, head_count * hs)
    updated = 0.25 * centroids + 0.75 * key_sums / jnp.maximum(counts, 1.0)[:, :, None]
    return (context, updated)


def attend_kernel(hs, local_rows, qkv_ref, id_col_ref, id_row_ref, out_ref):
    rows = qkv_ref.shape[0]
    owned = out_ref.shape[1] - local_rows
    block = min(256, local_rows)
    scale = hs ** (-0.5)
    for start in range(0, rows, block):
        stop = start + block
        queries = qkv_ref[start:stop, :hs]
        keys = qkv_ref[:stop, hs : 2 * hs]
        values = qkv_ref[:stop, 2 * hs :]
        scores = lax.dot_general(
            queries, keys, (((1,), (1,)), ((), ())), preferred_element_type=jnp.float32
        )
        allowed = id_col_ref[start:stop, :] == id_row_ref[:, :stop]
        row_at = lax.broadcasted_iota(jnp.int32, (block, stop), 0) + start
        col_at = lax.broadcasted_iota(jnp.int32, (block, stop), 1)
        scores = jnp.where(allowed & (col_at <= row_at), scores * scale, -1e30)
        raised = jnp.exp(scores - jnp.max(scores, axis=1, keepdims=True))
        total = jnp.sum(raised, axis=1, keepdims=True)
        mixed = jnp.dot(raised.astype(jnp.bfloat16), values, preferred_element_type=jnp.float32)
        at = start % local_rows
        out_ref[start // local_rows, at : at + block, :] = (mixed / total).astype(out_ref.dtype)
    keys = qkv_ref[:, hs : 2 * hs]
    for owner in range(out_ref.shape[0]):
        label = lax.broadcasted_iota(jnp.int32, (owned, rows), 0) + owner * owned
        onehot = (label == id_row_ref[...]).astype(jnp.float32)
        counts = jnp.sum(onehot, axis=1, keepdims=True)
        sums = jnp.dot(onehot.astype(jnp.bfloat16), keys, preferred_element_type=jnp.float32)
        mean = 0.75 * sums / jnp.maximum(counts, 1.0)
        out_ref[owner, local_rows:, :] = mean.astype(out_ref.dtype)


def attend(qkv, id_col, id_row, seq, owned, hs):
    rows = qkv.shape[0]
    local_rows = rows // seq
    return pl.pallas_call(
        lambda *refs: attend_kernel(hs, local_rows, *refs),
        out_shape=jax.ShapeDtypeStruct((seq, local_rows + owned, hs), jnp.bfloat16),
        cost_estimate=pl.CostEstimate(
            flops=2 * rows * rows * hs, bytes_accessed=rows * hs * 8, transcendentals=rows * rows
        ),
        name="attend",
    )(qkv, id_col, id_row)


def arrivals(size):
    table = []
    for z in range(size):
        order = []
        for step in range(1, size):
            if step <= z:
                order.append((0, step))
            if step <= size - 1 - z:
                order.append((1, step))
        table.append(order)
    return table


def copy_kernel(place, in_ref, out_ref):
    out_ref[...] = in_ref[...]


def take(tokens, place, rows, width, stride):
    depth = tokens.shape[1]
    runs, per = depth // stride, stride // width
    return pl.pallas_call(
        copy_kernel,
        out_shape=jax.ShapeDtypeStruct((rows, runs * width), tokens.dtype),
        grid_spec=pltpu.PrefetchScalarGridSpec(
            num_scalar_prefetch=1,
            grid=(runs,),
            in_specs=[pl.BlockSpec((rows, width), lambda i, p: (p[0], i * per + p[1]))],
            out_specs=pl.BlockSpec((rows, width), lambda i, p: (0, i)),
        ),
        cost_estimate=pl.CostEstimate(
            flops=0, bytes_accessed=4 * rows * runs * width, transcendentals=0
        ),
        name="take",
    )(place, tokens)


def unpack_kernel(hs, place, in_ref, out_ref):
    for head in range(out_ref.shape[0]):
        for which in range(3):
            out_ref[head, :, which * hs : (which + 1) * hs] = in_ref[
                which, :, head * hs : (head + 1) * hs
            ]


def unpack(weight, place, rows, hs):
    heads = weight.shape[2] // hs
    steps = 2 if rows % 32 == 0 else 1
    return pl.pallas_call(
        lambda *refs: unpack_kernel(hs, *refs),
        out_shape=jax.ShapeDtypeStruct((heads, rows, 3 * hs), weight.dtype),
        grid_spec=pltpu.PrefetchScalarGridSpec(
            num_scalar_prefetch=1,
            grid=(steps,),
            in_specs=[
                pl.BlockSpec(
                    (3, rows // steps, heads * hs), lambda i, p: (0, p[0] * steps + i, 0)
                )
            ],
            out_specs=pl.BlockSpec((heads, rows // steps, 3 * hs), lambda i, p: (0, i, 0)),
        ),
        cost_estimate=pl.CostEstimate(
            flops=0, bytes_accessed=12 * rows * heads * hs, transcendentals=0
        ),
        name="unpack",
    )(place, weight)


def by_head(tokens, proj_weight, cluster_ids, centroids):
    seq, heads, groups = (lax.axis_size(a) for a in ("seq", "head", "groups"))
    z, h, y = (lax.axis_index(a) for a in ("seq", "head", "groups"))
    core, x, xs = h % CORES, h // CORES, heads // CORES
    local_rows, _ = tokens.shape
    hs = centroids.shape[2]
    slice_depth = proj_weight.shape[1]
    half = slice_depth // CORES
    part = half // groups
    rows = local_rows // xs
    width = 3 * hs
    zero = jnp.int32(0)
    tie = lax.optimization_barrier

    def swap_core(v):
        return lax.ppermute(v, "head", [(i, i ^ 1) for i in range(heads)])

    def shift_x(v, d):
        pairs = [(i, (i // CORES + d) % xs * CORES + i % CORES) for i in range(heads)]
        return lax.ppermute(v, "head", pairs)

    def shift_y(v, d):
        return lax.ppermute(v, "groups", [(i, (i + d) % groups) for i in range(groups)])

    def shift_z(v, d):
        return lax.ppermute(v, "seq", [(i, (i + d) % seq) for i in range(seq)])

    def line_z(v, d):
        pairs = [(i, i + d) for i in range(seq) if 0 <= i + d < seq]
        return lax.ppermute(v, "seq", pairs)

    mine = take(tokens, jnp.stack([x, core]).astype(jnp.int32), rows, half, slice_depth)
    right, left = [(mine,)], [(mine,)]
    right.append((line_z(mine, 1),))
    left.append((line_z(mine, -1),))

    mine, weight, tokens = tie((mine, proj_weight, tokens))
    given = unpack(weight, jnp.stack([(1 - core) * groups + y]).astype(jnp.int32), part, hs)
    given = swap_core(given)
    kept = unpack(weight, jnp.stack([core * groups + y]).astype(jnp.int32), part, hs)
    own = take(tokens, jnp.stack([zero, core]).astype(jnp.int32), local_rows, half, slice_depth)
    both = jnp.concatenate([kept, given], axis=2)
    member = lax.all_to_all(cluster_ids[:, :, 0], "seq", split_axis=0, concat_axis=0, tiled=True)
    id_row = member.reshape(1, seq * local_rows)
    id_col = member.reshape(seq * local_rows, 1)

    right[1], left[1], both = tie((right[1], left[1], both))
    for step in range(2, seq):
        chunks = 2 if step == seq - 1 and rows % 32 == 0 else 1
        for way, d in ((right, 1), (left, -1)):
            parts = [p for v in way[-1] for p in jnp.split(v, chunks // len(way[-1]), axis=0)]
            way.append(tuple(line_z(p, d) for p in parts))
    pieces = []
    for d in sorted(range(seq), key=lambda d: min(d, seq - d)):
        piece = lax.dynamic_index_in_dim(both, (z + d) % seq, 0, keepdims=False)
        pieces.append((d, shift_z(piece, d) if d else piece))
    matrix = jnp.zeros((seq, groups, part, CORES * width), jnp.bfloat16)
    for d, piece in pieces:
        for g in range(groups):
            moved = shift_y(piece, g) if g else piece
            at = ((z - d) % seq, (y - g) % groups, zero, zero)
            matrix = lax.dynamic_update_slice(matrix, moved[None, None], at)
    matrix = matrix.reshape(seq * half, CORES * width)

    table = arrivals(seq)

    def project(block):
        return jnp.dot(block, matrix, preferred_element_type=jnp.float32)

    def finish(full):
        theirs = swap_core(full[:, width:])
        return (full[:, :width] + theirs).astype(jnp.bfloat16)

    qkv = jnp.zeros((seq, local_rows, width), jnp.bfloat16)
    qkv = lax.dynamic_update_slice(qkv, finish(project(own))[None], (z, zero, zero))
    last = None
    for k in range(seq - 1):
        picks = {}
        for at in range(seq):
            picks.setdefault(table[at][k], []).append(at)
        chunks = max(len((right, left)[a][b]) for a, b in picks)
        size = rows // chunks
        for chunk in range(chunks):
            block, source = None, None
            values = []
            for direction, step in picks:
                value = (right, left)[direction][step]
                if len(value) == chunks:
                    values.append(value[chunk])
                else:
                    values.append(value[0][chunk * size : (chunk + 1) * size])
            if last is not None:
                values, last = tie((values, last))
            for value, ((direction, step), where) in zip(values, picks.items()):
                origin = z + (step if direction else -step)
                if block is None:
                    block, source = value, origin
                else:
                    chosen = sum((z == at).astype(jnp.int32) for at in where) > 0
                    block = jnp.where(chosen, value, block)
                    source = jnp.where(chosen, origin, source)
            parts = [block] + [shift_x(block, d) for d in range(1, xs)]
            last = block
            done = finish(jnp.concatenate([project(p) for p in parts], axis=0))
            for d in range(xs):
                at = (source, (x - d) % xs * rows + chunk * size, zero)
                qkv = lax.dynamic_update_slice(qkv, done[d * size : (d + 1) * size][None], at)
    qkv = qkv.reshape(seq * local_rows, width)

    owned = centroids.shape[1]
    mixed = attend(qkv, id_col, id_row, seq, owned, hs)
    mixed = lax.all_to_all(mixed, "seq", split_axis=0, concat_axis=0, tiled=True)
    context = mixed[:, :local_rows].transpose(1, 0, 2).reshape(local_rows, seq * hs)
    updated = 0.25 * centroids + mixed[:, local_rows:].astype(jnp.float32)
    return (context, updated)


def local(tokens, proj_weight, cluster_ids, centroids):
    seq, heads = lax.axis_size("seq"), lax.axis_size("head")
    if cluster_ids.shape[0] == seq and heads % CORES == 0:
        return by_head(tokens, proj_weight, cluster_ids, centroids)
    return routed(tokens, proj_weight, cluster_ids, centroids)


def solution(mesh):
    return jax.shard_map(
        local,
        mesh=mesh,
        in_specs=(
            P(("groups", "seq"), None),
            P(None, "seq", "head"),
            P("head", ("groups", "seq"), None),
            P(("groups", "head"), "seq", None),
        ),
        out_specs=(P(("groups", "seq"), "head"), P(("groups", "head"), "seq", None)),
        check_vma=False,
    )
```

profile of v0, /device:TPU:0, one launch (start us, length us, event | category | flops | bytes accessed | tf_op | source)
XLA Modules:
  0.0 222.3 jit_solution(2001393936478526092)
XLA Ops:
  1.2 4.1 %take.2 = bf16[256,2048]{1,0:T(8,128)(2,1)} custom-call(s32[2]{0:T(128)} %pad_add_fusion.1.place, bf16[512,4096]{1,0:T(8,128)(2,1)} %in_ref.2), custom_call_target="tpu_custom_call" | custom-call | bytes 2097152 | tf_op jit(solution)/shard_map/take/pallas_call | solution.py:156
  5.3 5.0 %collective-permute-start = (bf16[256,2048]{1,0:T(8,128)(2,1)}, bf16[256,2048]{1,0:T(8,128)(2,1)S(1)}, u32[]{:S(2)}, u32[]{:S(2)}) collective-permute-start(bf16[256,2048]{1,0:T(8,128)(2,1)} %take.2), channel_id=1, source_target_pairs={{0,4},{4,8},{8,12},{1,5},{5,9},{9,13},{2,6},{6,10},{10,14},{3,7},{... | collective-permute-start | bytes 3145736 | tf_op jit(solution)/shard_map/ppermute | solution.py:232
  10.3 1.3 collective-permute-start.1
  11.6 2.0 unpack.3
  13.7 5.9 %all-to-all-start = ((s32[4,1,512]{2,1,0:T(1,128)}), s32[4,1,512]{2,1,0:T(1,128)S(1)}, u32[]{:S(2)}, u32[]{:S(2)}) async-start(s32[4,1,512]{2,1,0:T(1,128)} %bitcast.27), calls=%async_computation | async-start | bytes 16384 | tf_op jit(solution)/shard_map/all_to_all | solution.py:245
  20.2 2.0 unpack.2
  22.1 4.7 %take.3 = bf16[512,2048]{1,0:T(8,128)(2,1)} custom-call(s32[2]{0:T(128)} %pad_add_fusion.place, bf16[512,4096]{1,0:T(8,128)(2,1)} %in_ref.2), custom_call_target="tpu_custom_call" | custom-call | bytes 4194304 | tf_op jit(solution)/shard_map/take/pallas_call | solution.py:156
  26.8 12.3 %all-to-all-done = s32[4,1,512]{2,1,0:T(1,128)S(1)} async-done(((s32[4,1,512]{2,1,0:T(1,128)}), s32[4,1,512]{2,1,0:T(1,128)S(1)}, u32[]{:S(2)}, u32[]{:S(2)}) %all-to-all-start) | async-done | bytes 8224 | tf_op jit(solution)/shard_map/all_to_all | solution.py:245
  39.1 1.4 copy.6.refs_1_
  40.5 1.3 pad_maximum_fusion
  41.8 1.3 collective-permute-start.13
  43.1 4.6 %collective-permute-start.14 = (bf16[256,2048]{1,0:T(8,128)(2,1)S(1)}, bf16[256,2048]{1,0:T(8,128)(2,1)S(1)}, u32[]{:S(2)}, u32[]{:S(2)}) collective-permute-start(bf16[256,2048]{1,0:T(8,128)(2,1)S(1)} %collective-permute-done), channel_id=1, source_target_pairs={{0,4},{4,8},{8,12},{1,5},{5,9},{9,13},{2,6},{6,10},{10,14},{3,7},{... | collective-permute-start | bytes 3145736 | tf_op jit(solution)/shard_map/ppermute | solution.py:232
  47.8 1.6 collective-permute-start.3
  49.9 3.3 %collective-permute-start.6 = (bf16[256,768]{1,0:T(8,128)(2,1)S(1)}, bf16[256,768]{1,0:T(8,128)(2,1)S(1)}, u32[]{:S(2)}, u32[]{:S(2)}) collective-permute-start(bf16[256,768]{1,0:T(8,128)(2,1)S(1)} %get-tuple-element.38), channel_id=1, source_target_pairs={{0,12},{4,0},{8,4},{12,8},{1,13},{5,1},{9,5},{13,9},{2,14},{6,2},{... | collective-permute-start | bytes 1179656 | tf_op jit(solution)/shard_map/ppermute | solution.py:228
  53.6 3.1 %collective-permute-done.3 = bf16[256,768]{1,0:T(8,128)(2,1)S(1)} collective-permute-done((bf16[256,768]{1,0:T(8,128)(2,1)S(1)}, bf16[256,768]{1,0:T(8,128)(2,1)S(1)}, u32[]{:S(2)}, u32[]{:S(2)}) %collective-permute-start.3) | collective-permute-done | bytes 393248 | tf_op jit(solution)/shard_map/ppermute | solution.py:225
  56.7 0.9 collective-permute-start.8
  57.6 22.0 %collective-permute-done.4 = bf16[256,768]{1,0:T(8,128)(2,1)S(1)} collective-permute-done((bf16[256,768]{1,0:T(8,128)(2,1)S(1)}, bf16[256,768]{1,0:T(8,128)(2,1)S(1)}, u32[]{:S(2)}, u32[]{:S(2)}) %collective-permute-start.4) | collective-permute-done | bytes 393248 | tf_op jit(solution)/shard_map/ppermute | solution.py:228
  79.6 1.5 collective-permute-start.5
  81.2 6.9 %collective-permute-done.6 = bf16[256,768]{1,0:T(8,128)(2,1)S(1)} collective-permute-done((bf16[256,768]{1,0:T(8,128)(2,1)S(1)}, bf16[256,768]{1,0:T(8,128)(2,1)S(1)}, u32[]{:S(2)}, u32[]{:S(2)}) %collective-permute-start.6) | collective-permute-done | bytes 393248 | tf_op jit(solution)/shard_map/ppermute | solution.py:228
  88.0 1.5 collective-permute-start.11
  89.5 11.3 %collective-permute-done.8 = bf16[256,768]{1,0:T(8,128)(2,1)S(1)} collective-permute-done((bf16[256,768]{1,0:T(8,128)(2,1)S(1)}, bf16[256,768]{1,0:T(8,128)(2,1)S(1)}, u32[]{:S(2)}, u32[]{:S(2)}) %collective-permute-start.8) | collective-permute-done | bytes 393248 | tf_op jit(solution)/shard_map/ppermute | solution.py:228
  100.9 1.5 collective-permute-start.7
  103.0 9.9 %collective-permute-done.7 = bf16[256,768]{1,0:T(8,128)(2,1)S(1)} collective-permute-done((bf16[256,768]{1,0:T(8,128)(2,1)S(1)}, bf16[256,768]{1,0:T(8,128)(2,1)S(1)}, u32[]{:S(2)}, u32[]{:S(2)}) %collective-permute-start.7) | collective-permute-done | bytes 393248 | tf_op jit(solution)/shard_map/ppermute | solution.py:225
  112.9 4.9 %collective-permute-done.9 = bf16[256,768]{1,0:T(8,128)(2,1)S(1)} collective-permute-done((bf16[256,768]{1,0:T(8,128)(2,1)S(1)}, bf16[256,768]{1,0:T(8,128)(2,1)S(1)}, u32[]{:S(2)}, u32[]{:S(2)}) %collective-permute-start.9) | collective-permute-done | bytes 393248 | tf_op jit(solution)/shard_map/ppermute | solution.py:225
  117.9 1.8 fusion.25
  119.9 1.0 fusion.26
  121.0 1.3 collective-permute-start.17
  122.4 6.4 %collective-permute-start.18 = (bf16[128,2048]{1,0:T(8,128)(2,1)S(1)}, bf16[128,2048]{1,0:T(8,128)(2,1)S(1)}, u32[]{:S(2)}, u32[]{:S(2)}) collective-permute-start(bf16[128,2048]{1,0:T(8,128)(2,1)S(1)} %get-tuple-element.27), channel_id=1, source_target_pairs={{0,4},{4,8},{8,12},{1,5},{5,9},{9,13},{2,6},{6,10},{10,14},{3,7},{... | collective-permute-start | bytes 1572872 | tf_op jit(solution)/shard_map/ppermute | solution.py:232
  128.7 1.3 collective-permute-start.21
  130.3 1.0 fusion.28
  131.3 4.8 %collective-permute-start.22 = (bf16[128,2048]{1,0:T(8,128)(2,1)S(1)}, bf16[128,2048]{1,0:T(8,128)(2,1)S(1)}, u32[]{:S(2)}, u32[]{:S(2)}) collective-permute-start(bf16[128,2048]{1,0:T(8,128)(2,1)S(1)} %get-tuple-element.31), channel_id=1, source_target_pairs={{0,4},{4,8},{8,12},{1,5},{5,9},{9,13},{2,6},{6,10},{10,14},{3,7},{... | collective-permute-start | bytes 1572872 | tf_op jit(solution)/shard_map/ppermute | solution.py:232
  136.1 1.0 fusion.27
  137.1 2.3 %collective-permute-done.17 = bf16[128,2048]{1,0:T(8,128)(2,1)S(1)} collective-permute-done((bf16[128,2048]{1,0:T(8,128)(2,1)S(1)}, bf16[128,2048]{1,0:T(8,128)(2,1)S(1)}, u32[]{:S(2)}, u32[]{:S(2)}) %collective-permute-start.17) | collective-permute-done | bytes 524320 | tf_op jit(solution)/shard_map/ppermute | solution.py:232
  139.4 1.5 collective-permute-start.15
  141.1 9.4 %collective-permute-done.21 = bf16[128,2048]{1,0:T(8,128)(2,1)S(1)} collective-permute-done((bf16[128,2048]{1,0:T(8,128)(2,1)S(1)}, bf16[128,2048]{1,0:T(8,128)(2,1)S(1)}, u32[]{:S(2)}, u32[]{:S(2)}) %collective-permute-start.21) | collective-permute-done | bytes 524320 | tf_op jit(solution)/shard_map/ppermute | solution.py:232
  150.5 1.5 collective-permute-start.19
  152.1 1.3 collective-permute-start.23
  154.3 0.6 fusion.30
  155.1 10.4 %collective-permute-done.15 = bf16[256,2048]{1,0:T(8,128)(2,1)S(1)} collective-permute-done((bf16[256,2048]{1,0:T(8,128)(2,1)S(1)}, bf16[256,2048]{1,0:T(8,128)(2,1)S(1)}, u32[]{:S(2)}, u32[]{:S(2)}) %collective-permute-start.15) | collective-permute-done | bytes 1048608 | tf_op jit(solution)/shard_map/ppermute | solution.py:222
  165.5 1.0 fusion.29
  166.6 20.1 %collective-permute-done.23 = bf16[128,2048]{1,0:T(8,128)(2,1)S(1)} collective-permute-done((bf16[128,2048]{1,0:T(8,128)(2,1)S(1)}, bf16[128,2048]{1,0:T(8,128)(2,1)S(1)}, u32[]{:S(2)}, u32[]{:S(2)}) %collective-permute-start.23) | collective-permute-done | bytes 524320 | tf_op jit(solution)/shard_map/ppermute | solution.py:222
  187.4 0.6 fusion.31
  189.2 0.8 collective-permute-done.20
  190.4 1.2 copy-done.2
  191.6 8.5 %attend.1 = bf16[4,576,128]{2,1,0:T(8,128)(2,1)} custom-call(bf16[2048,384]{1,0:T(8,128)(2,1)} %bitcast.100, s32[2048,1]{1,0:T(8,128)} %copy.6.refs_1_, s32[1,2048]{1,0:T(1,128)} %bitcast.102), custom_call_target="tpu_custom_call" | custom-call | flops 1073741824 | bytes 2097152 | tf_op jit(solution)/shard_map/attend/pallas_call | solution.py:126
  200.1 20.3 %all_to_all.14 = bf16[4,576,128]{2,1,0:T(8,128)(2,1)S(1)} all-to-all(bf16[4,576,128]{2,1,0:T(8,128)(2,1)} %attend.1), channel_id=1, replica_groups=mesh['groups'=2,'seq'=4,'head'=4] {'seq'}, dimensions={0} | all-to-all | bytes 1179648 | tf_op jit(solution)/shard_map/all_to_all | solution.py:314
  220.6 1.0 copy.8
  221.6 0.7 convert_add_fusion
  (72 shorter events, 7.3 us)
Async XLA Ops:
  5.3 36.4 %collective-permute-start = (bf16[256,2048]{1,0:T(8,128)(2,1)}, bf16[256,2048]{1,0:T(8,128)(2,1)S(1)}, u32[]{:S(2)}, u32[]{:S(2)}) collective-permute-start(bf16[256,2048]{1,0:T(8,128)(2,1)} %take.2), channel_id=1, source_target_pairs={{0,4},{4,8},{8,12},{1,5},{5,9},{9,13},{2,6},{6,10},{10,14},{3,7},{... | collective-permute-start | bytes 3145736 | tf_op jit(solution)/shard_map/ppermute | solution.py:232
  10.3 31.4 %collective-permute-start.1 = (bf16[256,2048]{1,0:T(8,128)(2,1)}, bf16[256,2048]{1,0:T(8,128)(2,1)S(1)}, u32[]{:S(2)}, u32[]{:S(2)}) collective-permute-start(bf16[256,2048]{1,0:T(8,128)(2,1)} %take.2), channel_id=1, source_target_pairs={{4,0},{8,4},{12,8},{5,1},{9,5},{13,9},{6,2},{10,6},{14,10},{7,3},{... | collective-permute-start | bytes 3145736 | tf_op jit(solution)/shard_map/ppermute | solution.py:232
  13.6 26.8 %collective-permute-start.2 = (bf16[4,256,384]{2,1,0:T(8,128)(2,1)}, bf16[4,256,384]{2,1,0:T(8,128)(2,1)}, u32[]{:S(2)}, u32[]{:S(2)}) collective-permute-start(bf16[4,256,384]{2,1,0:T(8,128)(2,1)} %unpack.3), channel_id=1, source_target_pairs={{0,1},{1,0},{2,3},{3,2},{4,5},{5,4},{6,7},{7,6},{8,9},{9,8},{10,11... | collective-permute-start | bytes 2359304 | tf_op jit(solution)/shard_map/ppermute | solution.py:218
  13.7 25.4 %all-to-all-start = ((s32[4,1,512]{2,1,0:T(1,128)}), s32[4,1,512]{2,1,0:T(1,128)S(1)}, u32[]{:S(2)}, u32[]{:S(2)}) async-start(s32[4,1,512]{2,1,0:T(1,128)} %bitcast.27), calls=%async_computation | async-start | bytes 16384 | tf_op jit(solution)/shard_map/all_to_all | solution.py:245
  22.1 18.3 %copy-start = (bf16[4,256,384]{2,1,0:T(8,128)(2,1)S(1)}, bf16[4,256,384]{2,1,0:T(8,128)(2,1)}, u32[]{:S(2)}) copy-start(bf16[4,256,384]{2,1,0:T(8,128)(2,1)} %unpack.2) | copy-start | bytes 2359300
  39.1 8.7 %copy-start.4 = (s32[4,1,512]{2,1,0:T(1,128)}, s32[4,1,512]{2,1,0:T(1,128)S(1)}, u32[]{:S(2)}) copy-start(s32[4,1,512]{2,1,0:T(1,128)S(1)} %all-to-all-done) | copy-start | bytes 24580
  41.8 79.1 %collective-permute-start.13 = (bf16[256,2048]{1,0:T(8,128)(2,1)S(1)}, bf16[256,2048]{1,0:T(8,128)(2,1)S(1)}, u32[]{:S(2)}, u32[]{:S(2)}) collective-permute-start(bf16[256,2048]{1,0:T(8,128)(2,1)S(1)} %collective-permute-done.1), channel_id=1, source_target_pairs={{4,0},{8,4},{12,8},{5,1},{9,5},{13,9},{6,2},{10,6},{14,10},{7,3},{... | collective-permute-start | bytes 3145736 | tf_op jit(solution)/shard_map/ppermute | solution.py:232
  43.1 77.8 %collective-permute-start.14 = (bf16[256,2048]{1,0:T(8,128)(2,1)S(1)}, bf16[256,2048]{1,0:T(8,128)(2,1)S(1)}, u32[]{:S(2)}, u32[]{:S(2)}) collective-permute-start(bf16[256,2048]{1,0:T(8,128)(2,1)S(1)} %collective-permute-done), channel_id=1, source_target_pairs={{0,4},{4,8},{8,12},{1,5},{5,9},{9,13},{2,6},{6,10},{10,14},{3,7},{... | collective-permute-start | bytes 3145736 | tf_op jit(solution)/shard_map/ppermute | solution.py:232
  47.8 8.9 %collective-permute-start.3 = (bf16[256,768]{1,0:T(8,128)(2,1)S(1)}, bf16[256,768]{1,0:T(8,128)(2,1)S(1)}, u32[]{:S(2)}, u32[]{:S(2)}) collective-permute-start(bf16[256,768]{1,0:T(8,128)(2,1)S(1)} %get-tuple-element.37), channel_id=1, source_target_pairs={{0,16},{16,0},{1,17},{17,1},{2,18},{18,2},{3,19},{19,3},{4,20},{20... | collective-permute-start | bytes 1179656 | tf_op jit(solution)/shard_map/ppermute | solution.py:225
  49.4 30.2 %collective-permute-start.4 = (bf16[256,768]{1,0:T(8,128)(2,1)S(1)}, bf16[256,768]{1,0:T(8,128)(2,1)S(1)}, u32[]{:S(2)}, u32[]{:S(2)}) collective-permute-start(bf16[256,768]{1,0:T(8,128)(2,1)S(1)} %get-tuple-element.39), channel_id=1, source_target_pairs={{0,4},{4,8},{8,12},{12,0},{1,5},{5,9},{9,13},{13,1},{2,6},{6,10},{... | collective-permute-start | bytes 1179656 | tf_op jit(solution)/shard_map/ppermute | solution.py:228
  49.9 38.1 %collective-permute-start.6 = (bf16[256,768]{1,0:T(8,128)(2,1)S(1)}, bf16[256,768]{1,0:T(8,128)(2,1)S(1)}, u32[]{:S(2)}, u32[]{:S(2)}) collective-permute-start(bf16[256,768]{1,0:T(8,128)(2,1)S(1)} %get-tuple-element.38), channel_id=1, source_target_pairs={{0,12},{4,0},{8,4},{12,8},{1,13},{5,1},{9,5},{13,9},{2,14},{6,2},{... | collective-permute-start | bytes 1179656 | tf_op jit(solution)/shard_map/ppermute | solution.py:228
  53.6 64.3 %copy-start.1 = (bf16[512,2048]{1,0:T(8,128)(2,1)S(1)}, bf16[512,2048]{1,0:T(8,128)(2,1)}, u32[]{:S(2)}) copy-start(bf16[512,2048]{1,0:T(8,128)(2,1)} %take.3) | copy-start | bytes 6291460
  56.7 44.2 %collective-permute-start.8 = (bf16[256,768]{1,0:T(8,128)(2,1)S(1)}, bf16[256,768]{1,0:T(8,128)(2,1)S(1)}, u32[]{:S(2)}, u32[]{:S(2)}) collective-permute-start(bf16[256,768]{1,0:T(8,128)(2,1)S(1)} %get-tuple-element.36), channel_id=1, source_target_pairs={{0,8},{4,12},{8,0},{12,4},{1,9},{5,13},{9,1},{13,5},{2,10},{6,14},... | collective-permute-start | bytes 1179656 | tf_op jit(solution)/shard_map/ppermute | solution.py:228
  79.6 22.8 %collective-permute-start.5 = (bf16[256,768]{1,0:T(8,128)(2,1)S(1)}, bf16[256,768]{1,0:T(8,128)(2,1)S(1)}, u32[]{:S(2)}, u32[]{:S(2)}) collective-permute-start(bf16[256,768]{1,0:T(8,128)(2,1)S(1)} %collective-permute-done.4), channel_id=1, source_target_pairs={{0,16},{16,0},{1,17},{17,1},{2,18},{18,2},{3,19},{19,3},{4,20},{20... | collective-permute-start | bytes 1179656 | tf_op jit(solution)/shard_map/ppermute | solution.py:225
  88.0 43.2 %collective-permute-start.11 = (bf16[256,2048]{1,0:T(8,128)(2,1)S(1)}, bf16[256,2048]{1,0:T(8,128)(2,1)S(1)}, u32[]{:S(2)}, u32[]{:S(2)}) collective-permute-start(bf16[256,2048]{1,0:T(8,128)(2,1)S(1)} %broadcast_select_fusion), channel_id=1, source_target_pairs={{0,2},{1,3},{2,0},{3,1},{4,6},{5,7},{6,4},{7,5},{8,10},{9,11},{10,... | collective-permute-start | bytes 3145736 | tf_op jit(solution)/shard_map/ppermute | solution.py:222
  100.9 12.0 %collective-permute-start.7 = (bf16[256,768]{1,0:T(8,128)(2,1)S(1)}, bf16[256,768]{1,0:T(8,128)(2,1)S(1)}, u32[]{:S(2)}, u32[]{:S(2)}) collective-permute-start(bf16[256,768]{1,0:T(8,128)(2,1)S(1)} %collective-permute-done.6), channel_id=1, source_target_pairs={{0,16},{16,0},{1,17},{17,1},{2,18},{18,2},{3,19},{19,3},{4,20},{20... | collective-permute-start | bytes 1179656 | tf_op jit(solution)/shard_map/ppermute | solution.py:225
  102.4 15.5 %collective-permute-start.9 = (bf16[256,768]{1,0:T(8,128)(2,1)S(1)}, bf16[256,768]{1,0:T(8,128)(2,1)S(1)}, u32[]{:S(2)}, u32[]{:S(2)}) collective-permute-start(bf16[256,768]{1,0:T(8,128)(2,1)S(1)} %collective-permute-done.8), channel_id=1, source_target_pairs={{0,16},{16,0},{1,17},{17,1},{2,18},{18,2},{3,19},{19,3},{4,20},{20... | collective-permute-start | bytes 1179656 | tf_op jit(solution)/shard_map/ppermute | solution.py:225
  119.8 34.3 %collective-permute-start.10 = (f32[512,384]{1,0:T(8,128)S(1)}, f32[512,384]{1,0:T(8,128)S(1)}, u32[]{:S(2)}, u32[]{:S(2)}) collective-permute-start(f32[512,384]{1,0:T(8,128)S(1)} %slice.91), channel_id=1, source_target_pairs={{0,1},{1,0},{2,3},{3,2},{4,5},{5,4},{6,7},{7,6},{8,9},{9,8},{10,11... | collective-permute-start | bytes 2359304 | tf_op jit(solution)/shard_map/ppermute | solution.py:218
  121.0 18.5 %collective-permute-start.17 = (bf16[128,2048]{1,0:T(8,128)(2,1)S(1)}, bf16[128,2048]{1,0:T(8,128)(2,1)S(1)}, u32[]{:S(2)}, u32[]{:S(2)}) collective-permute-start(bf16[128,2048]{1,0:T(8,128)(2,1)S(1)} %get-tuple-element.28), channel_id=1, source_target_pairs={{4,0},{8,4},{12,8},{5,1},{9,5},{13,9},{6,2},{10,6},{14,10},{7,3},{... | collective-permute-start | bytes 1572872 | tf_op jit(solution)/shard_map/ppermute | solution.py:232
  122.4 18.6 %collective-permute-start.18 = (bf16[128,2048]{1,0:T(8,128)(2,1)S(1)}, bf16[128,2048]{1,0:T(8,128)(2,1)S(1)}, u32[]{:S(2)}, u32[]{:S(2)}) collective-permute-start(bf16[128,2048]{1,0:T(8,128)(2,1)S(1)} %get-tuple-element.27), channel_id=1, source_target_pairs={{0,4},{4,8},{8,12},{1,5},{5,9},{9,13},{2,6},{6,10},{10,14},{3,7},{... | collective-permute-start | bytes 1572872 | tf_op jit(solution)/shard_map/ppermute | solution.py:232
  128.7 21.8 %collective-permute-start.21 = (bf16[128,2048]{1,0:T(8,128)(2,1)S(1)}, bf16[128,2048]{1,0:T(8,128)(2,1)S(1)}, u32[]{:S(2)}, u32[]{:S(2)}) collective-permute-start(bf16[128,2048]{1,0:T(8,128)(2,1)S(1)} %get-tuple-element.32), channel_id=1, source_target_pairs={{4,0},{8,4},{12,8},{5,1},{9,5},{13,9},{6,2},{10,6},{14,10},{7,3},{... | collective-permute-start | bytes 1572872 | tf_op jit(solution)/shard_map/ppermute | solution.py:232
  131.3 20.7 %collective-permute-start.22 = (bf16[128,2048]{1,0:T(8,128)(2,1)S(1)}, bf16[128,2048]{1,0:T(8,128)(2,1)S(1)}, u32[]{:S(2)}, u32[]{:S(2)}) collective-permute-start(bf16[128,2048]{1,0:T(8,128)(2,1)S(1)} %get-tuple-element.31), channel_id=1, source_target_pairs={{0,4},{4,8},{8,12},{1,5},{5,9},{9,13},{2,6},{6,10},{10,14},{3,7},{... | collective-permute-start | bytes 1572872 | tf_op jit(solution)/shard_map/ppermute | solution.py:232
  139.4 26.0 %collective-permute-start.15 = (bf16[256,2048]{1,0:T(8,128)(2,1)S(1)}, bf16[256,2048]{1,0:T(8,128)(2,1)S(1)}, u32[]{:S(2)}, u32[]{:S(2)}) collective-permute-start(bf16[256,2048]{1,0:T(8,128)(2,1)S(1)} %select_select_fusion), channel_id=1, source_target_pairs={{0,2},{1,3},{2,0},{3,1},{4,6},{5,7},{6,4},{7,5},{8,10},{9,11},{10,... | collective-permute-start | bytes 3145736 | tf_op jit(solution)/shard_map/ppermute | solution.py:222
  141.0 14.0 %collective-permute-start.12 = (f32[512,384]{1,0:T(8,128)S(1)}, f32[512,384]{1,0:T(8,128)S(1)}, u32[]{:S(2)}, u32[]{:S(2)}) collective-permute-start(f32[512,384]{1,0:T(8,128)S(1)} %pad_maximum_fusion.2), channel_id=1, source_target_pairs={{0,1},{1,0},{2,3},{3,2},{4,5},{5,4},{6,7},{7,6},{8,9},{9,8},{10,11... | collective-permute-start | bytes 2359304 | tf_op jit(solution)/shard_map/ppermute | solution.py:218
  150.5 36.9 %collective-permute-start.19 = (bf16[128,2048]{1,0:T(8,128)(2,1)S(1)}, bf16[128,2048]{1,0:T(8,128)(2,1)S(1)}, u32[]{:S(2)}, u32[]{:S(2)}) collective-permute-start(bf16[128,2048]{1,0:T(8,128)(2,1)S(1)} %select_select_fusion.2), channel_id=1, source_target_pairs={{0,2},{1,3},{2,0},{3,1},{4,6},{5,7},{6,4},{7,5},{8,10},{9,11},{10,... | collective-permute-start | bytes 1572872 | tf_op jit(solution)/shard_map/ppermute | solution.py:222
  152.1 34.6 %collective-permute-start.23 = (bf16[128,2048]{1,0:T(8,128)(2,1)S(1)}, bf16[128,2048]{1,0:T(8,128)(2,1)S(1)}, u32[]{:S(2)}, u32[]{:S(2)}) collective-permute-start(bf16[128,2048]{1,0:T(8,128)(2,1)S(1)} %select_select_fusion.1), channel_id=1, source_target_pairs={{0,2},{1,3},{2,0},{3,1},{4,6},{5,7},{6,4},{7,5},{8,10},{9,11},{10,... | collective-permute-start | bytes 1572872 | tf_op jit(solution)/shard_map/ppermute | solution.py:222
  166.6 23.5 %collective-permute-start.16 = (f32[512,384]{1,0:T(8,128)S(1)}, f32[512,384]{1,0:T(8,128)S(1)}, u32[]{:S(2)}, u32[]{:S(2)}) collective-permute-start(f32[512,384]{1,0:T(8,128)S(1)} %pad_maximum_fusion.1), channel_id=1, source_target_pairs={{0,1},{1,0},{2,3},{3,2},{4,5},{5,4},{6,7},{7,6},{8,9},{9,8},{10,11... | collective-permute-start | bytes 2359304 | tf_op jit(solution)/shard_map/ppermute | solution.py:218
  187.4 1.8 collective-permute-start.24
  188.1 1.9 collective-permute-start.20
  190.4 1.2 copy-start.2
  200.0 21.6 %copy-start.3 = (f32[4,64,128]{2,1,0:T(8,128)S(1)}, f32[4,64,128]{2,1,0:T(8,128)}, u32[]{:S(2)}) copy-start(f32[4,64,128]{2,1,0:T(8,128)} %param.7) | copy-start | bytes 393220
where the time goes:
time: 223 us; the launch traced here: 222 us
  waiting for transfers between devices  114 us (51%)
  starting transfers between devices  48.3 us (22%)
  Pallas kernels  21.2 us (10%)
  blocking collectives  20.3 us (9%)
  matrix products  8.17 us (4%)
  local copies, waits for them, and re-layouts  4.98 us (2%)
  other arithmetic  4.28 us (2%)
    ppermute x3, waiting for transfers between devices, shift_z(): return lax.ppermute(v, 'seq', [(i, (i + d) % seq) for i in range(seq)])  40.2 us
    ppermute x4, waiting for transfers between devices, shift_x(): return lax.ppermute(v, 'head', pairs)  30.5 us
    ppermute x8, starting transfers between devices, line_z(): return lax.ppermute(v, 'seq', pairs)  25.9 us
    all_to_all x1, blocking collectives, by_head(): lax.all_to_all(mixed, 'seq', split_axis=0, concat_axis=0, tiled=True)  20.3 us
    ppermute x4, waiting for transfers between devices, shift_y(): lax.ppermute(v, 'groups', [(i, (i + d) % groups) for i in range(groups)])  17.9 us
    all_to_all x1, waiting for transfers between devices, by_head(): lax.all_to_all(cluster_ids[:, :, 0], 'seq', split_axis=0, concat_axis=0,...  12.3 us
    ppermute x8, waiting for transfers between devices, line_z(): return lax.ppermute(v, 'seq', pairs)  11.8 us
    pallas_call x2, Pallas kernels, take(): pl.pallas_call(copy_kernel, out_shape=jax.ShapeDtypeStruct((rows, runs *...  8.76 us
  transfers between devices with their start and end apart: 26, of which 13 were waited for; matrix products, arithmetic and copies ran while one was open for 6% of the time, Pallas kernels for 4%

commit v1 on v0

--- a/solution.py
+++ b/solution.py
@@ -7,6 +7,7 @@
 
 SLOTS = 4
 CORES = 2
+SMALL_VMEM = 16 << 20
 
 
 def routed(tokens, proj_weight, cluster_ids, centroids):
@@ -88,49 +89,270 @@
     return (context, updated)
 
 
-def attend_kernel(hs, local_rows, qkv_ref, id_col_ref, id_row_ref, out_ref):
+def attend_kernel(hs, local_rows, place, qkv_ref, id_col_ref, id_row_ref, out_ref):
     rows = qkv_ref.shape[0]
-    owned = out_ref.shape[1] - local_rows
+    owned = out_ref.shape[0] - local_rows
     block = min(256, local_rows)
     scale = hs ** (-0.5)
-    for start in range(0, rows, block):
-        stop = start + block
-        queries = qkv_ref[start:stop, :hs]
-        keys = qkv_ref[:stop, hs : 2 * hs]
-        values = qkv_ref[:stop, 2 * hs :]
-        scores = lax.dot_general(
-            queries, keys, (((1,), (1,)), ((), ())), preferred_element_type=jnp.float32
+    at = place[0] * local_rows
+
+    for first in range(0, local_rows, block):
+        here = pl.multiple_of(at + first, block)
+        queries = qkv_ref[pl.ds(here, block), :hs]
+        ids = id_col_ref[pl.ds(here, block), :]
+
+        def scores_of(start, size):
+            keys = qkv_ref[pl.ds(start, size), hs : 2 * hs]
+            scores = lax.dot_general(
+                queries, keys, (((1,), (1,)), ((), ())), preferred_element_type=jnp.float32
+            )
+            return scores * scale, ids == id_row_ref[:, pl.ds(start, size)]
+
+        def mix(raised, start, size):
+            values = qkv_ref[pl.ds(start, size), 2 * hs :]
+            return jnp.dot(raised.astype(jnp.bfloat16), values, preferred_element_type=jnp.float32)
+
+        size = first + block
+        base = pl.multiple_of(at, local_rows)
+        scores, allowed = scores_of(base, size)
+        row_at = lax.broadcasted_iota(jnp.int32, (block, size), 0) + first
+        col_at = lax.broadcasted_iota(jnp.int32, (block, size), 1)
+        scores = jnp.where(allowed & (col_at <= row_at), scores, -1e30)
+        peak = jnp.max(scores, axis=1, keepdims=True)
+        raised = jnp.exp(scores - peak)
+        total = jnp.sum(raised, axis=1, keepdims=True)
+        mixed = mix(raised, base, size)
+
+        def earlier(j, carry):
+            peak, total, mixed = carry
+            start = pl.multiple_of(j * local_rows, local_rows)
+            scores, allowed = scores_of(start, local_rows)
+            scores = jnp.where(allowed, scores, -1e30)
+            higher = jnp.maximum(peak, jnp.max(scores, axis=1, keepdims=True))
+            kept = jnp.exp(peak - higher)
+            raised = jnp.exp(scores - higher)
+            total = total * kept + jnp.sum(raised, axis=1, keepdims=True)
+            return higher, total, mixed * kept + mix(raised, start, local_rows)
+
+        _, total, mixed = lax.fori_loop(0, place[0], earlier, (peak, total, mixed))
+        out_ref[first : first + block, :] = (mixed / total).astype(out_ref.dtype)
+    label = lax.broadcasted_iota(jnp.int32, (owned, rows), 0) + place[0] * owned
+    onehot = (label == id_row_ref[...]).astype(jnp.float32)
+    counts = jnp.sum(onehot, axis=1, keepdims=True)
+    keys = qkv_ref[:, hs : 2 * hs]
+    sums = jnp.dot(onehot.astype(jnp.bfloat16), keys, preferred_element_type=jnp.float32)
+    mean = 0.75 * sums / jnp.maximum(counts, 1.0)
+    out_ref[local_rows:, :] = mean.astype(out_ref.dtype)
+
+
+def whole(shape):
+    return pl.BlockSpec(shape, lambda i, p: (0,) * len(shape))
+
+
+def attend(place, qkv, id_col, id_row, seq, owned, hs):
+    rows = qkv.shape[0]
+    shape = (rows // seq + owned, hs)
+    return pl.pallas_call(
+        lambda *refs: attend_kernel(hs, rows // seq, *refs),
+        out_shape=jax.ShapeDtypeStruct(shape, jnp.bfloat16),
+        grid_spec=pltpu.PrefetchScalarGridSpec(
+            num_scalar_prefetch=1,
+            grid=(1,),
+            in_specs=[whole(v.shape) for v in (qkv, id_col, id_row)],
+            out_specs=whole(shape),
+        ),
+        compiler_params=pltpu.CompilerParams(vmem_limit_bytes=SMALL_VMEM),
+        cost_estimate=pl.CostEstimate(
+            flops=rows * rows * hs, bytes_accessed=rows * hs * 8, transcendentals=rows * rows // 4
+        ),
+        name="attend",
+    )(place, qkv, id_col, id_row)
+
+
+def collect_kernel(hs, local_rows, place, *refs):
+    *pieces, centroid_ref, context_ref, updated_ref = refs
+    for d, piece in enumerate(pieces):
+        source = place[d]
+        columns = pl.ds(pl.multiple_of(source * hs, hs), hs)
+        context_ref[:, columns] = piece[:local_rows, :]
+        mean = piece[local_rows:, :].astype(jnp.float32)
+        updated_ref[source] = 0.25 * centroid_ref[source] + mean
+
+
+def collect(place, pieces, centroids, local_rows):
+    hs = centroids.shape[2]
+    shape = (local_rows, len(pieces) * hs)
+    return pl.pallas_call(
+        lambda *refs: collect_kernel(hs, local_rows, *refs),
+        out_shape=(
+            jax.ShapeDtypeStruct(shape, jnp.bfloat16),
+            jax.ShapeDtypeStruct(centroids.shape, jnp.float32),
+        ),
+        grid_spec=pltpu.PrefetchScalarGridSpec(
+            num_scalar_prefetch=1,
+            grid=(1,),
+            in_specs=[whole(v.shape) for v in (*pieces, centroids)],
+            out_specs=[whole(shape), whole(centroids.shape)],
+        ),
+        compiler_params=pltpu.CompilerParams(vmem_limit_bytes=SMALL_VMEM),
+        cost_estimate=pl.CostEstimate(flops=0, bytes_accessed=1 << 20, transcendentals=0),
+        name="collect",
+    )(place, *pieces, centroids)
+
+
+def choose(index, values):
+    chosen = values[0]
+    for i, value in enumerate(values[1:], 1):
+        chosen = jnp.where(index == i, value, chosen)
+    return chosen
+
+
+def project_kernel(counts, spots, *refs):
+    weights, tokens = refs[: counts[0]], refs[counts[0] : sum(counts)]
+    kept_ref, sent_ref, matrix, held, weight_sem, token_sem = refs[sum(counts) :]
+    step = pl.program_id(0)
+    block, width = kept_ref.shape
+    part = weights[0].shape[0]
+    copies, row = {}, 0
+    for i, ref in enumerate(tokens):
+        to = held.at[row : row + ref.shape[0], :]
+        copy = pltpu.make_async_copy(ref, to, token_sem.at[i])
+        copies.setdefault(row // block, []).append(copy)
+        row += ref.shape[0]
+
+    @pl.when(step == 0)
+    def _():
+        loads = []
+        for i, ref in enumerate(weights):
+            to = matrix.at[pl.ds(pl.multiple_of(spots[i] * part, part), part), :]
+            loads.append(pltpu.make_async_copy(ref, to, weight_sem.at[i]))
+        loads += copies[0]
+        for copy in loads:
+            copy.start()
+        for copy in loads:
+            copy.wait()
+        for at, group in copies.items():
+            for copy in group if at else []:
+                copy.start()
+
+    for at, group in copies.items():
+
+        @pl.when(step == at)
+        def _(group=group):
+            for copy in group if at else []:
+                copy.wait()
+
+    left = held[pl.ds(pl.multiple_of(step * block, block), block), :]
+    full = jnp.dot(left, matrix[...], preferred_element_type=jnp.float32)
+    kept_ref[...] = full[:, :width]
+    sent_ref[...] = full[:, width:].astype(sent_ref.dtype)
+
+
+def project(spots, weights, tokens, block):
+    depth = weights[0].shape[0] * len(weights)
+    width = weights[0].shape[1] // CORES
+    total = sum(v.shape[0] for v in tokens)
+    counts = len(weights), len(tokens)
+    return pl.pallas_call(
+        lambda *refs: project_kernel(counts, *refs),
+        out_shape=(
+            jax.ShapeDtypeStruct((total, width), jnp.float32),
+            jax.ShapeDtypeStruct((total, width), jnp.bfloat16),
+        ),
+        grid_spec=pltpu.PrefetchScalarGridSpec(
+            num_scalar_prefetch=1,
+            grid=(total // block,),
+            in_specs=[pl.BlockSpec(memory_space=pl.ANY)] * sum(counts),
+            out_specs=[pl.BlockSpec((block, width), lambda i, p: (i, 0))] * 2,
+            scratch_shapes=[
+                pltpu.VMEM((depth, CORES * width), jnp.bfloat16),
+                pltpu.VMEM((total, depth), jnp.bfloat16),
+                pltpu.SemaphoreType.DMA((counts[0],)),
+                pltpu.SemaphoreType.DMA((counts[1],)),
+            ],
+        ),
+        compiler_params=pltpu.CompilerParams(dimension_semantics=("arbitrary",)),
+        cost_estimate=pl.CostEstimate(
+            flops=2 * total * depth * CORES * width,
+            bytes_accessed=2 * depth * (total + CORES * width) + 8 * total * width,
+            transcendentals=0,
+        ),
+        name="project",
+    )(spots, *weights, *tokens)
+
+
+def merge_kernel(block, place, kept_hbm, theirs_hbm, out_ref, kept, theirs, sems):
+    count = kept.shape[0] // block
+    copies = []
+    for i in range(count):
+        down = pl.ds(i * block, block)
+        pair = (
+            pltpu.make_async_copy(kept_hbm.at[down], kept.at[down], sems.at[0, i]),
+            pltpu.make_async_copy(theirs_hbm.at[down], theirs.at[down], sems.at[1, i]),
         )
-        allowed = id_col_ref[start:stop, :] == id_row_ref[:, :stop]
-        row_at = lax.broadcasted_iota(jnp.int32, (block, stop), 0) + start
-        col_at = lax.broadcasted_iota(jnp.int32, (block, stop), 1)
-        scores = jnp.where(allowed & (col_at <= row_at), scores * scale, -1e30)
-        raised = jnp.exp(scores - jnp.max(scores, axis=1, keepdims=True))
-        total = jnp.sum(raised, axis=1, keepdims=True)
-        mixed = jnp.dot(raised.astype(jnp.bfloat16), values, preferred_element_type=jnp.float32)
-        at = start % local_rows
-        out_ref[start // local_rows, at : at + block, :] = (mixed / total).astype(out_ref.dtype)
-    keys = qkv_ref[:, hs : 2 * hs]
-    for owner in range(out_ref.shape[0]):
-        label = lax.broadcasted_iota(jnp.int32, (owned, rows), 0) + owner * owned
-        onehot = (label == id_row_ref[...]).astype(jnp.float32)
-        counts = jnp.sum(onehot, axis=1, keepdims=True)
-        sums = jnp.dot(onehot.astype(jnp.bfloat16), keys, preferred_element_type=jnp.float32)
-        mean = 0.75 * sums / jnp.maximum(counts, 1.0)
-        out_ref[owner, local_rows:, :] = mean.astype(out_ref.dtype)
-
-
-def attend(qkv, id_col, id_row, seq, owned, hs):
-    rows = qkv.shape[0]
-    local_rows = rows // seq
-    return pl.pallas_call(
-        lambda *refs: attend_kernel(hs, local_rows, *refs),
-        out_shape=jax.ShapeDtypeStruct((seq, local_rows + owned, hs), jnp.bfloat16),
+        for copy in pair:
+            copy.start()
+        copies.append(pair)
+    for i, pair in enumerate(copies):
+        for copy in pair:
+            copy.wait()
+        here = slice(i * block, (i + 1) * block)
+        both = kept[here, :] + theirs[here, :].astype(jnp.float32)
+        to = pl.ds(pl.multiple_of(place[i] * block, block), block)
+        out_ref[to, :] = both.astype(out_ref.dtype)
+
+
+def merge(at, kept, theirs, total, block):
+    rows, width = kept.shape
+    anywhere = pl.BlockSpec(memory_space=pl.ANY)
+    return pl.pallas_call(
+        lambda *refs: merge_kernel(block, *refs),
+        out_shape=jax.ShapeDtypeStruct((total, width), jnp.bfloat16),
+        grid_spec=pltpu.PrefetchScalarGridSpec(
+            num_scalar_prefetch=1,
+            grid=(1,),
+            in_specs=[anywhere, anywhere],
+            out_specs=whole((total, width)),
+            scratch_shapes=[
+                pltpu.VMEM((rows, width), kept.dtype),
+                pltpu.VMEM((rows, width), theirs.dtype),
+                pltpu.SemaphoreType.DMA((2, rows // block)),
+            ],
+        ),
         cost_estimate=pl.CostEstimate(
-            flops=2 * rows * rows * hs, bytes_accessed=rows * hs * 8, transcendentals=rows * rows
-        ),
-        name="attend",
-    )(qkv, id_col, id_row)
+            flops=kept.size, bytes_accessed=8 * kept.size, transcendentals=0
+        ),
+        name="merge",
+    )(jnp.stack(at).astype(jnp.int32), kept, theirs)
+
+
+def merge_more_kernel(place, kept_ref, theirs_ref, base_ref, out_ref):
+    theirs = theirs_ref[...].astype(jnp.float32)
+    out_ref[...] = (kept_ref[...] + theirs).astype(out_ref.dtype)
+
+
+def merge_more(at, kept, theirs, base, block):
+    share = pl.BlockSpec((block, kept.shape[1]), lambda i, p: (i, 0))
+    return pl.pallas_call(
+        merge_more_kernel,
+        out_shape=jax.ShapeDtypeStruct(base.shape, base.dtype),
+        grid_spec=pltpu.PrefetchScalarGridSpec(
+            num_scalar_prefetch=1,
+            grid=(kept.shape[0] // block,),
+            in_specs=[share, share, pl.BlockSpec(memory_space=pl.ANY)],
+            out_specs=pl.BlockSpec((block, kept.shape[1]), lambda i, p: (p[i], 0)),
+        ),
+        input_output_aliases={3: 0},
+        compiler_params=pltpu.CompilerParams(vmem_limit_bytes=SMALL_VMEM),
+        cost_estimate=pl.CostEstimate(
+            flops=kept.size, bytes_accessed=8 * kept.size, transcendentals=0
+        ),
+        name="merge_more",
+    )(jnp.stack(at).astype(jnp.int32), kept, theirs, base)
+
+
+def nearest(size):
+    return sorted(range(size), key=lambda d: min(d, size - d))
 
 
 def arrivals(size):
@@ -146,27 +368,50 @@
     return table
 
 
-def copy_kernel(place, in_ref, out_ref):
-    out_ref[...] = in_ref[...]
-
-
-def take(tokens, place, rows, width, stride):
-    depth = tokens.shape[1]
-    runs, per = depth // stride, stride // width
-    return pl.pallas_call(
-        copy_kernel,
-        out_shape=jax.ShapeDtypeStruct((rows, runs * width), tokens.dtype),
-        grid_spec=pltpu.PrefetchScalarGridSpec(
-            num_scalar_prefetch=1,
-            grid=(runs,),
-            in_specs=[pl.BlockSpec((rows, width), lambda i, p: (p[0], i * per + p[1]))],
-            out_specs=pl.BlockSpec((rows, width), lambda i, p: (0, i)),
+def take_kernel(runs, stride, place, in_ref, *refs):
+    *outs, arrived = refs
+    width = outs[0].shape[1] // runs
+    first = place[0] * sum(out_ref.shape[0] for out_ref in outs)
+    copies = []
+    for n, out_ref in enumerate(outs):
+        rows = out_ref.shape[0]
+        down = pl.ds(pl.multiple_of(first, 16), rows)
+        first = first + rows
+        for i in range(runs):
+            across = pl.ds(pl.multiple_of(i * stride + place[1] * width, width), width)
+            to = out_ref.at[:, i * width : (i + 1) * width]
+            sem = arrived.at[n * runs + i]
+            copies.append(pltpu.make_async_copy(in_ref.at[down, across], to, sem))
+    for copy in copies:
+        copy.start()
+    for copy in copies:
+        copy.wait()
+
+
+def take(tokens, place, sizes, width, stride):
+    runs = tokens.shape[1] // stride
+    shapes = [(size, runs * width) for size in sizes]
+    return pl.pallas_call(
+        lambda *refs: take_kernel(runs, stride, *refs),
+        out_shape=[jax.ShapeDtypeStruct(shape, tokens.dtype) for shape in shapes],
+        grid_spec=pltpu.PrefetchScalarGridSpec(
+            num_scalar_prefetch=1,
+            grid=(1,),
+            in_specs=[pl.BlockSpec(memory_space=pl.ANY)],
+            out_specs=[whole(shape) for shape in shapes],
+            scratch_shapes=[pltpu.SemaphoreType.DMA((len(sizes) * runs,))],
         ),
         cost_estimate=pl.CostEstimate(
-            flops=0, bytes_accessed=4 * rows * runs * width, transcendentals=0
+            flops=0, bytes_accessed=4 * sum(sizes) * runs * width, transcendentals=0
         ),
         name="take",
     )(place, tokens)
+
+
+def chunked(rows):
+    if rows % 32:
+        return (rows,)
+    return (rows // 2 + 16, rows // 2 - 16)
 
 
 def unpack_kernel(hs, place, in_ref, out_ref):
@@ -210,7 +455,6 @@
     half = slice_depth // CORES
     part = half // groups
     rows = local_rows // xs
-    width = 3 * hs
     zero = jnp.int32(0)
     tie = lax.optimization_barrier
 
@@ -227,93 +471,108 @@
     def shift_z(v, d):
         return lax.ppermute(v, "seq", [(i, (i + d) % seq) for i in range(seq)])
 
-    def line_z(v, d):
-        pairs = [(i, i + d) for i in range(seq) if 0 <= i + d < seq]
-        return lax.ppermute(v, "seq", pairs)
-
-    mine = take(tokens, jnp.stack([x, core]).astype(jnp.int32), rows, half, slice_depth)
-    right, left = [(mine,)], [(mine,)]
-    right.append((line_z(mine, 1),))
-    left.append((line_z(mine, -1),))
+    def rightward(step):
+        return [(i, i + 1) for i in range(step - 1, seq - 1)]
+
+    def leftward(step):
+        return [(i, i - 1) for i in range(1, seq - step + 1)]
+
+    sizes = chunked(rows)
+    at = jnp.stack([x, core]).astype(jnp.int32)
+    mine = take(tokens, at, sizes, half, slice_depth)
+    right, left = [mine], [mine]
+    right.append([lax.ppermute(v, "seq", rightward(1)) for v in mine])
+    left.append([lax.ppermute(v, "seq", leftward(1)) for v in mine])
 
     mine, weight, tokens = tie((mine, proj_weight, tokens))
     given = unpack(weight, jnp.stack([(1 - core) * groups + y]).astype(jnp.int32), part, hs)
     given = swap_core(given)
     kept = unpack(weight, jnp.stack([core * groups + y]).astype(jnp.int32), part, hs)
-    own = take(tokens, jnp.stack([zero, core]).astype(jnp.int32), local_rows, half, slice_depth)
+    at = jnp.stack([zero, core]).astype(jnp.int32)
+    (own,) = take(tokens, at, (local_rows,), half, slice_depth)
     both = jnp.concatenate([kept, given], axis=2)
     member = lax.all_to_all(cluster_ids[:, :, 0], "seq", split_axis=0, concat_axis=0, tiled=True)
     id_row = member.reshape(1, seq * local_rows)
     id_col = member.reshape(seq * local_rows, 1)
 
-    right[1], left[1], both = tie((right[1], left[1], both))
-    for step in range(2, seq):
-        chunks = 2 if step == seq - 1 and rows % 32 == 0 else 1
-        for way, d in ((right, 1), (left, -1)):
-            parts = [p for v in way[-1] for p in jnp.split(v, chunks // len(way[-1]), axis=0)]
-            way.append(tuple(line_z(p, d) for p in parts))
     pieces = []
-    for d in sorted(range(seq), key=lambda d: min(d, seq - d)):
+    for d in nearest(seq)[::-1]:
         piece = lax.dynamic_index_in_dim(both, (z + d) % seq, 0, keepdims=False)
         pieces.append((d, shift_z(piece, d) if d else piece))
-    matrix = jnp.zeros((seq, groups, part, CORES * width), jnp.bfloat16)
-    for d, piece in pieces:
-        for g in range(groups):
-            moved = shift_y(piece, g) if g else piece
-            at = ((z - d) % seq, (y - g) % groups, zero, zero)
-            matrix = lax.dynamic_update_slice(matrix, moved[None, None], at)
-    matrix = matrix.reshape(seq * half, CORES * width)
-
     table = arrivals(seq)
-
-    def project(block):
-        return jnp.dot(block, matrix, preferred_element_type=jnp.float32)
-
-    def finish(full):
-        theirs = swap_core(full[:, width:])
-        return (full[:, :width] + theirs).astype(jnp.bfloat16)
-
-    qkv = jnp.zeros((seq, local_rows, width), jnp.bfloat16)
-    qkv = lax.dynamic_update_slice(qkv, finish(project(own))[None], (z, zero, zero))
-    last = None
+    for step in range(1, seq):
+        crossing = 2 * step <= seq + 1
+        if step > 1 and crossing:
+            for way, pairs in ((right, rightward), (left, leftward)):
+                way.append([lax.ppermute(v, "seq", pairs(step)) for v in way[-1]])
+        elif step > 1:
+            sent, forward = [], (z >= step - 1).astype(jnp.int32)
+            for ways in zip(left[-1], right[-1]):
+                if sent:
+                    ways, _ = tie((ways, sent[-1]))
+                sent.append(choose(forward, ways))
+            pairs = rightward(step) + leftward(step)
+            got = [lax.ppermute(v, "seq", pairs) for v in sent]
+            right.append(got)
+            left.append(got)
+
+    arrived, sources, last = [], [], None
     for k in range(seq - 1):
         picks = {}
         for at in range(seq):
             picks.setdefault(table[at][k], []).append(at)
-        chunks = max(len((right, left)[a][b]) for a, b in picks)
-        size = rows // chunks
-        for chunk in range(chunks):
-            block, source = None, None
-            values = []
-            for direction, step in picks:
-                value = (right, left)[direction][step]
-                if len(value) == chunks:
-                    values.append(value[chunk])
-                else:
-                    values.append(value[0][chunk * size : (chunk + 1) * size])
+        index, source = jnp.int32(0), jnp.int32(0)
+        for i, ((direction, step), where) in enumerate(picks.items()):
+            chosen = sum((z == at).astype(jnp.int32) for at in where) > 0
+            index = jnp.where(chosen, i, index)
+            source = jnp.where(chosen, z + (step if direction else -step), source)
+        shares = [[] for _ in range(xs)]
+        for chunk in range(len(sizes)):
+            values = [(right, left)[direction][step][chunk] for direction, step in picks]
             if last is not None:
                 values, last = tie((values, last))
-            for value, ((direction, step), where) in zip(values, picks.items()):
-                origin = z + (step if direction else -step)
-                if block is None:
-                    block, source = value, origin
-                else:
-                    chosen = sum((z == at).astype(jnp.int32) for at in where) > 0
-                    block = jnp.where(chosen, value, block)
-                    source = jnp.where(chosen, origin, source)
-            parts = [block] + [shift_x(block, d) for d in range(1, xs)]
-            last = block
-            done = finish(jnp.concatenate([project(p) for p in parts], axis=0))
+            block = last = choose(index, values)
             for d in range(xs):
-                at = (source, (x - d) % xs * rows + chunk * size, zero)
-                qkv = lax.dynamic_update_slice(qkv, done[d * size : (d + 1) * size][None], at)
-    qkv = qkv.reshape(seq * local_rows, width)
+                shares[d].append(shift_x(block, d) if d else block)
+        arrived.append(shares)
+        sources.append(source)
+
+    laid, spots = [], []
+    for d, piece in pieces:
+        for g in range(groups):
+            laid.append(shift_y(piece, g) if g else piece)
+            spots.append((z - d) % seq * groups + (y - g) % groups)
+    spots = jnp.stack(spots).astype(jnp.int32)
+
+    def place(k, d):
+        return sources[k] * xs + (x - d) % xs
+
+    early = [own] + [v for k in range(seq - 2) for share in arrived[k] for v in share]
+    early_at = [z * xs + i for i in range(xs)]
+    early_at += [place(k, d) for k in range(seq - 2) for d in range(xs)]
+    early += arrived[-1][0]
+    early_at.append(place(seq - 2, 0))
+    late = [v for share in arrived[-1][1:] for v in share]
+    late_at = [place(seq - 2, d) for d in range(1, xs)]
+
+    units = 2 * sum(v.shape[0] for v in early) // rows
+    tall = rows // 2 * max(n for n in range(1, units // 2 + 1) if units % n == 0)
+    kept, sent = project(spots, laid, early, tall)
+    theirs = swap_core(sent)
+    qkv = merge(early_at, kept, theirs, seq * local_rows, rows)
+    kept, sent = project(spots, laid, late, rows)
+    theirs = swap_core(sent)
+    qkv = merge_more(late_at, kept, theirs, qkv, rows)
 
     owned = centroids.shape[1]
-    mixed = attend(qkv, id_col, id_row, seq, owned, hs)
-    mixed = lax.all_to_all(mixed, "seq", split_axis=0, concat_axis=0, tiled=True)
-    context = mixed[:, :local_rows].transpose(1, 0, 2).reshape(local_rows, seq * hs)
-    updated = 0.25 * centroids + mixed[:, local_rows:].astype(jnp.float32)
+    back = {}
+    for d in nearest(seq)[::-1]:
+        where = jnp.stack([(z + d) % seq]).astype(jnp.int32)
+        block = attend(where, qkv, id_col, id_row, seq, owned, hs)
+        back[d] = shift_z(block, d) if d else block
+    sources = jnp.stack([(z - d) % seq for d in range(seq)]).astype(jnp.int32)
+    pieces = [back[d] for d in range(seq)]
+    context, updated = collect(sources, pieces, centroids, local_rows)
     return (context, updated)
 
 

time: 223 us -> 222 us (level)
  Pallas kernels: 21.2 us -> 43.4 us
  blocking collectives: 20.3 us -> 0 us
  matrix products: 8.17 us -> 0 us
  local copies, waits for them, and re-layouts: 4.98 us -> 10.6 us
    ppermute x8 -> x10, waiting for transfers between devices: 11.8 us -> 60.1 us  [the longest x2 33.3 us: by_head(): got = [lax.ppermute(v, 'seq', pairs) for v in sent]]
    ppermute x3 -> x6, waiting for transfers between devices: 40.2 us -> 3.96 us  [shift_z(): return lax.ppermute(v, 'seq', [(i, (i + d) % seq) for i in range(seq)])]
    pallas_call x3 -> x11, Pallas kernels: 17.3 us -> 39.4 us  [the longest x2 15.9 us: project(): pl.pallas_call(lambda *refs: project_kernel(counts, *refs), out_shape=(ja...]
    all_to_all x1 -> x0, blocking collectives: 20.3 us -> none  [by_head(): lax.all_to_all(mixed, 'seq', split_axis=0, concat_axis=0, tiled=True)]
    ppermute x3 -> x6, starting transfers between devices: 4.72 us -> 14.3 us  [shift_z(): return lax.ppermute(v, 'seq', [(i, (i + d) % seq) for i in range(seq)])]
    dot_general x9 -> x0, matrix products: 8.17 us -> none  [project(): return jnp.dot(block, matrix, preferred_element_type=jnp.float32)]
    all_to_all x1, waiting for transfers between devices: 12.3 us -> 4.86 us  [by_head(): lax.all_to_all(cluster_ids[:, :, 0], 'seq', split_axis=0, concat_axis=0,...]
    ppermute x4 -> x6, waiting for transfers between devices: 30.5 us -> 23.5 us  [shift_x(): return lax.ppermute(v, 'head', pairs)]
  transfers between devices with their start and end apart: 26 -> 30, of which waited for: 13 -> 12; matrix products, arithmetic and copies ran while one was open for 6% -> 2% of each run, Pallas kernels for 4% -> 11%
where the time goes in v1:
time: 222 us; the launch traced here: 221 us
  waiting for transfers between devices  112 us (50%)
  starting transfers between devices  50.3 us (23%)
  Pallas kernels  43.4 us (20%)
  local copies, waits for them, and re-layouts  10.6 us (5%)
  other arithmetic  3.57 us (2%)
    ppermute x2, waiting for transfers between devices, by_head(): got = [lax.ppermute(v, 'seq', pairs) for v in sent]  33.3 us
    ppermute x6, waiting for transfers between devices, shift_x(): return lax.ppermute(v, 'head', pairs)  23.5 us
    ppermute x4, waiting for transfers between devices, by_head(): way.append([lax.ppermute(v, 'seq', pairs(step)) for v in way[-1]])  20.2 us
    ppermute x4, waiting for transfers between devices, shift_y(): lax.ppermute(v, 'groups', [(i, (i + d) % groups) for i in range(groups)])  19.9 us
    pallas_call x2, Pallas kernels, project(): pl.pallas_call(lambda *refs: project_kernel(counts, *refs), out_shape=(ja...  15.9 us
    ppermute x6, starting transfers between devices, shift_z(): return lax.ppermute(v, 'seq', [(i, (i + d) % seq) for i in range(seq)])  14.3 us
    pallas_call x4, Pallas kernels, attend(): pl.pallas_call(lambda *refs: attend_kernel(hs, rows // seq, *refs), out_s...  11.2 us
    ppermute x2, starting transfers between devices, by_head(): right.append([lax.ppermute(v, 'seq', rightward(1)) for v in mine])  10.2 us
  transfers between devices with their start and end apart: 30, of which 12 were waited for; matrix products, arithmetic and copies ran while one was open for 2% of the time, Pallas kernels for 11%

profile of v1, /device:TPU:0, one launch (start us, length us, event | category | flops | bytes accessed | tf_op | source)
XLA Modules:
  0.0 221.4 jit_solution(13872899729039677711)
XLA Ops:
  1.2 3.0 %take.2 = (bf16[144,2048]{1,0:T(8,128)(2,1)}, bf16[112,2048]{1,0:T(8,128)(2,1)}) custom-call(s32[2]{0:T(128)} %pad_add_fusion.1.refs_0_, bf16[512,4096]{1,0:T(8,128)(2,1)} %refs_1_.4), custom_call_target="tpu_custom_call" | custom-call | bytes 2097152 | tf_op jit(solution)/shard_map/take/pallas_call | solution.py:394
  4.2 1.3 collective-permute-start.10
  5.5 5.6 %collective-permute-start.8 = (bf16[144,2048]{1,0:T(8,128)(2,1)}, bf16[144,2048]{1,0:T(8,128)(2,1)S(1)}, u32[]{:S(2)}, u32[]{:S(2)}) collective-permute-start(bf16[144,2048]{1,0:T(8,128)(2,1)} %get-tuple-element.28), channel_id=1, source_target_pairs={{0,4},{4,8},{8,12},{1,5},{5,9},{9,13},{2,6},{6,10},{10,14},{3,7},{... | collective-permute-start | bytes 1769480 | tf_op jit(solution)/shard_map/ppermute | solution.py:484
  11.2 1.3 collective-permute-start.13
  12.5 4.6 %collective-permute-start.15 = (bf16[112,2048]{1,0:T(8,128)(2,1)}, bf16[112,2048]{1,0:T(8,128)(2,1)S(1)}, u32[]{:S(2)}, u32[]{:S(2)}) collective-permute-start(bf16[112,2048]{1,0:T(8,128)(2,1)} %get-tuple-element.29), channel_id=1, source_target_pairs={{0,4},{4,8},{8,12},{1,5},{5,9},{9,13},{2,6},{6,10},{10,14},{3,7},{... | collective-permute-start | bytes 1376264 | tf_op jit(solution)/shard_map/ppermute | solution.py:484
  17.1 2.0 unpack.3
  19.1 1.9 unpack.2
  21.6 3.6 %take.3.refs_9_ = bf16[512,2048]{1,0:T(8,128)(2,1)} custom-call(s32[2]{0:T(128)} %pad_add_fusion.2.refs_0_, bf16[512,4096]{1,0:T(8,128)(2,1)} %refs_1_.4), custom_call_target="tpu_custom_call" | custom-call | bytes 4194304 | tf_op jit(solution)/shard_map/take/pallas_call | solution.py:394
  25.9 6.7 %collective-permute-done.13 = bf16[112,2048]{1,0:T(8,128)(2,1)S(1)} collective-permute-done((bf16[112,2048]{1,0:T(8,128)(2,1)}, bf16[112,2048]{1,0:T(8,128)(2,1)S(1)}, u32[]{:S(2)}, u32[]{:S(2)}) %collective-permute-start.13) | collective-permute-done | bytes 458784 | tf_op jit(solution)/shard_map/ppermute | solution.py:485
  32.6 1.3 collective-permute-start.14
  34.7 1.3 collective-permute-start.11
  36.7 1.7 collective-permute-start.21
  38.6 20.2 %collective-permute-done.11 = bf16[144,2048]{1,0:T(8,128)(2,1)S(1)} collective-permute-done((bf16[144,2048]{1,0:T(8,128)(2,1)S(1)}, bf16[144,2048]{1,0:T(8,128)(2,1)S(1)}, u32[]{:S(2)}, u32[]{:S(2)}) %collective-permute-start.11) | collective-permute-done | bytes 589856 | tf_op jit(solution)/shard_map/ppermute | solution.py:507
  58.8 1.4 collective-permute-start.22
  60.1 3.2 %collective-permute-start.1 = (bf16[256,768]{1,0:T(8,128)(2,1)S(1)}, bf16[256,768]{1,0:T(8,128)(2,1)S(1)}, u32[]{:S(2)}, u32[]{:S(2)}) collective-permute-start(bf16[256,768]{1,0:T(8,128)(2,1)S(1)} %get-tuple-element.55), channel_id=1, source_target_pairs={{0,8},{4,12},{8,0},{12,4},{1,9},{5,13},{9,1},{13,5},{2,10},{6,14},... | collective-permute-start | bytes 1179656 | tf_op jit(solution)/shard_map/ppermute | solution.py:472
  63.4 1.3 collective-permute-start.12
  64.8 1.3 collective-permute-start.18
  66.3 22.8 %collective-permute-done.12 = bf16[144,2048]{1,0:T(8,128)(2,1)S(1)} collective-permute-done((bf16[144,2048]{1,0:T(8,128)(2,1)S(1)}, bf16[144,2048]{1,0:T(8,128)(2,1)S(1)}, u32[]{:S(2)}, u32[]{:S(2)}) %collective-permute-start.12) | collective-permute-done | bytes 589856 | tf_op jit(solution)/shard_map/ppermute | solution.py:515
  89.1 5.5 %collective-permute-start.3 = (bf16[256,768]{1,0:T(8,128)(2,1)S(1)}, bf16[256,768]{1,0:T(8,128)(2,1)S(1)}, u32[]{:S(2)}, u32[]{:S(2)}) collective-permute-start(bf16[256,768]{1,0:T(8,128)(2,1)S(1)} %get-tuple-element.56), channel_id=1, source_target_pairs={{0,12},{4,0},{8,4},{12,8},{1,13},{5,1},{9,5},{13,9},{2,14},{6,2},{... | collective-permute-start | bytes 1179656 | tf_op jit(solution)/shard_map/ppermute | solution.py:472
  95.4 1.5 collective-permute-start.7
  96.9 10.4 %collective-permute-done.18 = bf16[112,2048]{1,0:T(8,128)(2,1)S(1)} collective-permute-done((bf16[112,2048]{1,0:T(8,128)(2,1)S(1)}, bf16[112,2048]{1,0:T(8,128)(2,1)S(1)}, u32[]{:S(2)}, u32[]{:S(2)}) %collective-permute-start.18) | collective-permute-done | bytes 458784 | tf_op jit(solution)/shard_map/ppermute | solution.py:515
  107.4 1.5 collective-permute-start.23
  109.8 2.6 %collective-permute-done.3.refs_3_ = bf16[256,768]{1,0:T(8,128)(2,1)S(1)} collective-permute-done((bf16[256,768]{1,0:T(8,128)(2,1)S(1)}, bf16[256,768]{1,0:T(8,128)(2,1)S(1)}, u32[]{:S(2)}, u32[]{:S(2)}) %collective-permute-start.3) | collective-permute-done | bytes 393248 | tf_op jit(solution)/shard_map/ppermute | solution.py:472
  112.4 1.5 collective-permute-start.24
  113.9 1.5 collective-permute-start.2
  115.9 1.5 collective-permute-start.6
  118.3 7.6 %collective-permute-done.2.refs_2_ = bf16[256,768]{1,0:T(8,128)(2,1)S(1)} collective-permute-done((bf16[256,768]{1,0:T(8,128)(2,1)S(1)}, bf16[256,768]{1,0:T(8,128)(2,1)S(1)}, u32[]{:S(2)}, u32[]{:S(2)}) %collective-permute-start.2) | collective-permute-done | bytes 393248 | tf_op jit(solution)/shard_map/ppermute | solution.py:469
  125.9 8.1 %collective-permute-done.4.refs_4_ = bf16[256,768]{1,0:T(8,128)(2,1)S(1)} collective-permute-done((bf16[256,768]{1,0:T(8,128)(2,1)S(1)}, bf16[256,768]{1,0:T(8,128)(2,1)S(1)}, u32[]{:S(2)}, u32[]{:S(2)}) %collective-permute-start.4) | collective-permute-done | bytes 393248 | tf_op jit(solution)/shard_map/ppermute | solution.py:469
  134.0 4.2 %collective-permute-done.6.refs_6_ = bf16[256,768]{1,0:T(8,128)(2,1)S(1)} collective-permute-done((bf16[256,768]{1,0:T(8,128)(2,1)S(1)}, bf16[256,768]{1,0:T(8,128)(2,1)S(1)}, u32[]{:S(2)}, u32[]{:S(2)}) %collective-permute-start.6) | collective-permute-done | bytes 393248 | tf_op jit(solution)/shard_map/ppermute | solution.py:469
  139.8 11.2 %project.3 = (f32[1792,384]{1,0:T(8,128)}, bf16[1792,384]{1,0:T(8,128)(2,1)}) custom-call(s32[8]{0:T(128)} %stack.112.refs_0_, bf16[256,768]{1,0:T(8,128)(2,1)} %copy-done.16, bf16[256,768]{1,0:T(8,128)(2,1)} %copy-done.20, bf16[256,768]{1,0:T(8,128)(2,1)} %copy-done.17, bf16[256,768]{1,0:T(8,128)(2,1)} %copy-done.21, bf16[256,768]{1,0:T(8,128)(2,1)} %copy-done.18, ...), custom_call_target="tpu_custom_call" | custom-call | flops 5637144576 | bytes 15990784 | tf_op jit(solution)/shard_map/project/pallas_call | solution.py:256
  151.6 1.5 collective-permute-start.19
  153.1 23.5 %collective-permute-done.19.refs_10_ = bf16[112,2048]{1,0:T(8,128)(2,1)S(1)} collective-permute-done((bf16[112,2048]{1,0:T(8,128)(2,1)S(1)}, bf16[112,2048]{1,0:T(8,128)(2,1)S(1)}, u32[]{:S(2)}, u32[]{:S(2)}) %collective-permute-start.19) | collective-permute-done | bytes 458784 | tf_op jit(solution)/shard_map/ppermute | solution.py:466
  178.2 4.7 %project.2 = (f32[256,384]{1,0:T(8,128)}, bf16[256,384]{1,0:T(8,128)(2,1)}) custom-call(s32[8]{0:T(128)} %stack.112.refs_0_, bf16[256,768]{1,0:T(8,128)(2,1)} %copy-done.16, bf16[256,768]{1,0:T(8,128)(2,1)} %copy-done.20, bf16[256,768]{1,0:T(8,128)(2,1)} %copy-done.17, bf16[256,768]{1,0:T(8,128)(2,1)} %copy-done.21, bf16[256,768]{1,0:T(8,128)(2,1)} %copy-done.18, ...), custom_call_target="tpu_custom_call" | custom-call | flops 805306368 | bytes 4980736 | tf_op jit(solution)/shard_map/project/pallas_call | solution.py:256
  182.9 3.3 %all-to-all-start = ((s32[4,1,512]{2,1,0:T(1,128)}), s32[4,1,512]{2,1,0:T(1,128)S(1)}, u32[]{:S(2)}, u32[]{:S(2)}) async-start(s32[4,1,512]{2,1,0:T(1,128)} %bitcast.28), calls=%async_computation | async-start | bytes 16384 | tf_op jit(solution)/shard_map/all_to_all | solution.py:494
  186.9 4.9 %all-to-all-done = s32[4,1,512]{2,1,0:T(1,128)S(1)} async-done(((s32[4,1,512]{2,1,0:T(1,128)}), s32[4,1,512]{2,1,0:T(1,128)S(1)}, u32[]{:S(2)}, u32[]{:S(2)}) %all-to-all-start) | async-done | bytes 8224 | tf_op jit(solution)/shard_map/all_to_all | solution.py:494
  192.2 1.1 copy-done.7
  193.3 4.2 %merge.1.base_ref = bf16[2048,384]{1,0:T(8,128)(2,1)} custom-call(s32[7]{0:T(128)} %stack.125.refs_0_, f32[1792,384]{1,0:T(8,128)} %get-tuple-element.52.refs_1_, bf16[1792,384]{1,0:T(8,128)(2,1)} %copy-done.7), custom_call_target="tpu_custom_call" | custom-call | flops 688128 | bytes 5505024 | tf_op jit(solution)/shard_map/merge/pallas_call | solution.py:308
  197.6 1.4 copy-done
  199.0 1.2 copy-done.1
  200.2 1.4 copy-done.2
  201.6 2.3 %attend.5 = bf16[576,128]{1,0:T(8,128)(2,1)S(1)} custom-call(s32[1]{0:T(128)} %bitcast.31.refs_0_, bf16[2048,384]{1,0:T(8,128)(2,1)S(1)} %copy-done.2, s32[2048,1]{1,0:T(8,128)S(1)} %copy.7.refs_2_, s32[1,2048]{1,0:T(1,128)S(1)} %bitcast.39), custom_call_target="tpu_custom_call" | custom-call | flops 536870912 | bytes 2097152 | tf_op jit(solution)/shard_map/attend/pallas_call | solution.py:155
  203.9 1.7 collective-permute-start.26
  205.5 3.3 %attend.6 = bf16[576,128]{1,0:T(8,128)(2,1)S(1)} custom-call(s32[1]{0:T(128)} %bitcast.32.refs_0_, bf16[2048,384]{1,0:T(8,128)(2,1)S(1)} %copy-done.2, s32[2048,1]{1,0:T(8,128)S(1)} %copy.7.refs_2_, s32[1,2048]{1,0:T(1,128)S(1)} %bitcast.40), custom_call_target="tpu_custom_call" | custom-call | flops 536870912 | bytes 2097152 | tf_op jit(solution)/shard_map/attend/pallas_call | solution.py:155
  208.9 4.4 %attend.7 = bf16[576,128]{1,0:T(8,128)(2,1)S(1)} custom-call(s32[1]{0:T(128)} %bitcast.33.refs_0_, bf16[2048,384]{1,0:T(8,128)(2,1)S(1)} %copy-done.2, s32[2048,1]{1,0:T(8,128)S(1)} %copy.7.refs_2_, s32[1,2048]{1,0:T(1,128)S(1)} %bitcast.41), custom_call_target="tpu_custom_call" | custom-call | flops 536870912 | bytes 2097152 | tf_op jit(solution)/shard_map/attend/pallas_call | solution.py:155
  213.4 3.9 %collective-permute-start.28 = (bf16[576,128]{1,0:T(8,128)(2,1)S(1)}, bf16[576,128]{1,0:T(8,128)(2,1)S(1)}, u32[]{:S(2)}, u32[]{:S(2)}) collective-permute-start(bf16[576,128]{1,0:T(8,128)(2,1)S(1)} %attend.7), channel_id=1, source_target_pairs={{0,12},{4,0},{8,4},{12,8},{1,13},{5,1},{9,5},{13,9},{2,14},{6,2},{... | collective-permute-start | bytes 442376 | tf_op jit(solution)/shard_map/ppermute | solution.py:472
  217.3 1.2 attend.4.refs_1_
  218.6 1.0 collective-permute-done.27.refs_3_
  219.9 1.5 collect.1
  (92 shorter events, 12.3 us)
Async XLA Ops:
  4.2 30.3 %collective-permute-start.10 = (bf16[144,2048]{1,0:T(8,128)(2,1)}, bf16[144,2048]{1,0:T(8,128)(2,1)S(1)}, u32[]{:S(2)}, u32[]{:S(2)}) collective-permute-start(bf16[144,2048]{1,0:T(8,128)(2,1)} %get-tuple-element.28), channel_id=1, source_target_pairs={{4,0},{8,4},{12,8},{5,1},{9,5},{13,9},{6,2},{10,6},{14,10},{7,3},{... | collective-permute-start | bytes 1769480 | tf_op jit(solution)/shard_map/ppermute | solution.py:485
  5.5 29.0 %collective-permute-start.8 = (bf16[144,2048]{1,0:T(8,128)(2,1)}, bf16[144,2048]{1,0:T(8,128)(2,1)S(1)}, u32[]{:S(2)}, u32[]{:S(2)}) collective-permute-start(bf16[144,2048]{1,0:T(8,128)(2,1)} %get-tuple-element.28), channel_id=1, source_target_pairs={{0,4},{4,8},{8,12},{1,5},{5,9},{9,13},{2,6},{6,10},{10,14},{3,7},{... | collective-permute-start | bytes 1769480 | tf_op jit(solution)/shard_map/ppermute | solution.py:484
  11.2 21.4 %collective-permute-start.13 = (bf16[112,2048]{1,0:T(8,128)(2,1)}, bf16[112,2048]{1,0:T(8,128)(2,1)S(1)}, u32[]{:S(2)}, u32[]{:S(2)}) collective-permute-start(bf16[112,2048]{1,0:T(8,128)(2,1)} %get-tuple-element.29), channel_id=1, source_target_pairs={{4,0},{8,4},{12,8},{5,1},{9,5},{13,9},{6,2},{10,6},{14,10},{7,3},{... | collective-permute-start | bytes 1376264 | tf_op jit(solution)/shard_map/ppermute | solution.py:485
  12.5 21.4 %collective-permute-start.15 = (bf16[112,2048]{1,0:T(8,128)(2,1)}, bf16[112,2048]{1,0:T(8,128)(2,1)S(1)}, u32[]{:S(2)}, u32[]{:S(2)}) collective-permute-start(bf16[112,2048]{1,0:T(8,128)(2,1)} %get-tuple-element.29), channel_id=1, source_target_pairs={{0,4},{4,8},{8,12},{1,5},{5,9},{9,13},{2,6},{6,10},{10,14},{3,7},{... | collective-permute-start | bytes 1376264 | tf_op jit(solution)/shard_map/ppermute | solution.py:484
  19.1 17.7 %collective-permute-start = (bf16[4,256,384]{2,1,0:T(8,128)(2,1)}, bf16[4,256,384]{2,1,0:T(8,128)(2,1)S(1)}, u32[]{:S(2)}, u32[]{:S(2)}) collective-permute-start(bf16[4,256,384]{2,1,0:T(8,128)(2,1)} %unpack.3), channel_id=1, source_target_pairs={{0,1},{1,0},{2,3},{3,2},{4,5},{5,4},{6,7},{7,6},{8,9},{9,8},{10,11... | collective-permute-start | bytes 2359304 | tf_op jit(solution)/shard_map/ppermute | solution.py:462
  25.9 12.6 %copy-start.5 = (bf16[4,256,384]{2,1,0:T(8,128)(2,1)S(1)}, bf16[4,256,384]{2,1,0:T(8,128)(2,1)}, u32[]{:S(2)}) copy-start(bf16[4,256,384]{2,1,0:T(8,128)(2,1)} %unpack.2) | copy-start | bytes 2359300
  32.6 30.9 %collective-permute-start.14 = (bf16[112,2048]{1,0:T(8,128)(2,1)S(1)}, bf16[112,2048]{1,0:T(8,128)(2,1)S(1)}, u32[]{:S(2)}, u32[]{:S(2)}) collective-permute-start(bf16[112,2048]{1,0:T(8,128)(2,1)S(1)} %collective-permute-done.13), channel_id=1, source_target_pairs={{4,0},{8,4},{5,1},{9,5},{6,2},{10,6},{7,3},{11,7},{20,16},{24,20},... | collective-permute-start | bytes 1376264 | tf_op jit(solution)/shard_map/ppermute | solution.py:507
  33.9 30.9 %collective-permute-start.16 = (bf16[112,2048]{1,0:T(8,128)(2,1)S(1)}, bf16[112,2048]{1,0:T(8,128)(2,1)S(1)}, u32[]{:S(2)}, u32[]{:S(2)}) collective-permute-start(bf16[112,2048]{1,0:T(8,128)(2,1)S(1)} %collective-permute-done.15), channel_id=1, source_target_pairs={{4,8},{8,12},{5,9},{9,13},{6,10},{10,14},{7,11},{11,15},{20,24},{2... | collective-permute-start | bytes 1376264 | tf_op jit(solution)/shard_map/ppermute | solution.py:507
  34.7 3.9 %copy-start.9 = (bf16[144,2048]{1,0:T(8,128)(2,1)}, bf16[144,2048]{1,0:T(8,128)(2,1)S(1)}, u32[]{:S(2)}) copy-start(bf16[144,2048]{1,0:T(8,128)(2,1)S(1)} %broadcast_select_fusion.refs_10_) | copy-start | bytes 1769476
  34.7 24.1 %collective-permute-start.11 = (bf16[144,2048]{1,0:T(8,128)(2,1)S(1)}, bf16[144,2048]{1,0:T(8,128)(2,1)S(1)}, u32[]{:S(2)}, u32[]{:S(2)}) collective-permute-start(bf16[144,2048]{1,0:T(8,128)(2,1)S(1)} %collective-permute-done.10), channel_id=1, source_target_pairs={{4,0},{8,4},{5,1},{9,5},{6,2},{10,6},{7,3},{11,7},{20,16},{24,20},... | collective-permute-start | bytes 1769480 | tf_op jit(solution)/shard_map/ppermute | solution.py:507
  36.0 24.2 %collective-permute-start.9 = (bf16[144,2048]{1,0:T(8,128)(2,1)S(1)}, bf16[144,2048]{1,0:T(8,128)(2,1)S(1)}, u32[]{:S(2)}, u32[]{:S(2)}) collective-permute-start(bf16[144,2048]{1,0:T(8,128)(2,1)S(1)} %collective-permute-done.8), channel_id=1, source_target_pairs={{4,8},{8,12},{5,9},{9,13},{6,10},{10,14},{7,11},{11,15},{20,24},{2... | collective-permute-start | bytes 1769480 | tf_op jit(solution)/shard_map/ppermute | solution.py:507
  36.7 22.0 %copy-start.13 = (bf16[112,2048]{1,0:T(8,128)(2,1)}, bf16[112,2048]{1,0:T(8,128)(2,1)S(1)}, u32[]{:S(2)}) copy-start(bf16[112,2048]{1,0:T(8,128)(2,1)S(1)} %broadcast_select_fusion.3.refs_11_) | copy-start | bytes 1376260
  36.7 79.2 %collective-permute-start.21 = (bf16[144,2048]{1,0:T(8,128)(2,1)S(1)}, bf16[144,2048]{1,0:T(8,128)(2,1)S(1)}, u32[]{:S(2)}, u32[]{:S(2)}) collective-permute-start(bf16[144,2048]{1,0:T(8,128)(2,1)S(1)} %broadcast_select_fusion.refs_10_), channel_id=1, source_target_pairs={{0,2},{1,3},{2,0},{3,1},{4,6},{5,7},{6,4},{7,5},{8,10},{9,11},{10,... | collective-permute-start | bytes 1769480 | tf_op jit(solution)/shard_map/ppermute | solution.py:466
  38.6 56.8 %copy-start.6 = (bf16[256,768]{1,0:T(8,128)(2,1)}, bf16[256,768]{1,0:T(8,128)(2,1)S(1)}, u32[]{:S(2)}) copy-start(bf16[256,768]{1,0:T(8,128)(2,1)S(1)} %get-tuple-element.54.refs_7_) | copy-start | bytes 1179652
  58.8 35.9 %collective-permute-start.22 = (bf16[112,2048]{1,0:T(8,128)(2,1)S(1)}, bf16[112,2048]{1,0:T(8,128)(2,1)S(1)}, u32[]{:S(2)}, u32[]{:S(2)}) collective-permute-start(bf16[112,2048]{1,0:T(8,128)(2,1)S(1)} %broadcast_select_fusion.3.refs_11_), channel_id=1, source_target_pairs={{0,2},{1,3},{2,0},{3,1},{4,6},{5,7},{6,4},{7,5},{8,10},{9,11},{10,... | collective-permute-start | bytes 1376264 | tf_op jit(solution)/shard_map/ppermute | solution.py:466
  60.1 34.5 %collective-permute-start.1 = (bf16[256,768]{1,0:T(8,128)(2,1)S(1)}, bf16[256,768]{1,0:T(8,128)(2,1)S(1)}, u32[]{:S(2)}, u32[]{:S(2)}) collective-permute-start(bf16[256,768]{1,0:T(8,128)(2,1)S(1)} %get-tuple-element.55), channel_id=1, source_target_pairs={{0,8},{4,12},{8,0},{12,4},{1,9},{5,13},{9,1},{13,5},{2,10},{6,14},... | collective-permute-start | bytes 1179656 | tf_op jit(solution)/shard_map/ppermute | solution.py:472
  63.4 25.7 %collective-permute-start.12 = (bf16[144,2048]{1,0:T(8,128)(2,1)S(1)}, bf16[144,2048]{1,0:T(8,128)(2,1)S(1)}, u32[]{:S(2)}, u32[]{:S(2)}) collective-permute-start(bf16[144,2048]{1,0:T(8,128)(2,1)S(1)} %broadcast_select_fusion.1), channel_id=1, source_target_pairs={{8,12},{4,0},{9,13},{5,1},{10,14},{6,2},{11,15},{7,3},{24,28},{20,... | collective-permute-start | bytes 1769480 | tf_op jit(solution)/shard_map/ppermute | solution.py:515
  64.8 42.6 %collective-permute-start.18 = (bf16[112,2048]{1,0:T(8,128)(2,1)S(1)}, bf16[112,2048]{1,0:T(8,128)(2,1)S(1)}, u32[]{:S(2)}, u32[]{:S(2)}) collective-permute-start(bf16[112,2048]{1,0:T(8,128)(2,1)S(1)} %broadcast_select_fusion.2), channel_id=1, source_target_pairs={{8,12},{4,0},{9,13},{5,1},{10,14},{6,2},{11,15},{7,3},{24,28},{20,... | collective-permute-start | bytes 1376264 | tf_op jit(solution)/shard_map/ppermute | solution.py:515
  66.2 43.6 %copy-start.10 = (bf16[144,2048]{1,0:T(8,128)(2,1)}, bf16[144,2048]{1,0:T(8,128)(2,1)S(1)}, u32[]{:S(2)}) copy-start(bf16[144,2048]{1,0:T(8,128)(2,1)S(1)} %select_select_fusion.1.refs_14_) | copy-start | bytes 1769476
  66.3 52.0 %copy-start.14 = (bf16[112,2048]{1,0:T(8,128)(2,1)}, bf16[112,2048]{1,0:T(8,128)(2,1)S(1)}, u32[]{:S(2)}) copy-start(bf16[112,2048]{1,0:T(8,128)(2,1)S(1)} %select_select_fusion.3.refs_15_) | copy-start | bytes 1376260
  89.1 23.3 %collective-permute-start.3 = (bf16[256,768]{1,0:T(8,128)(2,1)S(1)}, bf16[256,768]{1,0:T(8,128)(2,1)S(1)}, u32[]{:S(2)}, u32[]{:S(2)}) collective-permute-start(bf16[256,768]{1,0:T(8,128)(2,1)S(1)} %get-tuple-element.56), channel_id=1, source_target_pairs={{0,12},{4,0},{8,4},{12,8},{1,13},{5,1},{9,5},{13,9},{2,14},{6,2},{... | collective-permute-start | bytes 1179656 | tf_op jit(solution)/shard_map/ppermute | solution.py:472
  94.6 19.3 %collective-permute-start.5 = (bf16[256,768]{1,0:T(8,128)(2,1)S(1)}, bf16[256,768]{1,0:T(8,128)(2,1)S(1)}, u32[]{:S(2)}, u32[]{:S(2)}) collective-permute-start(bf16[256,768]{1,0:T(8,128)(2,1)S(1)} %get-tuple-element.57), channel_id=1, source_target_pairs={{0,4},{4,8},{8,12},{12,0},{1,5},{5,9},{9,13},{13,1},{2,6},{6,10},{... | collective-permute-start | bytes 1179656 | tf_op jit(solution)/shard_map/ppermute | solution.py:472
  95.4 22.9 %copy-start.16 = (bf16[256,768]{1,0:T(8,128)(2,1)}, bf16[256,768]{1,0:T(8,128)(2,1)S(1)}, u32[]{:S(2)}) copy-start(bf16[256,768]{1,0:T(8,128)(2,1)S(1)} %collective-permute-done.1.refs_1_) | copy-start | bytes 1179652
  95.4 20.0 %collective-permute-start.7 = (bf16[256,768]{1,0:T(8,128)(2,1)S(1)}, bf16[256,768]{1,0:T(8,128)(2,1)S(1)}, u32[]{:S(2)}, u32[]{:S(2)}) collective-permute-start(bf16[256,768]{1,0:T(8,128)(2,1)S(1)} %get-tuple-element.54.refs_7_), channel_id=1, source_target_pairs={{0,16},{16,0},{1,17},{17,1},{2,18},{18,2},{3,19},{19,3},{4,20},{20... | collective-permute-start | bytes 1179656 | tf_op jit(solution)/shard_map/ppermute | solution.py:469
  107.4 32.4 %collective-permute-start.23 = (bf16[144,2048]{1,0:T(8,128)(2,1)S(1)}, bf16[144,2048]{1,0:T(8,128)(2,1)}, u32[]{:S(2)}, u32[]{:S(2)}) collective-permute-start(bf16[144,2048]{1,0:T(8,128)(2,1)S(1)} %select_select_fusion.1.refs_14_), channel_id=1, source_target_pairs={{0,2},{1,3},{2,0},{3,1},{4,6},{5,7},{6,4},{7,5},{8,10},{9,11},{10,... | collective-permute-start | bytes 1769480 | tf_op jit(solution)/shard_map/ppermute | solution.py:466
  112.4 27.3 %copy-start.17 = (bf16[256,768]{1,0:T(8,128)(2,1)}, bf16[256,768]{1,0:T(8,128)(2,1)S(1)}, u32[]{:S(2)}) copy-start(bf16[256,768]{1,0:T(8,128)(2,1)S(1)} %collective-permute-done.3.refs_3_) | copy-start | bytes 1179652
  112.4 25.8 %collective-permute-start.24 = (bf16[112,2048]{1,0:T(8,128)(2,1)S(1)}, bf16[112,2048]{1,0:T(8,128)(2,1)S(1)}, u32[]{:S(2)}, u32[]{:S(2)}) collective-permute-start(bf16[112,2048]{1,0:T(8,128)(2,1)S(1)} %select_select_fusion.3.refs_15_), channel_id=1, source_target_pairs={{0,2},{1,3},{2,0},{3,1},{4,6},{5,7},{6,4},{7,5},{8,10},{9,11},{10,... | collective-permute-start | bytes 1376264 | tf_op jit(solution)/shard_map/ppermute | solution.py:466
  113.9 24.3 %copy-start.18 = (bf16[256,768]{1,0:T(8,128)(2,1)}, bf16[256,768]{1,0:T(8,128)(2,1)S(1)}, u32[]{:S(2)}) copy-start(bf16[256,768]{1,0:T(8,128)(2,1)S(1)} %collective-permute-done.5.refs_5_) | copy-start | bytes 1179652
  113.9 12.0 %collective-permute-start.2 = (bf16[256,768]{1,0:T(8,128)(2,1)S(1)}, bf16[256,768]{1,0:T(8,128)(2,1)S(1)}, u32[]{:S(2)}, u32[]{:S(2)}) collective-permute-start(bf16[256,768]{1,0:T(8,128)(2,1)S(1)} %collective-permute-done.1.refs_1_), channel_id=1, source_target_pairs={{0,16},{16,0},{1,17},{17,1},{2,18},{18,2},{3,19},{19,3},{4,20},{20... | collective-permute-start | bytes 1179656 | tf_op jit(solution)/shard_map/ppermute | solution.py:469
  115.4 22.8 %copy-start.19 = (bf16[256,768]{1,0:T(8,128)(2,1)}, bf16[256,768]{1,0:T(8,128)(2,1)S(1)}, u32[]{:S(2)}) copy-start(bf16[256,768]{1,0:T(8,128)(2,1)S(1)} %collective-permute-done.7.refs_8_) | copy-start | bytes 1179652
  115.4 18.6 %collective-permute-start.4 = (bf16[256,768]{1,0:T(8,128)(2,1)S(1)}, bf16[256,768]{1,0:T(8,128)(2,1)S(1)}, u32[]{:S(2)}, u32[]{:S(2)}) collective-permute-start(bf16[256,768]{1,0:T(8,128)(2,1)S(1)} %collective-permute-done.3.refs_3_), channel_id=1, source_target_pairs={{0,16},{16,0},{1,17},{17,1},{2,18},{18,2},{3,19},{19,3},{4,20},{20... | collective-permute-start | bytes 1179656 | tf_op jit(solution)/shard_map/ppermute | solution.py:469
  115.9 22.3 %copy-start.23 = (bf16[144,2048]{1,0:T(8,128)(2,1)}, bf16[144,2048]{1,0:T(8,128)(2,1)S(1)}, u32[]{:S(2)}) copy-start(bf16[144,2048]{1,0:T(8,128)(2,1)S(1)} %collective-permute-done.21.refs_12_) | copy-start | bytes 1769476
  115.9 22.3 %collective-permute-start.6 = (bf16[256,768]{1,0:T(8,128)(2,1)S(1)}, bf16[256,768]{1,0:T(8,128)(2,1)S(1)}, u32[]{:S(2)}, u32[]{:S(2)}) collective-permute-start(bf16[256,768]{1,0:T(8,128)(2,1)S(1)} %collective-permute-done.5.refs_5_), channel_id=1, source_target_pairs={{0,16},{16,0},{1,17},{17,1},{2,18},{18,2},{3,19},{19,3},{4,20},{20... | collective-permute-start | bytes 1179656 | tf_op jit(solution)/shard_map/ppermute | solution.py:469
  118.3 32.7 %copy-start.11 = (bf16[144,2048]{1,0:T(8,128)(2,1)S(1)}, bf16[144,2048]{1,0:T(8,128)(2,1)}, u32[]{:S(2)}) copy-start(bf16[144,2048]{1,0:T(8,128)(2,1)} %select_select_fusion.refs_18_) | copy-start | bytes 1769476
  118.3 33.3 %copy-start.15 = (bf16[112,2048]{1,0:T(8,128)(2,1)S(1)}, bf16[112,2048]{1,0:T(8,128)(2,1)}, u32[]{:S(2)}) copy-start(bf16[112,2048]{1,0:T(8,128)(2,1)} %select_select_fusion.2.refs_19_) | copy-start | bytes 1376260
  125.9 13.9 %copy-start.20 = (bf16[256,768]{1,0:T(8,128)(2,1)}, bf16[256,768]{1,0:T(8,128)(2,1)S(1)}, u32[]{:S(2)}) copy-start(bf16[256,768]{1,0:T(8,128)(2,1)S(1)} %collective-permute-done.2.refs_2_) | copy-start | bytes 1179652
  134.0 5.8 %copy-start.21 = (bf16[256,768]{1,0:T(8,128)(2,1)}, bf16[256,768]{1,0:T(8,128)(2,1)S(1)}, u32[]{:S(2)}) copy-start(bf16[256,768]{1,0:T(8,128)(2,1)S(1)} %collective-permute-done.4.refs_4_) | copy-start | bytes 1179652
  150.9 41.2 %collective-permute-start.25 = (bf16[1792,384]{1,0:T(8,128)(2,1)}, bf16[1792,384]{1,0:T(8,128)(2,1)S(1)}, u32[]{:S(2)}, u32[]{:S(2)}) collective-permute-start(bf16[1792,384]{1,0:T(8,128)(2,1)} %get-tuple-element.53), channel_id=1, source_target_pairs={{0,1},{1,0},{2,3},{3,2},{4,5},{5,4},{6,7},{7,6},{8,9},{9,8},{10,11... | collective-permute-start | bytes 4128776 | tf_op jit(solution)/shard_map/ppermute | solution.py:462
  151.0 25.6 %collective-permute-start.17 = (bf16[144,2048]{1,0:T(8,128)(2,1)S(1)}, bf16[144,2048]{1,0:T(8,128)(2,1)S(1)}, u32[]{:S(2)}, u32[]{:S(2)}) collective-permute-start(bf16[144,2048]{1,0:T(8,128)(2,1)S(1)} %copy-done.11), channel_id=1, source_target_pairs={{0,2},{1,3},{2,0},{3,1},{4,6},{5,7},{6,4},{7,5},{8,10},{9,11},{10,... | collective-permute-start | bytes 1769480 | tf_op jit(solution)/shard_map/ppermute | solution.py:466
  151.6 25.0 %collective-permute-start.19 = (bf16[112,2048]{1,0:T(8,128)(2,1)S(1)}, bf16[112,2048]{1,0:T(8,128)(2,1)S(1)}, u32[]{:S(2)}, u32[]{:S(2)}) collective-permute-start(bf16[112,2048]{1,0:T(8,128)(2,1)S(1)} %copy-done.15), channel_id=1, source_target_pairs={{0,2},{1,3},{2,0},{3,1},{4,6},{5,7},{6,4},{7,5},{8,10},{9,11},{10,... | collective-permute-start | bytes 1376264 | tf_op jit(solution)/shard_map/ppermute | solution.py:466
  182.9 14.7 %collective-permute-start.20 = (bf16[256,384]{1,0:T(8,128)(2,1)}, bf16[256,384]{1,0:T(8,128)(2,1)S(1)}, u32[]{:S(2)}, u32[]{:S(2)}) collective-permute-start(bf16[256,384]{1,0:T(8,128)(2,1)} %get-tuple-element.50), channel_id=1, source_target_pairs={{0,1},{1,0},{2,3},{3,2},{4,5},{5,4},{6,7},{7,6},{8,9},{9,8},{10,11... | collective-permute-start | bytes 589832 | tf_op jit(solution)/shard_map/ppermute | solution.py:462
  182.9 8.8 %all-to-all-start = ((s32[4,1,512]{2,1,0:T(1,128)}), s32[4,1,512]{2,1,0:T(1,128)S(1)}, u32[]{:S(2)}, u32[]{:S(2)}) async-start(s32[4,1,512]{2,1,0:T(1,128)} %bitcast.28), calls=%async_computation | async-start | bytes 16384 | tf_op jit(solution)/shard_map/all_to_all | solution.py:494
  193.3 4.3 %copy-start.3 = (f32[256,384]{1,0:T(8,128)S(1)}, f32[256,384]{1,0:T(8,128)}, u32[]{:S(2)}) copy-start(f32[256,384]{1,0:T(8,128)} %get-tuple-element.49.kept_ref) | copy-start | bytes 1179652
  197.6 1.4 copy-start
  203.9 14.7 %collective-permute-start.26 = (bf16[576,128]{1,0:T(8,128)(2,1)S(1)}, bf16[576,128]{1,0:T(8,128)(2,1)S(1)}, u32[]{:S(2)}, u32[]{:S(2)}) collective-permute-start(bf16[576,128]{1,0:T(8,128)(2,1)S(1)} %attend.5), channel_id=1, source_target_pairs={{0,4},{4,8},{8,12},{12,0},{1,5},{5,9},{9,13},{13,1},{2,6},{6,10},{... | collective-permute-start | bytes 442376 | tf_op jit(solution)/shard_map/ppermute | solution.py:472
  208.8 10.7 %collective-permute-start.27 = (bf16[576,128]{1,0:T(8,128)(2,1)S(1)}, bf16[576,128]{1,0:T(8,128)(2,1)S(1)}, u32[]{:S(2)}, u32[]{:S(2)}) collective-permute-start(bf16[576,128]{1,0:T(8,128)(2,1)S(1)} %attend.6), channel_id=1, source_target_pairs={{0,8},{4,12},{8,0},{12,4},{1,9},{5,13},{9,1},{13,5},{2,10},{6,14},... | collective-permute-start | bytes 442376 | tf_op jit(solution)/shard_map/ppermute | solution.py:472
  213.3 6.6 %copy-start.4 = (f32[4,64,128]{2,1,0:T(8,128)S(1)}, f32[4,64,128]{2,1,0:T(8,128)}, u32[]{:S(2)}) copy-start(f32[4,64,128]{2,1,0:T(8,128)} %refs_5_.1) | copy-start | bytes 393220
  213.4 6.6 %collective-permute-start.28 = (bf16[576,128]{1,0:T(8,128)(2,1)S(1)}, bf16[576,128]{1,0:T(8,128)(2,1)S(1)}, u32[]{:S(2)}, u32[]{:S(2)}) collective-permute-start(bf16[576,128]{1,0:T(8,128)(2,1)S(1)} %attend.7), channel_id=1, source_target_pairs={{0,12},{4,0},{8,4},{12,8},{1,13},{5,1},{9,5},{13,9},{2,14},{6,2},{... | collective-permute-start | bytes 442376 | tf_op jit(solution)/shard_map/ppermute | solution.py:472
  (8 other events, 7.6 us)

commit v2 on v1

--- a/solution.py
+++ b/solution.py
@@ -7,6 +7,8 @@
 
 SLOTS = 4
 CORES = 2
+LOG2_E = 1.4426950408889634
+LINE = 4
 SMALL_VMEM = 16 << 20
 
 
@@ -93,7 +95,7 @@
     rows = qkv_ref.shape[0]
     owned = out_ref.shape[0] - local_rows
     block = min(256, local_rows)
-    scale = hs ** (-0.5)
+    scale = hs ** (-0.5) * LOG2_E
     at = place[0] * local_rows
 
     for first in range(0, local_rows, block):
@@ -119,7 +121,7 @@
         col_at = lax.broadcasted_iota(jnp.int32, (block, size), 1)
         scores = jnp.where(allowed & (col_at <= row_at), scores, -1e30)
         peak = jnp.max(scores, axis=1, keepdims=True)
-        raised = jnp.exp(scores - peak)
+        raised = jnp.exp2(scores - peak)
         total = jnp.sum(raised, axis=1, keepdims=True)
         mixed = mix(raised, base, size)
 
@@ -129,8 +131,8 @@
             scores, allowed = scores_of(start, local_rows)
             scores = jnp.where(allowed, scores, -1e30)
             higher = jnp.maximum(peak, jnp.max(scores, axis=1, keepdims=True))
-            kept = jnp.exp(peak - higher)
-            raised = jnp.exp(scores - higher)
+            kept = jnp.exp2(peak - higher)
+            raised = jnp.exp2(scores - higher)
             total = total * kept + jnp.sum(raised, axis=1, keepdims=True)
             return higher, total, mixed * kept + mix(raised, start, local_rows)
 
@@ -200,47 +202,55 @@
     )(place, *pieces, centroids)
 
 
-def choose(index, values):
-    chosen = values[0]
-    for i, value in enumerate(values[1:], 1):
-        chosen = jnp.where(index == i, value, chosen)
-    return chosen
-
-
-def project_kernel(counts, spots, *refs):
-    weights, tokens = refs[: counts[0]], refs[counts[0] : sum(counts)]
-    kept_ref, sent_ref, matrix, held, weight_sem, token_sem = refs[sum(counts) :]
-    step = pl.program_id(0)
+def start_one(copies, flag):
+    if len(copies) == 1:
+        copies[0].start()
+        return
+    for i, copy in enumerate(copies):
+
+        @pl.when(flag == i)
+        def _(copy=copy):
+            copy.start()
+
+
+def project_kernel(count, choices, spots, *refs):
+    weights, refs = refs[:count], refs[count:]
+    tokens = []
+    for n in choices:
+        tokens.append(refs[:n])
+        refs = refs[n:]
+    kept_ref, sent_ref, matrix, held, weight_sem, token_sem = refs
+    step, flag = pl.program_id(0), spots[count]
     block, width = kept_ref.shape
     part = weights[0].shape[0]
     copies, row = {}, 0
-    for i, ref in enumerate(tokens):
-        to = held.at[row : row + ref.shape[0], :]
-        copy = pltpu.make_async_copy(ref, to, token_sem.at[i])
+    for i, options in enumerate(tokens):
+        to = held.at[row : row + options[0].shape[0], :]
+        copy = [pltpu.make_async_copy(ref, to, token_sem.at[i]) for ref in options]
         copies.setdefault(row // block, []).append(copy)
-        row += ref.shape[0]
+        row += options[0].shape[0]
 
     @pl.when(step == 0)
     def _():
         loads = []
         for i, ref in enumerate(weights):
             to = matrix.at[pl.ds(pl.multiple_of(spots[i] * part, part), part), :]
-            loads.append(pltpu.make_async_copy(ref, to, weight_sem.at[i]))
+            loads.append([pltpu.make_async_copy(ref, to, weight_sem.at[i])])
         loads += copies[0]
         for copy in loads:
-            copy.start()
+            start_one(copy, flag)
         for copy in loads:
-            copy.wait()
+            copy[0].wait()
         for at, group in copies.items():
             for copy in group if at else []:
-                copy.start()
+                start_one(copy, flag)
 
     for at, group in copies.items():
 
         @pl.when(step == at)
         def _(group=group):
             for copy in group if at else []:
-                copy.wait()
+                copy[0].wait()
 
     left = held[pl.ds(pl.multiple_of(step * block, block), block), :]
     full = jnp.dot(left, matrix[...], preferred_element_type=jnp.float32)
@@ -249,12 +259,13 @@
 
 
 def project(spots, weights, tokens, block):
+    tokens = [v if isinstance(v, tuple) else (v,) for v in tokens]
     depth = weights[0].shape[0] * len(weights)
     width = weights[0].shape[1] // CORES
-    total = sum(v.shape[0] for v in tokens)
-    counts = len(weights), len(tokens)
-    return pl.pallas_call(
-        lambda *refs: project_kernel(counts, *refs),
+    total = sum(v[0].shape[0] for v in tokens)
+    choices = [len(v) for v in tokens]
+    return pl.pallas_call(
+        lambda *refs: project_kernel(len(weights), choices, *refs),
         out_shape=(
             jax.ShapeDtypeStruct((total, width), jnp.float32),
             jax.ShapeDtypeStruct((total, width), jnp.bfloat16),
@@ -262,13 +273,13 @@
         grid_spec=pltpu.PrefetchScalarGridSpec(
             num_scalar_prefetch=1,
             grid=(total // block,),
-            in_specs=[pl.BlockSpec(memory_space=pl.ANY)] * sum(counts),
+            in_specs=[pl.BlockSpec(memory_space=pl.ANY)] * (len(weights) + sum(choices)),
             out_specs=[pl.BlockSpec((block, width), lambda i, p: (i, 0))] * 2,
             scratch_shapes=[
                 pltpu.VMEM((depth, CORES * width), jnp.bfloat16),
                 pltpu.VMEM((total, depth), jnp.bfloat16),
-                pltpu.SemaphoreType.DMA((counts[0],)),
-                pltpu.SemaphoreType.DMA((counts[1],)),
+                pltpu.SemaphoreType.DMA((len(weights),)),
+                pltpu.SemaphoreType.DMA((len(tokens),)),
             ],
         ),
         compiler_params=pltpu.CompilerParams(dimension_semantics=("arbitrary",)),
@@ -278,52 +289,55 @@
             transcendentals=0,
         ),
         name="project",
-    )(spots, *weights, *tokens)
-
-
-def merge_kernel(block, place, kept_hbm, theirs_hbm, out_ref, kept, theirs, sems):
-    count = kept.shape[0] // block
-    copies = []
-    for i in range(count):
-        down = pl.ds(i * block, block)
-        pair = (
-            pltpu.make_async_copy(kept_hbm.at[down], kept.at[down], sems.at[0, i]),
-            pltpu.make_async_copy(theirs_hbm.at[down], theirs.at[down], sems.at[1, i]),
-        )
-        for copy in pair:
-            copy.start()
-        copies.append(pair)
-    for i, pair in enumerate(copies):
+    )(spots, *weights, *[v for options in tokens for v in options])
+
+
+def merge_kernel(block, groups, place, *refs):
+    sources, (out_ref, *held, sems) = refs[: 2 * groups], refs[2 * groups :]
+    copies, i = [], 0
+    for n in range(groups):
+        for row in range(0, held[2 * n].shape[0], block):
+            down = pl.ds(row, block)
+            pair = [
+                pltpu.make_async_copy(
+                    sources[2 * n + j].at[down], held[2 * n + j].at[down], sems.at[j, i]
+                )
+                for j in range(2)
+            ]
+            for copy in pair:
+                copy.start()
+            copies.append((n, row, pair))
+            i += 1
+    for i, (n, row, pair) in enumerate(copies):
         for copy in pair:
             copy.wait()
-        here = slice(i * block, (i + 1) * block)
-        both = kept[here, :] + theirs[here, :].astype(jnp.float32)
+        here = slice(row, row + block)
+        both = held[2 * n][here, :] + held[2 * n + 1][here, :].astype(jnp.float32)
         to = pl.ds(pl.multiple_of(place[i] * block, block), block)
         out_ref[to, :] = both.astype(out_ref.dtype)
 
 
-def merge(at, kept, theirs, total, block):
-    rows, width = kept.shape
+def merge(at, sums, total, block):
+    flat = [v for pair in sums for v in pair]
+    where = [i for group in at for i in group]
+    width = flat[0].shape[1]
     anywhere = pl.BlockSpec(memory_space=pl.ANY)
     return pl.pallas_call(
-        lambda *refs: merge_kernel(block, *refs),
+        lambda *refs: merge_kernel(block, len(sums), *refs),
         out_shape=jax.ShapeDtypeStruct((total, width), jnp.bfloat16),
         grid_spec=pltpu.PrefetchScalarGridSpec(
             num_scalar_prefetch=1,
             grid=(1,),
-            in_specs=[anywhere, anywhere],
+            in_specs=[anywhere] * len(flat),
             out_specs=whole((total, width)),
-            scratch_shapes=[
-                pltpu.VMEM((rows, width), kept.dtype),
-                pltpu.VMEM((rows, width), theirs.dtype),
-                pltpu.SemaphoreType.DMA((2, rows // block)),
-            ],
+            scratch_shapes=[pltpu.VMEM(v.shape, v.dtype) for v in flat]
+            + [pltpu.SemaphoreType.DMA((2, len(where)))],
         ),
         cost_estimate=pl.CostEstimate(
-            flops=kept.size, bytes_accessed=8 * kept.size, transcendentals=0
+            flops=total * width, bytes_accessed=8 * total * width, transcendentals=0
         ),
         name="merge",
-    )(jnp.stack(at).astype(jnp.int32), kept, theirs)
+    )(jnp.stack(where).astype(jnp.int32), *flat)
 
 
 def merge_more_kernel(place, kept_ref, theirs_ref, base_ref, out_ref):
@@ -353,19 +367,6 @@
 
 def nearest(size):
     return sorted(range(size), key=lambda d: min(d, size - d))
-
-
-def arrivals(size):
-    table = []
-    for z in range(size):
-        order = []
-        for step in range(1, size):
-            if step <= z:
-                order.append((0, step))
-            if step <= size - 1 - z:
-                order.append((1, step))
-        table.append(order)
-    return table
 
 
 def take_kernel(runs, stride, place, in_ref, *refs):
@@ -461,10 +462,6 @@
     def swap_core(v):
         return lax.ppermute(v, "head", [(i, i ^ 1) for i in range(heads)])
 
-    def shift_x(v, d):
-        pairs = [(i, (i // CORES + d) % xs * CORES + i % CORES) for i in range(heads)]
-        return lax.ppermute(v, "head", pairs)
-
     def shift_y(v, d):
         return lax.ppermute(v, "groups", [(i, (i + d) % groups) for i in range(groups)])
 
@@ -499,69 +496,70 @@
     for d in nearest(seq)[::-1]:
         piece = lax.dynamic_index_in_dim(both, (z + d) % seq, 0, keepdims=False)
         pieces.append((d, shift_z(piece, d) if d else piece))
-    table = arrivals(seq)
-    for step in range(1, seq):
-        crossing = 2 * step <= seq + 1
-        if step > 1 and crossing:
-            for way, pairs in ((right, rightward), (left, leftward)):
-                way.append([lax.ppermute(v, "seq", pairs(step)) for v in way[-1]])
-        elif step > 1:
-            sent, forward = [], (z >= step - 1).astype(jnp.int32)
-            for ways in zip(left[-1], right[-1]):
-                if sent:
-                    ways, _ = tie((ways, sent[-1]))
-                sent.append(choose(forward, ways))
-            pairs = rightward(step) + leftward(step)
-            got = [lax.ppermute(v, "seq", pairs) for v in sent]
-            right.append(got)
-            left.append(got)
-
-    arrived, sources, last = [], [], None
-    for k in range(seq - 1):
-        picks = {}
-        for at in range(seq):
-            picks.setdefault(table[at][k], []).append(at)
-        index, source = jnp.int32(0), jnp.int32(0)
-        for i, ((direction, step), where) in enumerate(picks.items()):
-            chosen = sum((z == at).astype(jnp.int32) for at in where) > 0
-            index = jnp.where(chosen, i, index)
-            source = jnp.where(chosen, z + (step if direction else -step), source)
-        shares = [[] for _ in range(xs)]
-        for chunk in range(len(sizes)):
-            values = [(right, left)[direction][step][chunk] for direction, step in picks]
+    inner = (z > 0) & (z < seq - 1)
+    right.append([lax.ppermute(v, "seq", rightward(2)) for v in right[1]])
+    left.append([lax.ppermute(v, "seq", leftward(2)) for v in left[1]])
+
+    def chosen(flag, values, others, last=None):
+        result = []
+        for pair in zip(values, others):
             if last is not None:
-                values, last = tie((values, last))
-            block = last = choose(index, values)
-            for d in range(xs):
-                shares[d].append(shift_x(block, d) if d else block)
-        arrived.append(shares)
-        sources.append(source)
+                pair, last = tie((pair, last))
+            last = jnp.where(flag, *pair)
+            result.append(last)
+        return result
+
+    ends_z = (0, seq - 1)
+    inner_z = range(1, seq - 1)
+
+    def shares_x(values, where):
+        pairs = [
+            (at * heads + i, at * heads + (i // CORES + d) % xs * CORES + i % CORES)
+            for d in range(1, xs)
+            for at in where
+            for i in range(heads)
+        ]
+        return [lax.ppermute(v, ("seq", "head"), pairs) for v in values]
+
+    near = chosen(z == 0, left[1], right[1])
+    near_x = shares_x(near, range(seq))
+    other_x = shares_x(left[1], inner_z)
+    far_off = chosen(z < seq // 2, left[2], right[2], near[-1])
+    far_x = shares_x(far_off, range(seq))
+    pairs = [(seq - 2, seq - 1), (1, 0)]
+    ends = [lax.ppermute(v, "seq", pairs) for v in far_off]
+    ends_x = shares_x(ends, ends_z)
+    near_z = jnp.where(z == 0, 1, z - 1)
+    far_z = jnp.where(z < seq // 2, z + 2, z - 2)
+    last_z = jnp.where(inner, z + 1, seq - 1 - z)
 
     laid, spots = [], []
     for d, piece in pieces:
         for g in range(groups):
             laid.append(shift_y(piece, g) if g else piece)
             spots.append((z - d) % seq * groups + (y - g) % groups)
-    spots = jnp.stack(spots).astype(jnp.int32)
-
-    def place(k, d):
-        return sources[k] * xs + (x - d) % xs
-
-    early = [own] + [v for k in range(seq - 2) for share in arrived[k] for v in share]
-    early_at = [z * xs + i for i in range(xs)]
-    early_at += [place(k, d) for k in range(seq - 2) for d in range(xs)]
-    early += arrived[-1][0]
-    early_at.append(place(seq - 2, 0))
-    late = [v for share in arrived[-1][1:] for v in share]
-    late_at = [place(seq - 2, d) for d in range(1, xs)]
-
-    units = 2 * sum(v.shape[0] for v in early) // rows
-    tall = rows // 2 * max(n for n in range(1, units // 2 + 1) if units % n == 0)
-    kept, sent = project(spots, laid, early, tall)
-    theirs = swap_core(sent)
-    qkv = merge(early_at, kept, theirs, seq * local_rows, rows)
-    kept, sent = project(spots, laid, late, rows)
-    theirs = swap_core(sent)
+    spots = jnp.stack([*spots, inner]).astype(jnp.int32)
+
+    def place(source, d):
+        return source * xs + (x - d) % xs
+
+    both_d = range(xs)
+    first = [own, *near, *near_x]
+    first_at = [z * xs + i for i in both_d] + [place(near_z, d) for d in both_d]
+    middle = [*far_off, *far_x, *zip(ends, left[1])]
+    middle_at = [place(far_z, d) for d in both_d] + [place(last_z, 0)]
+    late, late_at = list(zip(ends_x, other_x)), [place(last_z, 1)]
+
+    def projected(tokens):
+        flat = [v[0] if isinstance(v, tuple) else v for v in tokens]
+        units = 2 * sum(v.shape[0] for v in flat) // rows
+        tall = rows // 2 * max(n for n in range(1, max(units // 2, 2) + 1) if units % n == 0)
+        kept, sent = project(spots, laid, tokens, tall)
+        return kept, swap_core(sent)
+
+    sums = projected(first), projected(middle)
+    qkv = merge((first_at, middle_at), sums, seq * local_rows, rows)
+    kept, theirs = projected(late)
     qkv = merge_more(late_at, kept, theirs, qkv, rows)
 
     owned = centroids.shape[1]
@@ -578,7 +576,7 @@
 
 def local(tokens, proj_weight, cluster_ids, centroids):
     seq, heads = lax.axis_size("seq"), lax.axis_size("head")
-    if cluster_ids.shape[0] == seq and heads % CORES == 0:
+    if cluster_ids.shape[0] == seq == LINE and heads == 2 * CORES:
         return by_head(tokens, proj_weight, cluster_ids, centroids)
     return routed(tokens, proj_weight, cluster_ids, centroids)
 

time: 222 us -> 195 us (0.88)
  waiting for transfers between devices: 112 us -> 81.9 us
  starting transfers between devices: 50.3 us -> 54.3 us
  Pallas kernels: 43.4 us -> 47.1 us
  local copies, waits for them, and re-layouts: 10.6 us -> 8.28 us
    ppermute x12 -> x14, waiting for transfers between devices: 76.9 us -> 25.4 us  [the longest x2 20.1 us: by_head(): left.append([lax.ppermute(v, 'seq', leftward(2)) for v in left[1]])]
    ppermute x6, waiting for transfers between devices: 3.96 us -> 28.1 us  [shift_z(): return lax.ppermute(v, 'seq', [(i, (i + d) % seq) for i in range(seq)])]
    ppermute x2, waiting for transfers between devices: 0.01 us -> 10.8 us  [by_head(): right.append([lax.ppermute(v, 'seq', rightward(1)) for v in mine])]
    ppermute x4, waiting for transfers between devices: 19.9 us -> 9.19 us  [shift_y(): lax.ppermute(v, 'groups', [(i, (i + d) % groups) for i in range(groups)])]
    ppermute x6, starting transfers between devices: 14.3 us -> 8.02 us  [shift_z(): return lax.ppermute(v, 'seq', [(i, (i + d) % seq) for i in range(seq)])]
    ppermute x12 -> x14, starting transfers between devices: 14.7 us -> 19.9 us  [the longest x8 13.4 us: shares_x(): return [lax.ppermute(v, ('seq', 'head'), pairs) for v in values]]
    all_to_all x1, starting transfers between devices: 3.26 us -> 8.29 us  [by_head(): lax.all_to_all(cluster_ids[:, :, 0], 'seq', split_axis=0, concat_axis=0,...]
    pallas_call x3 -> x4, Pallas kernels: 20.1 us -> 23.9 us  [the longest x3 19.7 us: project(): pl.pallas_call(lambda *refs: project_kernel(len(weights), choices, *refs)...]
  transfers between devices with their start and end apart: 30 -> 33, of which waited for: 12 -> 11; matrix products, arithmetic and copies ran while one was open for 2% -> 1% of each run, Pallas kernels for 11% -> 17%
where the time goes in v2:
time: 195 us; the launch traced here: 194 us
  waiting for transfers between devices  81.9 us (42%)
  starting transfers between devices  54.3 us (28%)
  Pallas kernels  47.1 us (24%)
  local copies, waits for them, and re-layouts  8.28 us (4%)
    ppermute x6, waiting for transfers between devices, shift_z(): return lax.ppermute(v, 'seq', [(i, (i + d) % seq) for i in range(seq)])  28.1 us
    ppermute x2, waiting for transfers between devices, by_head(): left.append([lax.ppermute(v, 'seq', leftward(2)) for v in left[1]])  20.1 us
    pallas_call x3, Pallas kernels, project(): pl.pallas_call(lambda *refs: project_kernel(len(weights), choices, *refs)...  19.7 us
    ppermute x8, starting transfers between devices, shares_x(): return [lax.ppermute(v, ('seq', 'head'), pairs) for v in values]  13.4 us
    pallas_call x4, Pallas kernels, attend(): pl.pallas_call(lambda *refs: attend_kernel(hs, rows // seq, *refs), out_s...  11.1 us
    ppermute x2, waiting for transfers between devices, by_head(): right.append([lax.ppermute(v, 'seq', rightward(1)) for v in mine])  10.8 us
    ppermute x2, starting transfers between devices, by_head(): right.append([lax.ppermute(v, 'seq', rightward(1)) for v in mine])  10.3 us
    ppermute x4, waiting for transfers between devices, shift_y(): lax.ppermute(v, 'groups', [(i, (i + d) % groups) for i in range(groups)])  9.19 us
  transfers between devices with their start and end apart: 33, of which 11 were waited for; matrix products, arithmetic and copies ran while one was open for 1% of the time, Pallas kernels for 17%

profile of v2, /device:TPU:0, one launch (start us, length us, event | category | flops | bytes accessed | tf_op | source)
XLA Modules:
  0.0 194.5 jit_solution(2956354809340323598)
XLA Ops:
  1.2 3.0 %take.2 = (bf16[144,2048]{1,0:T(8,128)(2,1)}, bf16[112,2048]{1,0:T(8,128)(2,1)}) custom-call(s32[2]{0:T(128)} %pad_add_fusion.1.refs_0_, bf16[512,4096]{1,0:T(8,128)(2,1)} %refs_1_.4), custom_call_target="tpu_custom_call" | custom-call | bytes 2097152 | tf_op jit(solution)/shard_map/take/pallas_call | solution.py:395
  4.2 5.0 %collective-permute-start.10 = (bf16[144,2048]{1,0:T(8,128)(2,1)}, bf16[144,2048]{1,0:T(8,128)(2,1)S(1)}, u32[]{:S(2)}, u32[]{:S(2)}) collective-permute-start(bf16[144,2048]{1,0:T(8,128)(2,1)} %get-tuple-element.18), channel_id=1, source_target_pairs={{0,4},{4,8},{8,12},{1,5},{5,9},{9,13},{2,6},{6,10},{10,14},{3,7},{... | collective-permute-start | bytes 1769480 | tf_op jit(solution)/shard_map/ppermute | solution.py:481
  9.2 1.3 collective-permute-start.8
  10.5 5.3 %collective-permute-start.13 = (bf16[112,2048]{1,0:T(8,128)(2,1)}, bf16[112,2048]{1,0:T(8,128)(2,1)}, u32[]{:S(2)}, u32[]{:S(2)}) collective-permute-start(bf16[112,2048]{1,0:T(8,128)(2,1)} %get-tuple-element.19), channel_id=1, source_target_pairs={{0,4},{4,8},{8,12},{1,5},{5,9},{9,13},{2,6},{6,10},{10,14},{3,7},{... | collective-permute-start | bytes 1376264 | tf_op jit(solution)/shard_map/ppermute | solution.py:481
  15.9 1.3 collective-permute-start.12
  17.2 2.0 %unpack.3 = bf16[4,256,384]{2,1,0:T(8,128)(2,1)} custom-call(s32[1]{0:T(128)} %bitcast.17.refs_0_, bf16[3,1024,512]{2,1,0:T(8,128)(2,1)} %refs_1_.3), custom_call_target="tpu_custom_call" | custom-call | bytes 1572864 | tf_op jit(solution)/shard_map/unpack/pallas_call | solution.py:429
  19.2 1.9 %unpack.2 = bf16[4,256,384]{2,1,0:T(8,128)(2,1)} custom-call(s32[1]{0:T(128)} %bitcast.14.refs_0_, bf16[3,1024,512]{2,1,0:T(8,128)(2,1)} %refs_1_.3), custom_call_target="tpu_custom_call" | custom-call | bytes 1572864 | tf_op jit(solution)/shard_map/unpack/pallas_call | solution.py:429
  21.1 10.8 %collective-permute-done.13 = bf16[112,2048]{1,0:T(8,128)(2,1)} collective-permute-done((bf16[112,2048]{1,0:T(8,128)(2,1)}, bf16[112,2048]{1,0:T(8,128)(2,1)}, u32[]{:S(2)}, u32[]{:S(2)}) %collective-permute-start.13) | collective-permute-done | bytes 458784 | tf_op jit(solution)/shard_map/ppermute | solution.py:481
  32.6 3.4 %collective-permute-done.12.refs_16_ = bf16[112,2048]{1,0:T(8,128)(2,1)S(1)} collective-permute-done((bf16[112,2048]{1,0:T(8,128)(2,1)}, bf16[112,2048]{1,0:T(8,128)(2,1)S(1)}, u32[]{:S(2)}, u32[]{:S(2)}) %collective-permute-start.12) | collective-permute-done | bytes 458784 | tf_op jit(solution)/shard_map/ppermute | solution.py:482
  36.0 1.3 collective-permute-start.17
  38.1 1.3 collective-permute-start.9
  39.5 1.6 collective-permute-start.23
  41.8 20.1 %collective-permute-done.9 = bf16[144,2048]{1,0:T(8,128)(2,1)S(1)} collective-permute-done((bf16[144,2048]{1,0:T(8,128)(2,1)S(1)}, bf16[144,2048]{1,0:T(8,128)(2,1)S(1)}, u32[]{:S(2)}, u32[]{:S(2)}) %collective-permute-start.9) | collective-permute-done | bytes 589856 | tf_op jit(solution)/shard_map/ppermute | solution.py:501
  61.9 1.2 collective-permute-start.1
  63.1 2.9 %collective-permute-start.3 = (bf16[256,768]{1,0:T(8,128)(2,1)S(1)}, bf16[256,768]{1,0:T(8,128)(2,1)S(1)}, u32[]{:S(2)}, u32[]{:S(2)}) collective-permute-start(bf16[256,768]{1,0:T(8,128)(2,1)S(1)} %get-tuple-element.36), channel_id=1, source_target_pairs={{0,12},{4,0},{8,4},{12,8},{1,13},{5,1},{9,5},{13,9},{2,14},{6,2},{... | collective-permute-start | bytes 1179656 | tf_op jit(solution)/shard_map/ppermute | solution.py:469
  66.1 1.6 collective-permute-start.7
  67.7 1.3 collective-permute-start.14
  69.0 15.4 %collective-permute-done.1.refs_1_ = bf16[256,768]{1,0:T(8,128)(2,1)S(1)} collective-permute-done((bf16[256,768]{1,0:T(8,128)(2,1)S(1)}, bf16[256,768]{1,0:T(8,128)(2,1)S(1)}, u32[]{:S(2)}, u32[]{:S(2)}) %collective-permute-start.1) | collective-permute-done | bytes 393248 | tf_op jit(solution)/shard_map/ppermute | solution.py:469
  84.4 1.5 collective-permute-start.2
  86.0 4.8 %collective-permute-done.3.refs_3_ = bf16[256,768]{1,0:T(8,128)(2,1)S(1)} collective-permute-done((bf16[256,768]{1,0:T(8,128)(2,1)S(1)}, bf16[256,768]{1,0:T(8,128)(2,1)S(1)}, u32[]{:S(2)}, u32[]{:S(2)}) %collective-permute-start.3) | collective-permute-done | bytes 393248 | tf_op jit(solution)/shard_map/ppermute | solution.py:469
  90.8 1.6 collective-permute-start.4
  93.5 3.0 %collective-permute-done.2.refs_2_ = bf16[256,768]{1,0:T(8,128)(2,1)S(1)} collective-permute-done((bf16[256,768]{1,0:T(8,128)(2,1)S(1)}, bf16[256,768]{1,0:T(8,128)(2,1)S(1)}, u32[]{:S(2)}, u32[]{:S(2)}) %collective-permute-start.2) | collective-permute-done | bytes 393248 | tf_op jit(solution)/shard_map/ppermute | solution.py:466
  96.4 1.5 collective-permute-start.26
  97.9 6.2 %collective-permute-done.4.refs_4_ = bf16[256,768]{1,0:T(8,128)(2,1)S(1)} collective-permute-done((bf16[256,768]{1,0:T(8,128)(2,1)S(1)}, bf16[256,768]{1,0:T(8,128)(2,1)S(1)}, u32[]{:S(2)}, u32[]{:S(2)}) %collective-permute-start.4) | collective-permute-done | bytes 393248 | tf_op jit(solution)/shard_map/ppermute | solution.py:466
  104.9 1.3 collective-permute-start.19
  106.9 3.6 %take.3.refs_9_ = bf16[512,2048]{1,0:T(8,128)(2,1)} custom-call(s32[2]{0:T(128)} %pad_add_fusion.2.refs_0_, bf16[512,4096]{1,0:T(8,128)(2,1)} %refs_1_.4), custom_call_target="tpu_custom_call" | custom-call | bytes 4194304 | tf_op jit(solution)/shard_map/take/pallas_call | solution.py:395
  111.3 1.4 collective-permute-start.21
  112.7 1.5 collective-permute-start.16
  114.2 3.4 %collective-permute-start.15 = (bf16[144,2048]{1,0:T(8,128)(2,1)}, bf16[144,2048]{1,0:T(8,128)(2,1)}, u32[]{:S(2)}, u32[]{:S(2)}) collective-permute-start(bf16[144,2048]{1,0:T(8,128)(2,1)} %collective-permute-done.14.refs_13_), channel_id=1, source_target_pairs={{0,2},{1,3},{2,0},{3,1},{12,14},{13,15},{14,12},{15,13},{16,18},{1... | collective-permute-start | bytes 1769480 | tf_op jit(solution)/shard_map/ppermute | solution.py:522
  117.6 8.0 %project.4 = (f32[1024,384]{1,0:T(8,128)}, bf16[1024,384]{1,0:T(8,128)(2,1)}) custom-call(s32[9]{0:T(128)} %stack.120.refs_0_, bf16[256,768]{1,0:T(8,128)(2,1)} %copy-done.16, bf16[256,768]{1,0:T(8,128)(2,1)} %copy-done.19, bf16[256,768]{1,0:T(8,128)(2,1)} %copy-done.17, bf16[256,768]{1,0:T(8,128)(2,1)} %copy-done.20, ...), custom_call_target="tpu_custom_call" | custom-call | flops 3221225472 | bytes 10485760 | tf_op jit(solution)/shard_map/project/pallas_call | solution.py:267
  125.8 2.4 %collective-permute-start.20 = (bf16[112,2048]{1,0:T(8,128)(2,1)}, bf16[112,2048]{1,0:T(8,128)(2,1)S(1)}, u32[]{:S(2)}, u32[]{:S(2)}) collective-permute-start(bf16[112,2048]{1,0:T(8,128)(2,1)} %collective-permute-done.19.refs_15_), channel_id=1, source_target_pairs={{0,2},{1,3},{2,0},{3,1},{12,14},{13,15},{14,12},{15,13},{16,18},{1... | collective-permute-start | bytes 1376264 | tf_op jit(solution)/shard_map/ppermute | solution.py:522
  128.2 6.9 %project.5 = (f32[768,384]{1,0:T(8,128)}, bf16[768,384]{1,0:T(8,128)(2,1)}) custom-call(s32[9]{0:T(128)} %stack.120.refs_0_, bf16[256,768]{1,0:T(8,128)(2,1)} %copy-done.16, bf16[256,768]{1,0:T(8,128)(2,1)} %copy-done.19, bf16[256,768]{1,0:T(8,128)(2,1)} %copy-done.17, bf16[256,768]{1,0:T(8,128)(2,1)} %copy-done.20, ...), custom_call_target="tpu_custom_call" | custom-call | flops 2415919104 | bytes 8650752 | tf_op jit(solution)/shard_map/project/pallas_call | solution.py:267
  135.4 5.4 %collective-permute-done.20.refs_11_ = bf16[112,2048]{1,0:T(8,128)(2,1)S(1)} collective-permute-done((bf16[112,2048]{1,0:T(8,128)(2,1)}, bf16[112,2048]{1,0:T(8,128)(2,1)S(1)}, u32[]{:S(2)}, u32[]{:S(2)}) %collective-permute-start.20) | collective-permute-done | bytes 458784 | tf_op jit(solution)/shard_map/ppermute | solution.py:522
  141.5 4.7 %project.3 = (f32[256,384]{1,0:T(8,128)}, bf16[256,384]{1,0:T(8,128)(2,1)}) custom-call(s32[9]{0:T(128)} %stack.120.refs_0_, bf16[256,768]{1,0:T(8,128)(2,1)} %copy-done.16, bf16[256,768]{1,0:T(8,128)(2,1)} %copy-done.19, bf16[256,768]{1,0:T(8,128)(2,1)} %copy-done.17, bf16[256,768]{1,0:T(8,128)(2,1)} %copy-done.20, ...), custom_call_target="tpu_custom_call" | custom-call | flops 805306368 | bytes 4980736 | tf_op jit(solution)/shard_map/project/pallas_call | solution.py:267
  146.4 8.3 %all-to-all-start = ((s32[4,1,512]{2,1,0:T(1,128)}), s32[4,1,512]{2,1,0:T(1,128)S(1)}, u32[]{:S(2)}, u32[]{:S(2)}) async-start(s32[4,1,512]{2,1,0:T(1,128)} %bitcast.29), calls=%async_computation | async-start | bytes 16384 | tf_op jit(solution)/shard_map/all_to_all | solution.py:491
  155.3 5.0 %all-to-all-done = s32[4,1,512]{2,1,0:T(1,128)S(1)} async-done(((s32[4,1,512]{2,1,0:T(1,128)}), s32[4,1,512]{2,1,0:T(1,128)S(1)}, u32[]{:S(2)}, u32[]{:S(2)}) %all-to-all-start) | async-done | bytes 8224 | tf_op jit(solution)/shard_map/all_to_all | solution.py:491
  161.7 4.3 %merge.1.base_ref = bf16[2048,384]{1,0:T(8,128)(2,1)} custom-call(s32[7]{0:T(128)} %stack.133.refs_0_, f32[1024,384]{1,0:T(8,128)} %get-tuple-element.30.refs_1_, bf16[1024,384]{1,0:T(8,128)(2,1)} %copy-done.7, f32[768,384]{1,0:T(8,128)} %get-tuple-element.32.refs_3_, bf16[768,384]{1,0:T(8,128)(2,1)} %copy-done.8), custom_call_target="tpu_custom_call" | custom-call | flops 786432 | bytes 6291456 | tf_op jit(solution)/shard_map/merge/pallas_call | solution.py:325
  166.0 1.4 copy-done
  167.5 1.2 copy-done.1
  168.6 1.4 copy-done.2
  170.0 4.2 %attend.7 = bf16[576,128]{1,0:T(8,128)(2,1)S(1)} custom-call(s32[1]{0:T(128)} %bitcast.34.refs_0_, bf16[2048,384]{1,0:T(8,128)(2,1)S(1)} %copy-done.2, s32[2048,1]{1,0:T(8,128)S(1)} %copy.7.refs_2_, s32[1,2048]{1,0:T(1,128)S(1)} %bitcast.40), custom_call_target="tpu_custom_call" | custom-call | flops 536870912 | bytes 2097152 | tf_op jit(solution)/shard_map/attend/pallas_call | solution.py:157
  174.3 3.2 %attend.6 = bf16[576,128]{1,0:T(8,128)(2,1)S(1)} custom-call(s32[1]{0:T(128)} %bitcast.33.refs_0_, bf16[2048,384]{1,0:T(8,128)(2,1)S(1)} %copy-done.2, s32[2048,1]{1,0:T(8,128)S(1)} %copy.7.refs_2_, s32[1,2048]{1,0:T(1,128)S(1)} %bitcast.41), custom_call_target="tpu_custom_call" | custom-call | flops 536870912 | bytes 2097152 | tf_op jit(solution)/shard_map/attend/pallas_call | solution.py:157
  177.5 2.4 %attend.5 = bf16[576,128]{1,0:T(8,128)(2,1)S(1)} custom-call(s32[1]{0:T(128)} %bitcast.32.refs_0_, bf16[2048,384]{1,0:T(8,128)(2,1)S(1)} %copy-done.2, s32[2048,1]{1,0:T(8,128)S(1)} %copy.7.refs_2_, s32[1,2048]{1,0:T(1,128)S(1)} %bitcast.42), custom_call_target="tpu_custom_call" | custom-call | flops 536870912 | bytes 2097152 | tf_op jit(solution)/shard_map/attend/pallas_call | solution.py:157
  180.1 3.7 %collective-permute-start.31 = (bf16[576,128]{1,0:T(8,128)(2,1)S(1)}, bf16[576,128]{1,0:T(8,128)(2,1)S(1)}, u32[]{:S(2)}, u32[]{:S(2)}) collective-permute-start(bf16[576,128]{1,0:T(8,128)(2,1)S(1)} %attend.7), channel_id=1, source_target_pairs={{0,12},{4,0},{8,4},{12,8},{1,13},{5,1},{9,5},{13,9},{2,14},{6,2},{... | collective-permute-start | bytes 442376 | tf_op jit(solution)/shard_map/ppermute | solution.py:469
  183.9 1.2 attend.4.refs_1_
  185.1 3.4 %collective-permute-done.29.refs_2_ = bf16[576,128]{1,0:T(8,128)(2,1)S(1)} collective-permute-done((bf16[576,128]{1,0:T(8,128)(2,1)S(1)}, bf16[576,128]{1,0:T(8,128)(2,1)S(1)}, u32[]{:S(2)}, u32[]{:S(2)}) %collective-permute-start.29) | collective-permute-done | bytes 147488 | tf_op jit(solution)/shard_map/ppermute | solution.py:469
  188.5 4.5 %collective-permute-done.30.refs_3_ = bf16[576,128]{1,0:T(8,128)(2,1)S(1)} collective-permute-done((bf16[576,128]{1,0:T(8,128)(2,1)S(1)}, bf16[576,128]{1,0:T(8,128)(2,1)S(1)}, u32[]{:S(2)}, u32[]{:S(2)}) %collective-permute-start.30) | collective-permute-done | bytes 147488 | tf_op jit(solution)/shard_map/ppermute | solution.py:469
  193.0 1.5 collect.1
  (89 shorter events, 9.6 us)
Async XLA Ops:
  4.2 33.0 %collective-permute-start.10 = (bf16[144,2048]{1,0:T(8,128)(2,1)}, bf16[144,2048]{1,0:T(8,128)(2,1)S(1)}, u32[]{:S(2)}, u32[]{:S(2)}) collective-permute-start(bf16[144,2048]{1,0:T(8,128)(2,1)} %get-tuple-element.18), channel_id=1, source_target_pairs={{0,4},{4,8},{8,12},{1,5},{5,9},{9,13},{2,6},{6,10},{10,14},{3,7},{... | collective-permute-start | bytes 1769480 | tf_op jit(solution)/shard_map/ppermute | solution.py:481
  9.2 28.0 %collective-permute-start.8 = (bf16[144,2048]{1,0:T(8,128)(2,1)}, bf16[144,2048]{1,0:T(8,128)(2,1)S(1)}, u32[]{:S(2)}, u32[]{:S(2)}) collective-permute-start(bf16[144,2048]{1,0:T(8,128)(2,1)} %get-tuple-element.18), channel_id=1, source_target_pairs={{4,0},{8,4},{12,8},{5,1},{9,5},{13,9},{6,2},{10,6},{14,10},{7,3},{... | collective-permute-start | bytes 1769480 | tf_op jit(solution)/shard_map/ppermute | solution.py:482
  10.5 21.4 %collective-permute-start.13 = (bf16[112,2048]{1,0:T(8,128)(2,1)}, bf16[112,2048]{1,0:T(8,128)(2,1)}, u32[]{:S(2)}, u32[]{:S(2)}) collective-permute-start(bf16[112,2048]{1,0:T(8,128)(2,1)} %get-tuple-element.19), channel_id=1, source_target_pairs={{0,4},{4,8},{8,12},{1,5},{5,9},{9,13},{2,6},{6,10},{10,14},{3,7},{... | collective-permute-start | bytes 1376264 | tf_op jit(solution)/shard_map/ppermute | solution.py:481
  15.9 20.1 %collective-permute-start.12 = (bf16[112,2048]{1,0:T(8,128)(2,1)}, bf16[112,2048]{1,0:T(8,128)(2,1)S(1)}, u32[]{:S(2)}, u32[]{:S(2)}) collective-permute-start(bf16[112,2048]{1,0:T(8,128)(2,1)} %get-tuple-element.19), channel_id=1, source_target_pairs={{4,0},{8,4},{12,8},{5,1},{9,5},{13,9},{6,2},{10,6},{14,10},{7,3},{... | collective-permute-start | bytes 1376264 | tf_op jit(solution)/shard_map/ppermute | solution.py:482
  19.2 20.3 %collective-permute-start = (bf16[4,256,384]{2,1,0:T(8,128)(2,1)}, bf16[4,256,384]{2,1,0:T(8,128)(2,1)S(1)}, u32[]{:S(2)}, u32[]{:S(2)}) collective-permute-start(bf16[4,256,384]{2,1,0:T(8,128)(2,1)} %unpack.3), channel_id=1, source_target_pairs={{0,1},{1,0},{2,3},{3,2},{4,5},{5,4},{6,7},{7,6},{8,9},{9,8},{10,11... | collective-permute-start | bytes 2359304 | tf_op jit(solution)/shard_map/ppermute | solution.py:463
  21.1 19.9 %copy-start.5 = (bf16[4,256,384]{2,1,0:T(8,128)(2,1)S(1)}, bf16[4,256,384]{2,1,0:T(8,128)(2,1)}, u32[]{:S(2)}) copy-start(bf16[4,256,384]{2,1,0:T(8,128)(2,1)} %unpack.2) | copy-start | bytes 2359300
  31.9 31.1 %collective-permute-start.18 = (bf16[112,2048]{1,0:T(8,128)(2,1)}, bf16[112,2048]{1,0:T(8,128)(2,1)S(1)}, u32[]{:S(2)}, u32[]{:S(2)}) collective-permute-start(bf16[112,2048]{1,0:T(8,128)(2,1)} %collective-permute-done.13), channel_id=1, source_target_pairs={{4,8},{8,12},{5,9},{9,13},{6,10},{10,14},{7,11},{11,15},{20,24},{2... | collective-permute-start | bytes 1376264 | tf_op jit(solution)/shard_map/ppermute | solution.py:500
  36.0 75.3 %copy-start.12 = (bf16[112,2048]{1,0:T(8,128)(2,1)}, bf16[112,2048]{1,0:T(8,128)(2,1)S(1)}, u32[]{:S(2)}) copy-start(bf16[112,2048]{1,0:T(8,128)(2,1)S(1)} %collective-permute-done.12.refs_16_) | copy-start | bytes 1376260
  36.0 30.1 %collective-permute-start.17 = (bf16[112,2048]{1,0:T(8,128)(2,1)S(1)}, bf16[112,2048]{1,0:T(8,128)(2,1)S(1)}, u32[]{:S(2)}, u32[]{:S(2)}) collective-permute-start(bf16[112,2048]{1,0:T(8,128)(2,1)S(1)} %collective-permute-done.12.refs_16_), channel_id=1, source_target_pairs={{4,0},{8,4},{5,1},{9,5},{6,2},{10,6},{7,3},{11,7},{20,16},{24,20},... | collective-permute-start | bytes 1376264 | tf_op jit(solution)/shard_map/ppermute | solution.py:501
  37.3 75.4 %copy-start.9 = (bf16[144,2048]{1,0:T(8,128)(2,1)}, bf16[144,2048]{1,0:T(8,128)(2,1)S(1)}, u32[]{:S(2)}) copy-start(bf16[144,2048]{1,0:T(8,128)(2,1)S(1)} %collective-permute-done.8.refs_14_) | copy-start | bytes 1769476
  37.4 3.8 %copy-start.10 = (bf16[144,2048]{1,0:T(8,128)(2,1)}, bf16[144,2048]{1,0:T(8,128)(2,1)S(1)}, u32[]{:S(2)}) copy-start(bf16[144,2048]{1,0:T(8,128)(2,1)S(1)} %broadcast_select_fusion.refs_10_) | copy-start | bytes 1769476
  37.4 3.8 %collective-permute-start.11 = (bf16[144,2048]{1,0:T(8,128)(2,1)S(1)}, bf16[144,2048]{1,0:T(8,128)(2,1)S(1)}, u32[]{:S(2)}, u32[]{:S(2)}) collective-permute-start(bf16[144,2048]{1,0:T(8,128)(2,1)S(1)} %collective-permute-done.10), channel_id=1, source_target_pairs={{4,8},{8,12},{5,9},{9,13},{6,10},{10,14},{7,11},{11,15},{20,24},{2... | collective-permute-start | bytes 1769480 | tf_op jit(solution)/shard_map/ppermute | solution.py:500
  38.1 23.8 %collective-permute-start.9 = (bf16[144,2048]{1,0:T(8,128)(2,1)S(1)}, bf16[144,2048]{1,0:T(8,128)(2,1)S(1)}, u32[]{:S(2)}, u32[]{:S(2)}) collective-permute-start(bf16[144,2048]{1,0:T(8,128)(2,1)S(1)} %collective-permute-done.8.refs_14_), channel_id=1, source_target_pairs={{4,0},{8,4},{5,1},{9,5},{6,2},{10,6},{7,3},{11,7},{20,16},{24,20},... | collective-permute-start | bytes 1769480 | tf_op jit(solution)/shard_map/ppermute | solution.py:501
  39.5 28.2 %collective-permute-start.23 = (bf16[144,2048]{1,0:T(8,128)(2,1)S(1)}, bf16[144,2048]{1,0:T(8,128)(2,1)S(1)}, u32[]{:S(2)}, u32[]{:S(2)}) collective-permute-start(bf16[144,2048]{1,0:T(8,128)(2,1)S(1)} %broadcast_select_fusion.refs_10_), channel_id=1, source_target_pairs={{0,2},{1,3},{2,0},{3,1},{4,6},{5,7},{6,4},{7,5},{8,10},{9,11},{10,... | collective-permute-start | bytes 1769480 | tf_op jit(solution)/shard_map/ppermute | solution.py:522
  41.2 51.3 %copy-start.6 = (bf16[256,768]{1,0:T(8,128)(2,1)}, bf16[256,768]{1,0:T(8,128)(2,1)S(1)}, u32[]{:S(2)}) copy-start(bf16[256,768]{1,0:T(8,128)(2,1)S(1)} %get-tuple-element.34.refs_7_) | copy-start | bytes 1179652
  41.2 24.9 %collective-permute-start.24 = (bf16[112,2048]{1,0:T(8,128)(2,1)S(1)}, bf16[112,2048]{1,0:T(8,128)(2,1)S(1)}, u32[]{:S(2)}, u32[]{:S(2)}) collective-permute-start(bf16[112,2048]{1,0:T(8,128)(2,1)S(1)} %broadcast_select_fusion.3.refs_11_), channel_id=1, source_target_pairs={{0,2},{1,3},{2,0},{3,1},{4,6},{5,7},{6,4},{7,5},{8,10},{9,11},{10,... | collective-permute-start | bytes 1376264 | tf_op jit(solution)/shard_map/ppermute | solution.py:522
  61.9 22.6 %collective-permute-start.1 = (bf16[256,768]{1,0:T(8,128)(2,1)S(1)}, bf16[256,768]{1,0:T(8,128)(2,1)S(1)}, u32[]{:S(2)}, u32[]{:S(2)}) collective-permute-start(bf16[256,768]{1,0:T(8,128)(2,1)S(1)} %get-tuple-element.35), channel_id=1, source_target_pairs={{0,8},{4,12},{8,0},{12,4},{1,9},{5,13},{9,1},{13,5},{2,10},{6,14},... | collective-permute-start | bytes 1179656 | tf_op jit(solution)/shard_map/ppermute | solution.py:469
  63.1 27.7 %collective-permute-start.3 = (bf16[256,768]{1,0:T(8,128)(2,1)S(1)}, bf16[256,768]{1,0:T(8,128)(2,1)S(1)}, u32[]{:S(2)}, u32[]{:S(2)}) collective-permute-start(bf16[256,768]{1,0:T(8,128)(2,1)S(1)} %get-tuple-element.36), channel_id=1, source_target_pairs={{0,12},{4,0},{8,4},{12,8},{1,13},{5,1},{9,5},{13,9},{2,14},{6,2},{... | collective-permute-start | bytes 1179656 | tf_op jit(solution)/shard_map/ppermute | solution.py:469
  66.0 44.5 %copy-start.11 = (bf16[144,2048]{1,0:T(8,128)(2,1)}, bf16[144,2048]{1,0:T(8,128)(2,1)S(1)}, u32[]{:S(2)}) copy-start(bf16[144,2048]{1,0:T(8,128)(2,1)S(1)} %broadcast_select_fusion.1.refs_9_) | copy-start | bytes 1769476
  66.0 26.4 %collective-permute-start.5 = (bf16[256,768]{1,0:T(8,128)(2,1)S(1)}, bf16[256,768]{1,0:T(8,128)(2,1)}, u32[]{:S(2)}, u32[]{:S(2)}) collective-permute-start(bf16[256,768]{1,0:T(8,128)(2,1)S(1)} %get-tuple-element.37), channel_id=1, source_target_pairs={{0,4},{4,8},{8,12},{12,0},{1,5},{5,9},{9,13},{13,1},{2,6},{6,10},{... | collective-permute-start | bytes 1179656 | tf_op jit(solution)/shard_map/ppermute | solution.py:469
  66.1 24.6 %copy-start.22 = (bf16[112,2048]{1,0:T(8,128)(2,1)}, bf16[112,2048]{1,0:T(8,128)(2,1)S(1)}, u32[]{:S(2)}) copy-start(bf16[112,2048]{1,0:T(8,128)(2,1)S(1)} %collective-permute-done.24.refs_13_) | copy-start | bytes 1376260
  66.1 27.3 %collective-permute-start.7 = (bf16[256,768]{1,0:T(8,128)(2,1)S(1)}, bf16[256,768]{1,0:T(8,128)(2,1)S(1)}, u32[]{:S(2)}, u32[]{:S(2)}) collective-permute-start(bf16[256,768]{1,0:T(8,128)(2,1)S(1)} %get-tuple-element.34.refs_7_), channel_id=1, source_target_pairs={{0,16},{16,0},{1,17},{17,1},{2,18},{18,2},{3,19},{19,3},{4,20},{20... | collective-permute-start | bytes 1179656 | tf_op jit(solution)/shard_map/ppermute | solution.py:466
  67.7 49.9 %copy-start.21 = (bf16[144,2048]{1,0:T(8,128)(2,1)}, bf16[144,2048]{1,0:T(8,128)(2,1)S(1)}, u32[]{:S(2)}) copy-start(bf16[144,2048]{1,0:T(8,128)(2,1)S(1)} %collective-permute-done.23.refs_12_) | copy-start | bytes 1769476
  67.7 46.5 %collective-permute-start.14 = (bf16[144,2048]{1,0:T(8,128)(2,1)S(1)}, bf16[144,2048]{1,0:T(8,128)(2,1)}, u32[]{:S(2)}, u32[]{:S(2)}) collective-permute-start(bf16[144,2048]{1,0:T(8,128)(2,1)S(1)} %broadcast_select_fusion.1.refs_9_), channel_id=1, source_target_pairs={{8,12},{4,0},{9,13},{5,1},{10,14},{6,2},{11,15},{7,3},{24,28},{20,... | collective-permute-start | bytes 1769480 | tf_op jit(solution)/shard_map/ppermute | solution.py:530
  84.4 26.1 %copy-start.16 = (bf16[256,768]{1,0:T(8,128)(2,1)}, bf16[256,768]{1,0:T(8,128)(2,1)S(1)}, u32[]{:S(2)}) copy-start(bf16[256,768]{1,0:T(8,128)(2,1)S(1)} %collective-permute-done.1.refs_1_) | copy-start | bytes 1179652
  84.4 12.0 %collective-permute-start.2 = (bf16[256,768]{1,0:T(8,128)(2,1)S(1)}, bf16[256,768]{1,0:T(8,128)(2,1)S(1)}, u32[]{:S(2)}, u32[]{:S(2)}) collective-permute-start(bf16[256,768]{1,0:T(8,128)(2,1)S(1)} %collective-permute-done.1.refs_1_), channel_id=1, source_target_pairs={{0,16},{16,0},{1,17},{17,1},{2,18},{18,2},{3,19},{19,3},{4,20},{20... | collective-permute-start | bytes 1179656 | tf_op jit(solution)/shard_map/ppermute | solution.py:466
  90.8 7.2 %copy-start.17 = (bf16[256,768]{1,0:T(8,128)(2,1)}, bf16[256,768]{1,0:T(8,128)(2,1)S(1)}, u32[]{:S(2)}) copy-start(bf16[256,768]{1,0:T(8,128)(2,1)S(1)} %collective-permute-done.3.refs_3_) | copy-start | bytes 1179652
  90.8 13.4 %collective-permute-start.4 = (bf16[256,768]{1,0:T(8,128)(2,1)S(1)}, bf16[256,768]{1,0:T(8,128)(2,1)S(1)}, u32[]{:S(2)}, u32[]{:S(2)}) collective-permute-start(bf16[256,768]{1,0:T(8,128)(2,1)S(1)} %collective-permute-done.3.refs_3_), channel_id=1, source_target_pairs={{0,16},{16,0},{1,17},{17,1},{2,18},{18,2},{3,19},{19,3},{4,20},{20... | collective-permute-start | bytes 1179656 | tf_op jit(solution)/shard_map/ppermute | solution.py:466
  92.4 18.1 %copy-start.14 = (bf16[112,2048]{1,0:T(8,128)(2,1)}, bf16[112,2048]{1,0:T(8,128)(2,1)S(1)}, u32[]{:S(2)}) copy-start(bf16[112,2048]{1,0:T(8,128)(2,1)S(1)} %broadcast_select_fusion.2.refs_10_) | copy-start | bytes 1376260
  92.5 20.3 %collective-permute-start.27 = (bf16[112,2048]{1,0:T(8,128)(2,1)S(1)}, bf16[112,2048]{1,0:T(8,128)(2,1)}, u32[]{:S(2)}, u32[]{:S(2)}) collective-permute-start(bf16[112,2048]{1,0:T(8,128)(2,1)S(1)} %broadcast_select_fusion.2.refs_10_), channel_id=1, source_target_pairs={{0,2},{1,3},{2,0},{3,1},{4,6},{5,7},{6,4},{7,5},{8,10},{9,11},{10,... | collective-permute-start | bytes 1376264 | tf_op jit(solution)/shard_map/ppermute | solution.py:522
  93.5 10.7 %copy-start.18 = (bf16[256,768]{1,0:T(8,128)(2,1)}, bf16[256,768]{1,0:T(8,128)(2,1)S(1)}, u32[]{:S(2)}) copy-start(bf16[256,768]{1,0:T(8,128)(2,1)S(1)} %collective-permute-done.7.refs_8_) | copy-start | bytes 1179652
  93.5 17.8 %collective-permute-start.6 = (bf16[256,768]{1,0:T(8,128)(2,1)}, bf16[256,768]{1,0:T(8,128)(2,1)}, u32[]{:S(2)}, u32[]{:S(2)}) collective-permute-start(bf16[256,768]{1,0:T(8,128)(2,1)} %collective-permute-done.5.refs_5_), channel_id=1, source_target_pairs={{0,16},{16,0},{1,17},{17,1},{2,18},{18,2},{3,19},{19,3},{4,20},{20... | collective-permute-start | bytes 1179656 | tf_op jit(solution)/shard_map/ppermute | solution.py:466
  96.4 14.1 %copy-start.19 = (bf16[256,768]{1,0:T(8,128)(2,1)}, bf16[256,768]{1,0:T(8,128)(2,1)S(1)}, u32[]{:S(2)}) copy-start(bf16[256,768]{1,0:T(8,128)(2,1)S(1)} %collective-permute-done.2.refs_2_) | copy-start | bytes 1179652
  96.4 29.3 %collective-permute-start.26 = (bf16[144,2048]{1,0:T(8,128)(2,1)S(1)}, bf16[144,2048]{1,0:T(8,128)(2,1)}, u32[]{:S(2)}, u32[]{:S(2)}) collective-permute-start(bf16[144,2048]{1,0:T(8,128)(2,1)S(1)} %broadcast_select_fusion.1.refs_9_), channel_id=1, source_target_pairs={{0,2},{1,3},{2,0},{3,1},{4,6},{5,7},{6,4},{7,5},{8,10},{9,11},{10,... | collective-permute-start | bytes 1769480 | tf_op jit(solution)/shard_map/ppermute | solution.py:522
  104.9 20.7 %collective-permute-start.19 = (bf16[112,2048]{1,0:T(8,128)(2,1)S(1)}, bf16[112,2048]{1,0:T(8,128)(2,1)}, u32[]{:S(2)}, u32[]{:S(2)}) collective-permute-start(bf16[112,2048]{1,0:T(8,128)(2,1)S(1)} %broadcast_select_fusion.2.refs_10_), channel_id=1, source_target_pairs={{8,12},{4,0},{9,13},{5,1},{10,14},{6,2},{11,15},{7,3},{24,28},{20,... | collective-permute-start | bytes 1376264 | tf_op jit(solution)/shard_map/ppermute | solution.py:530
  111.3 23.9 %collective-permute-start.21 = (bf16[112,2048]{1,0:T(8,128)(2,1)S(1)}, bf16[112,2048]{1,0:T(8,128)(2,1)}, u32[]{:S(2)}, u32[]{:S(2)}) collective-permute-start(bf16[112,2048]{1,0:T(8,128)(2,1)S(1)} %collective-permute-done.12.refs_16_), channel_id=1, source_target_pairs={{4,6},{5,7},{6,4},{7,5},{8,10},{9,11},{10,8},{11,9},{20,22},{21,23... | collective-permute-start | bytes 1376264 | tf_op jit(solution)/shard_map/ppermute | solution.py:522
  112.7 22.7 %collective-permute-start.16 = (bf16[144,2048]{1,0:T(8,128)(2,1)S(1)}, bf16[144,2048]{1,0:T(8,128)(2,1)}, u32[]{:S(2)}, u32[]{:S(2)}) collective-permute-start(bf16[144,2048]{1,0:T(8,128)(2,1)S(1)} %collective-permute-done.8.refs_14_), channel_id=1, source_target_pairs={{4,6},{5,7},{6,4},{7,5},{8,10},{9,11},{10,8},{11,9},{20,22},{21,23... | collective-permute-start | bytes 1769480 | tf_op jit(solution)/shard_map/ppermute | solution.py:522
  114.2 26.6 %collective-permute-start.15 = (bf16[144,2048]{1,0:T(8,128)(2,1)}, bf16[144,2048]{1,0:T(8,128)(2,1)}, u32[]{:S(2)}, u32[]{:S(2)}) collective-permute-start(bf16[144,2048]{1,0:T(8,128)(2,1)} %collective-permute-done.14.refs_13_), channel_id=1, source_target_pairs={{0,2},{1,3},{2,0},{3,1},{12,14},{13,15},{14,12},{15,13},{16,18},{1... | collective-permute-start | bytes 1769480 | tf_op jit(solution)/shard_map/ppermute | solution.py:522
  125.7 35.0 %collective-permute-start.25 = (bf16[1024,384]{1,0:T(8,128)(2,1)}, bf16[1024,384]{1,0:T(8,128)(2,1)S(1)}, u32[]{:S(2)}, u32[]{:S(2)}) collective-permute-start(bf16[1024,384]{1,0:T(8,128)(2,1)} %get-tuple-element.31), channel_id=1, source_target_pairs={{0,1},{1,0},{2,3},{3,2},{4,5},{5,4},{6,7},{7,6},{8,9},{9,8},{10,11... | collective-permute-start | bytes 2359304 | tf_op jit(solution)/shard_map/ppermute | solution.py:463
  125.8 15.0 %collective-permute-start.20 = (bf16[112,2048]{1,0:T(8,128)(2,1)}, bf16[112,2048]{1,0:T(8,128)(2,1)S(1)}, u32[]{:S(2)}, u32[]{:S(2)}) collective-permute-start(bf16[112,2048]{1,0:T(8,128)(2,1)} %collective-permute-done.19.refs_15_), channel_id=1, source_target_pairs={{0,2},{1,3},{2,0},{3,1},{12,14},{13,15},{14,12},{15,13},{16,18},{1... | collective-permute-start | bytes 1376264 | tf_op jit(solution)/shard_map/ppermute | solution.py:522
  135.1 25.5 %collective-permute-start.28 = (bf16[768,384]{1,0:T(8,128)(2,1)}, bf16[768,384]{1,0:T(8,128)(2,1)S(1)}, u32[]{:S(2)}, u32[]{:S(2)}) collective-permute-start(bf16[768,384]{1,0:T(8,128)(2,1)} %get-tuple-element.33), channel_id=1, source_target_pairs={{0,1},{1,0},{2,3},{3,2},{4,5},{5,4},{6,7},{7,6},{8,9},{9,8},{10,11... | collective-permute-start | bytes 1769480 | tf_op jit(solution)/shard_map/ppermute | solution.py:463
  146.3 19.7 %collective-permute-start.22 = (bf16[256,384]{1,0:T(8,128)(2,1)}, bf16[256,384]{1,0:T(8,128)(2,1)S(1)}, u32[]{:S(2)}, u32[]{:S(2)}) collective-permute-start(bf16[256,384]{1,0:T(8,128)(2,1)} %get-tuple-element.28), channel_id=1, source_target_pairs={{0,1},{1,0},{2,3},{3,2},{4,5},{5,4},{6,7},{7,6},{8,9},{9,8},{10,11... | collective-permute-start | bytes 589832 | tf_op jit(solution)/shard_map/ppermute | solution.py:463
  146.4 13.9 %all-to-all-start = ((s32[4,1,512]{2,1,0:T(1,128)}), s32[4,1,512]{2,1,0:T(1,128)S(1)}, u32[]{:S(2)}, u32[]{:S(2)}) async-start(s32[4,1,512]{2,1,0:T(1,128)} %bitcast.29), calls=%async_computation | async-start | bytes 16384 | tf_op jit(solution)/shard_map/all_to_all | solution.py:491
  161.7 4.3 %copy-start.3 = (f32[256,384]{1,0:T(8,128)S(1)}, f32[256,384]{1,0:T(8,128)}, u32[]{:S(2)}) copy-start(f32[256,384]{1,0:T(8,128)} %get-tuple-element.27.kept_ref) | copy-start | bytes 1179652
  179.9 13.1 %copy-start.4 = (f32[4,64,128]{2,1,0:T(8,128)S(1)}, f32[4,64,128]{2,1,0:T(8,128)}, u32[]{:S(2)}) copy-start(f32[4,64,128]{2,1,0:T(8,128)} %refs_5_.1) | copy-start | bytes 393220
  179.9 8.6 %collective-permute-start.29 = (bf16[576,128]{1,0:T(8,128)(2,1)S(1)}, bf16[576,128]{1,0:T(8,128)(2,1)S(1)}, u32[]{:S(2)}, u32[]{:S(2)}) collective-permute-start(bf16[576,128]{1,0:T(8,128)(2,1)S(1)} %attend.5), channel_id=1, source_target_pairs={{0,4},{4,8},{8,12},{12,0},{1,5},{5,9},{9,13},{13,1},{2,6},{6,10},{... | collective-permute-start | bytes 442376 | tf_op jit(solution)/shard_map/ppermute | solution.py:469
  180.0 13.0 %collective-permute-start.30 = (bf16[576,128]{1,0:T(8,128)(2,1)S(1)}, bf16[576,128]{1,0:T(8,128)(2,1)S(1)}, u32[]{:S(2)}, u32[]{:S(2)}) collective-permute-start(bf16[576,128]{1,0:T(8,128)(2,1)S(1)} %attend.6), channel_id=1, source_target_pairs={{0,8},{4,12},{8,0},{12,4},{1,9},{5,13},{9,1},{13,5},{2,10},{6,14},... | collective-permute-start | bytes 442376 | tf_op jit(solution)/shard_map/ppermute | solution.py:469
  180.1 12.9 %collective-permute-start.31 = (bf16[576,128]{1,0:T(8,128)(2,1)S(1)}, bf16[576,128]{1,0:T(8,128)(2,1)S(1)}, u32[]{:S(2)}, u32[]{:S(2)}) collective-permute-start(bf16[576,128]{1,0:T(8,128)(2,1)S(1)} %attend.7), channel_id=1, source_target_pairs={{0,12},{4,0},{8,4},{12,8},{1,13},{5,1},{9,5},{13,9},{2,14},{6,2},{... | collective-permute-start | bytes 442376 | tf_op jit(solution)/shard_map/ppermute | solution.py:469
  (8 other events, 9.2 us)

commit v3 on v2

--- a/solution.py
+++ b/solution.py
@@ -94,7 +94,7 @@
 def attend_kernel(hs, local_rows, place, qkv_ref, id_col_ref, id_row_ref, out_ref):
     rows = qkv_ref.shape[0]
     owned = out_ref.shape[0] - local_rows
-    block = min(256, local_rows)
+    block = min(512, local_rows)
     scale = hs ** (-0.5) * LOG2_E
     at = place[0] * local_rows
 
@@ -200,6 +200,22 @@
         cost_estimate=pl.CostEstimate(flops=0, bytes_accessed=1 << 20, transcendentals=0),
         name="collect",
     )(place, *pieces, centroids)
+
+
+def hold_kernel(in_ref, out_ref):
+    for i in range(in_ref.shape[0]):
+        out_ref[i] = in_ref[i]
+
+
+def hold(values):
+    smem = pl.BlockSpec(memory_space=pltpu.SMEM)
+    return pl.pallas_call(
+        hold_kernel,
+        out_shape=jax.ShapeDtypeStruct(values.shape, values.dtype),
+        in_specs=[smem],
+        out_specs=smem,
+        name="hold",
+    )(values)
 
 
 def start_one(copies, flag):
@@ -538,7 +554,7 @@
         for g in range(groups):
             laid.append(shift_y(piece, g) if g else piece)
             spots.append((z - d) % seq * groups + (y - g) % groups)
-    spots = jnp.stack([*spots, inner]).astype(jnp.int32)
+    spots = hold(jnp.stack([*spots, inner]).astype(jnp.int32))
 
     def place(source, d):
         return source * xs + (x - d) % xs

time: 195 us -> 194 us (level)
    pallas_call x4, Pallas kernels: 11.1 us -> 8.95 us  [attend(): pl.pallas_call(lambda *refs: attend_kernel(hs, rows // seq, *refs), out_s...]
  transfers between devices with their start and end apart: 33 -> 33, of which waited for: 11 -> 11; matrix products, arithmetic and copies ran while one was open for 1% -> 1% of each run, Pallas kernels for 17% -> 18%
where the time goes in v3:
time: 194 us; the launch traced here: 193 us
  waiting for transfers between devices  82 us (42%)
  starting transfers between devices  53.8 us (28%)
  Pallas kernels  46.1 us (24%)
  local copies, waits for them, and re-layouts  8.27 us (4%)
    ppermute x6, waiting for transfers between devices, shift_z(): return lax.ppermute(v, 'seq', [(i, (i + d) % seq) for i in range(seq)])  28.2 us
    ppermute x2, waiting for transfers between devices, by_head(): left.append([lax.ppermute(v, 'seq', leftward(2)) for v in left[1]])  20.1 us
    pallas_call x3, Pallas kernels, project(): pl.pallas_call(lambda *refs: project_kernel(len(weights), choices, *refs)...  19.7 us
    ppermute x8, starting transfers between devices, shares_x(): return [lax.ppermute(v, ('seq', 'head'), pairs) for v in values]  13.4 us
    ppermute x2, waiting for transfers between devices, by_head(): right.append([lax.ppermute(v, 'seq', rightward(1)) for v in mine])  10.8 us
    ppermute x2, starting transfers between devices, by_head(): right.append([lax.ppermute(v, 'seq', rightward(1)) for v in mine])  10.3 us
    ppermute x4, waiting for transfers between devices, shift_y(): lax.ppermute(v, 'groups', [(i, (i + d) % groups) for i in range(groups)])  9.19 us
    pallas_call x4, Pallas kernels, attend(): pl.pallas_call(lambda *refs: attend_kernel(hs, rows // seq, *refs), out_s...  8.95 us
  transfers between devices with their start and end apart: 33, of which 11 were waited for; matrix products, arithmetic and copies ran while one was open for 1% of the time, Pallas kernels for 18%

profile of v3, /device:TPU:0, one launch (start us, length us, event | category | flops | bytes accessed | tf_op | source)
XLA Modules:
  0.0 193.0 jit_solution(8061054313533465555)
XLA Ops:
  1.2 3.0 %take.2 = (bf16[144,2048]{1,0:T(8,128)(2,1)}, bf16[112,2048]{1,0:T(8,128)(2,1)}) custom-call(s32[2]{0:T(128)} %pad_add_fusion.1.refs_0_, bf16[512,4096]{1,0:T(8,128)(2,1)} %refs_1_.4), custom_call_target="tpu_custom_call" | custom-call | bytes 2097152 | tf_op jit(solution)/shard_map/take/pallas_call | solution.py:411
  4.2 5.0 %collective-permute-start.10 = (bf16[144,2048]{1,0:T(8,128)(2,1)}, bf16[144,2048]{1,0:T(8,128)(2,1)S(1)}, u32[]{:S(2)}, u32[]{:S(2)}) collective-permute-start(bf16[144,2048]{1,0:T(8,128)(2,1)} %get-tuple-element.18), channel_id=1, source_target_pairs={{0,4},{4,8},{8,12},{1,5},{5,9},{9,13},{2,6},{6,10},{10,14},{3,7},{... | collective-permute-start | bytes 1769480 | tf_op jit(solution)/shard_map/ppermute | solution.py:497
  9.2 1.3 collective-permute-start.8
  10.5 5.3 %collective-permute-start.13 = (bf16[112,2048]{1,0:T(8,128)(2,1)}, bf16[112,2048]{1,0:T(8,128)(2,1)}, u32[]{:S(2)}, u32[]{:S(2)}) collective-permute-start(bf16[112,2048]{1,0:T(8,128)(2,1)} %get-tuple-element.19), channel_id=1, source_target_pairs={{0,4},{4,8},{8,12},{1,5},{5,9},{9,13},{2,6},{6,10},{10,14},{3,7},{... | collective-permute-start | bytes 1376264 | tf_op jit(solution)/shard_map/ppermute | solution.py:497
  15.9 1.3 collective-permute-start.12
  17.2 2.0 %unpack.3 = bf16[4,256,384]{2,1,0:T(8,128)(2,1)} custom-call(s32[1]{0:T(128)} %bitcast.17.refs_0_, bf16[3,1024,512]{2,1,0:T(8,128)(2,1)} %refs_1_.3), custom_call_target="tpu_custom_call" | custom-call | bytes 1572864 | tf_op jit(solution)/shard_map/unpack/pallas_call | solution.py:445
  19.2 1.9 %unpack.2 = bf16[4,256,384]{2,1,0:T(8,128)(2,1)} custom-call(s32[1]{0:T(128)} %bitcast.14.refs_0_, bf16[3,1024,512]{2,1,0:T(8,128)(2,1)} %refs_1_.3), custom_call_target="tpu_custom_call" | custom-call | bytes 1572864 | tf_op jit(solution)/shard_map/unpack/pallas_call | solution.py:445
  21.1 10.8 %collective-permute-done.13 = bf16[112,2048]{1,0:T(8,128)(2,1)} collective-permute-done((bf16[112,2048]{1,0:T(8,128)(2,1)}, bf16[112,2048]{1,0:T(8,128)(2,1)}, u32[]{:S(2)}, u32[]{:S(2)}) %collective-permute-start.13) | collective-permute-done | bytes 458784 | tf_op jit(solution)/shard_map/ppermute | solution.py:497
  32.6 3.4 %collective-permute-done.12.refs_16_ = bf16[112,2048]{1,0:T(8,128)(2,1)S(1)} collective-permute-done((bf16[112,2048]{1,0:T(8,128)(2,1)}, bf16[112,2048]{1,0:T(8,128)(2,1)S(1)}, u32[]{:S(2)}, u32[]{:S(2)}) %collective-permute-start.12) | collective-permute-done | bytes 458784 | tf_op jit(solution)/shard_map/ppermute | solution.py:498
  36.0 1.3 collective-permute-start.17
  38.1 1.3 collective-permute-start.9
  39.5 1.6 collective-permute-start.23
  41.8 20.1 %collective-permute-done.9 = bf16[144,2048]{1,0:T(8,128)(2,1)S(1)} collective-permute-done((bf16[144,2048]{1,0:T(8,128)(2,1)S(1)}, bf16[144,2048]{1,0:T(8,128)(2,1)S(1)}, u32[]{:S(2)}, u32[]{:S(2)}) %collective-permute-start.9) | collective-permute-done | bytes 589856 | tf_op jit(solution)/shard_map/ppermute | solution.py:517
  61.9 1.2 collective-permute-start.1
  63.1 2.9 %collective-permute-start.3 = (bf16[256,768]{1,0:T(8,128)(2,1)S(1)}, bf16[256,768]{1,0:T(8,128)(2,1)S(1)}, u32[]{:S(2)}, u32[]{:S(2)}) collective-permute-start(bf16[256,768]{1,0:T(8,128)(2,1)S(1)} %get-tuple-element.36), channel_id=1, source_target_pairs={{0,12},{4,0},{8,4},{12,8},{1,13},{5,1},{9,5},{13,9},{2,14},{6,2},{... | collective-permute-start | bytes 1179656 | tf_op jit(solution)/shard_map/ppermute | solution.py:485
  66.1 1.6 collective-permute-start.7
  67.7 1.3 collective-permute-start.14
  69.0 15.4 %collective-permute-done.1.refs_1_ = bf16[256,768]{1,0:T(8,128)(2,1)S(1)} collective-permute-done((bf16[256,768]{1,0:T(8,128)(2,1)S(1)}, bf16[256,768]{1,0:T(8,128)(2,1)S(1)}, u32[]{:S(2)}, u32[]{:S(2)}) %collective-permute-start.1) | collective-permute-done | bytes 393248 | tf_op jit(solution)/shard_map/ppermute | solution.py:485
  84.4 1.5 collective-permute-start.2
  86.0 4.8 %collective-permute-done.3.refs_3_ = bf16[256,768]{1,0:T(8,128)(2,1)S(1)} collective-permute-done((bf16[256,768]{1,0:T(8,128)(2,1)S(1)}, bf16[256,768]{1,0:T(8,128)(2,1)S(1)}, u32[]{:S(2)}, u32[]{:S(2)}) %collective-permute-start.3) | collective-permute-done | bytes 393248 | tf_op jit(solution)/shard_map/ppermute | solution.py:485
  90.8 1.6 collective-permute-start.4
  93.5 3.0 %collective-permute-done.2.refs_2_ = bf16[256,768]{1,0:T(8,128)(2,1)S(1)} collective-permute-done((bf16[256,768]{1,0:T(8,128)(2,1)S(1)}, bf16[256,768]{1,0:T(8,128)(2,1)S(1)}, u32[]{:S(2)}, u32[]{:S(2)}) %collective-permute-start.2) | collective-permute-done | bytes 393248 | tf_op jit(solution)/shard_map/ppermute | solution.py:482
  96.4 1.5 collective-permute-start.26
  97.9 6.2 %collective-permute-done.4.refs_4_ = bf16[256,768]{1,0:T(8,128)(2,1)S(1)} collective-permute-done((bf16[256,768]{1,0:T(8,128)(2,1)S(1)}, bf16[256,768]{1,0:T(8,128)(2,1)S(1)}, u32[]{:S(2)}, u32[]{:S(2)}) %collective-permute-start.4) | collective-permute-done | bytes 393248 | tf_op jit(solution)/shard_map/ppermute | solution.py:482
  104.9 1.3 collective-permute-start.19
  107.0 1.2 hold.1.refs_0_
  108.7 3.6 %take.3.refs_9_ = bf16[512,2048]{1,0:T(8,128)(2,1)} custom-call(s32[2]{0:T(128)} %pad_add_fusion.2.refs_0_, bf16[512,4096]{1,0:T(8,128)(2,1)} %refs_1_.4), custom_call_target="tpu_custom_call" | custom-call | bytes 4194304 | tf_op jit(solution)/shard_map/take/pallas_call | solution.py:411
  112.4 1.5 collective-permute-start.21
  113.9 1.5 collective-permute-start.16
  115.3 3.4 %collective-permute-start.15 = (bf16[144,2048]{1,0:T(8,128)(2,1)}, bf16[144,2048]{1,0:T(8,128)(2,1)}, u32[]{:S(2)}, u32[]{:S(2)}) collective-permute-start(bf16[144,2048]{1,0:T(8,128)(2,1)} %collective-permute-done.14.refs_13_), channel_id=1, source_target_pairs={{0,2},{1,3},{2,0},{3,1},{12,14},{13,15},{14,12},{15,13},{16,18},{1... | collective-permute-start | bytes 1769480 | tf_op jit(solution)/shard_map/ppermute | solution.py:538
  118.8 8.0 %project.4 = (f32[1024,384]{1,0:T(8,128)}, bf16[1024,384]{1,0:T(8,128)(2,1)}) custom-call(s32[9]{0:T(128)} %hold.1.refs_0_, bf16[256,768]{1,0:T(8,128)(2,1)} %copy-done.16, bf16[256,768]{1,0:T(8,128)(2,1)} %copy-done.19, bf16[256,768]{1,0:T(8,128)(2,1)} %copy-done.17, bf16[256,768]{1,0:T(8,128)(2,1)} %copy-done.20, ...), custom_call_target="tpu_custom_call" | custom-call | flops 3221225472 | bytes 10485760 | tf_op jit(solution)/shard_map/project/pallas_call | solution.py:283
  126.9 2.4 %collective-permute-start.20 = (bf16[112,2048]{1,0:T(8,128)(2,1)}, bf16[112,2048]{1,0:T(8,128)(2,1)S(1)}, u32[]{:S(2)}, u32[]{:S(2)}) collective-permute-start(bf16[112,2048]{1,0:T(8,128)(2,1)} %collective-permute-done.19.refs_15_), channel_id=1, source_target_pairs={{0,2},{1,3},{2,0},{3,1},{12,14},{13,15},{14,12},{15,13},{16,18},{1... | collective-permute-start | bytes 1376264 | tf_op jit(solution)/shard_map/ppermute | solution.py:538
  129.3 6.9 %project.5 = (f32[768,384]{1,0:T(8,128)}, bf16[768,384]{1,0:T(8,128)(2,1)}) custom-call(s32[9]{0:T(128)} %hold.1.refs_0_, bf16[256,768]{1,0:T(8,128)(2,1)} %copy-done.16, bf16[256,768]{1,0:T(8,128)(2,1)} %copy-done.19, bf16[256,768]{1,0:T(8,128)(2,1)} %copy-done.17, bf16[256,768]{1,0:T(8,128)(2,1)} %copy-done.20, ...), custom_call_target="tpu_custom_call" | custom-call | flops 2415919104 | bytes 8650752 | tf_op jit(solution)/shard_map/project/pallas_call | solution.py:283
  136.5 5.4 %collective-permute-done.20.refs_11_ = bf16[112,2048]{1,0:T(8,128)(2,1)S(1)} collective-permute-done((bf16[112,2048]{1,0:T(8,128)(2,1)}, bf16[112,2048]{1,0:T(8,128)(2,1)S(1)}, u32[]{:S(2)}, u32[]{:S(2)}) %collective-permute-start.20) | collective-permute-done | bytes 458784 | tf_op jit(solution)/shard_map/ppermute | solution.py:538
  142.7 4.7 %project.3 = (f32[256,384]{1,0:T(8,128)}, bf16[256,384]{1,0:T(8,128)(2,1)}) custom-call(s32[9]{0:T(128)} %hold.1.refs_0_, bf16[256,768]{1,0:T(8,128)(2,1)} %copy-done.16, bf16[256,768]{1,0:T(8,128)(2,1)} %copy-done.19, bf16[256,768]{1,0:T(8,128)(2,1)} %copy-done.17, bf16[256,768]{1,0:T(8,128)(2,1)} %copy-done.20, ...), custom_call_target="tpu_custom_call" | custom-call | flops 805306368 | bytes 4980736 | tf_op jit(solution)/shard_map/project/pallas_call | solution.py:283
  147.5 7.8 %all-to-all-start = ((s32[4,1,512]{2,1,0:T(1,128)}), s32[4,1,512]{2,1,0:T(1,128)S(1)}, u32[]{:S(2)}, u32[]{:S(2)}) async-start(s32[4,1,512]{2,1,0:T(1,128)} %bitcast.29), calls=%async_computation | async-start | bytes 16384 | tf_op jit(solution)/shard_map/all_to_all | solution.py:507
  155.9 5.0 %all-to-all-done = s32[4,1,512]{2,1,0:T(1,128)S(1)} async-done(((s32[4,1,512]{2,1,0:T(1,128)}), s32[4,1,512]{2,1,0:T(1,128)S(1)}, u32[]{:S(2)}, u32[]{:S(2)}) %all-to-all-start) | async-done | bytes 8224 | tf_op jit(solution)/shard_map/all_to_all | solution.py:507
  162.3 4.3 %merge.1.base_ref = bf16[2048,384]{1,0:T(8,128)(2,1)} custom-call(s32[7]{0:T(128)} %stack.133.refs_0_, f32[1024,384]{1,0:T(8,128)} %get-tuple-element.30.refs_1_, bf16[1024,384]{1,0:T(8,128)(2,1)} %copy-done.7, f32[768,384]{1,0:T(8,128)} %get-tuple-element.32.refs_3_, bf16[768,384]{1,0:T(8,128)(2,1)} %copy-done.8), custom_call_target="tpu_custom_call" | custom-call | flops 786432 | bytes 6291456 | tf_op jit(solution)/shard_map/merge/pallas_call | solution.py:341
  166.6 1.4 copy-done
  168.1 1.2 copy-done.1
  169.2 1.4 copy-done.2
  170.6 3.2 %attend.7 = bf16[576,128]{1,0:T(8,128)(2,1)S(1)} custom-call(s32[1]{0:T(128)} %bitcast.34.refs_0_, bf16[2048,384]{1,0:T(8,128)(2,1)S(1)} %copy-done.2, s32[2048,1]{1,0:T(8,128)S(1)} %copy.7.refs_2_, s32[1,2048]{1,0:T(1,128)S(1)} %bitcast.40), custom_call_target="tpu_custom_call" | custom-call | flops 536870912 | bytes 2097152 | tf_op jit(solution)/shard_map/attend/pallas_call | solution.py:157
  173.9 2.5 %attend.6 = bf16[576,128]{1,0:T(8,128)(2,1)S(1)} custom-call(s32[1]{0:T(128)} %bitcast.33.refs_0_, bf16[2048,384]{1,0:T(8,128)(2,1)S(1)} %copy-done.2, s32[2048,1]{1,0:T(8,128)S(1)} %copy.7.refs_2_, s32[1,2048]{1,0:T(1,128)S(1)} %bitcast.41), custom_call_target="tpu_custom_call" | custom-call | flops 536870912 | bytes 2097152 | tf_op jit(solution)/shard_map/attend/pallas_call | solution.py:157
  176.4 2.1 %attend.5 = bf16[576,128]{1,0:T(8,128)(2,1)S(1)} custom-call(s32[1]{0:T(128)} %bitcast.32.refs_0_, bf16[2048,384]{1,0:T(8,128)(2,1)S(1)} %copy-done.2, s32[2048,1]{1,0:T(8,128)S(1)} %copy.7.refs_2_, s32[1,2048]{1,0:T(1,128)S(1)} %bitcast.42), custom_call_target="tpu_custom_call" | custom-call | flops 536870912 | bytes 2097152 | tf_op jit(solution)/shard_map/attend/pallas_call | solution.py:157
  178.6 3.7 %collective-permute-start.31 = (bf16[576,128]{1,0:T(8,128)(2,1)S(1)}, bf16[576,128]{1,0:T(8,128)(2,1)S(1)}, u32[]{:S(2)}, u32[]{:S(2)}) collective-permute-start(bf16[576,128]{1,0:T(8,128)(2,1)S(1)} %attend.7), channel_id=1, source_target_pairs={{0,12},{4,0},{8,4},{12,8},{1,13},{5,1},{9,5},{13,9},{2,14},{6,2},{... | collective-permute-start | bytes 442376 | tf_op jit(solution)/shard_map/ppermute | solution.py:485
  183.6 3.5 %collective-permute-done.29.refs_2_ = bf16[576,128]{1,0:T(8,128)(2,1)S(1)} collective-permute-done((bf16[576,128]{1,0:T(8,128)(2,1)S(1)}, bf16[576,128]{1,0:T(8,128)(2,1)S(1)}, u32[]{:S(2)}, u32[]{:S(2)}) %collective-permute-start.29) | collective-permute-done | bytes 147488 | tf_op jit(solution)/shard_map/ppermute | solution.py:485
  187.1 4.5 %collective-permute-done.30.refs_3_ = bf16[576,128]{1,0:T(8,128)(2,1)S(1)} collective-permute-done((bf16[576,128]{1,0:T(8,128)(2,1)S(1)}, bf16[576,128]{1,0:T(8,128)(2,1)S(1)}, u32[]{:S(2)}, u32[]{:S(2)}) %collective-permute-start.30) | collective-permute-done | bytes 147488 | tf_op jit(solution)/shard_map/ppermute | solution.py:485
  191.6 1.5 collect.1
  (90 shorter events, 10.7 us)
Async XLA Ops:
  4.2 33.0 %collective-permute-start.10 = (bf16[144,2048]{1,0:T(8,128)(2,1)}, bf16[144,2048]{1,0:T(8,128)(2,1)S(1)}, u32[]{:S(2)}, u32[]{:S(2)}) collective-permute-start(bf16[144,2048]{1,0:T(8,128)(2,1)} %get-tuple-element.18), channel_id=1, source_target_pairs={{0,4},{4,8},{8,12},{1,5},{5,9},{9,13},{2,6},{6,10},{10,14},{3,7},{... | collective-permute-start | bytes 1769480 | tf_op jit(solution)/shard_map/ppermute | solution.py:497
  9.2 28.0 %collective-permute-start.8 = (bf16[144,2048]{1,0:T(8,128)(2,1)}, bf16[144,2048]{1,0:T(8,128)(2,1)S(1)}, u32[]{:S(2)}, u32[]{:S(2)}) collective-permute-start(bf16[144,2048]{1,0:T(8,128)(2,1)} %get-tuple-element.18), channel_id=1, source_target_pairs={{4,0},{8,4},{12,8},{5,1},{9,5},{13,9},{6,2},{10,6},{14,10},{7,3},{... | collective-permute-start | bytes 1769480 | tf_op jit(solution)/shard_map/ppermute | solution.py:498
  10.5 21.4 %collective-permute-start.13 = (bf16[112,2048]{1,0:T(8,128)(2,1)}, bf16[112,2048]{1,0:T(8,128)(2,1)}, u32[]{:S(2)}, u32[]{:S(2)}) collective-permute-start(bf16[112,2048]{1,0:T(8,128)(2,1)} %get-tuple-element.19), channel_id=1, source_target_pairs={{0,4},{4,8},{8,12},{1,5},{5,9},{9,13},{2,6},{6,10},{10,14},{3,7},{... | collective-permute-start | bytes 1376264 | tf_op jit(solution)/shard_map/ppermute | solution.py:497
  15.9 20.1 %collective-permute-start.12 = (bf16[112,2048]{1,0:T(8,128)(2,1)}, bf16[112,2048]{1,0:T(8,128)(2,1)S(1)}, u32[]{:S(2)}, u32[]{:S(2)}) collective-permute-start(bf16[112,2048]{1,0:T(8,128)(2,1)} %get-tuple-element.19), channel_id=1, source_target_pairs={{4,0},{8,4},{12,8},{5,1},{9,5},{13,9},{6,2},{10,6},{14,10},{7,3},{... | collective-permute-start | bytes 1376264 | tf_op jit(solution)/shard_map/ppermute | solution.py:498
  19.2 20.3 %collective-permute-start = (bf16[4,256,384]{2,1,0:T(8,128)(2,1)}, bf16[4,256,384]{2,1,0:T(8,128)(2,1)S(1)}, u32[]{:S(2)}, u32[]{:S(2)}) collective-permute-start(bf16[4,256,384]{2,1,0:T(8,128)(2,1)} %unpack.3), channel_id=1, source_target_pairs={{0,1},{1,0},{2,3},{3,2},{4,5},{5,4},{6,7},{7,6},{8,9},{9,8},{10,11... | collective-permute-start | bytes 2359304 | tf_op jit(solution)/shard_map/ppermute | solution.py:479
  21.1 19.9 %copy-start.5 = (bf16[4,256,384]{2,1,0:T(8,128)(2,1)S(1)}, bf16[4,256,384]{2,1,0:T(8,128)(2,1)}, u32[]{:S(2)}) copy-start(bf16[4,256,384]{2,1,0:T(8,128)(2,1)} %unpack.2) | copy-start | bytes 2359300
  31.9 31.1 %collective-permute-start.18 = (bf16[112,2048]{1,0:T(8,128)(2,1)}, bf16[112,2048]{1,0:T(8,128)(2,1)S(1)}, u32[]{:S(2)}, u32[]{:S(2)}) collective-permute-start(bf16[112,2048]{1,0:T(8,128)(2,1)} %collective-permute-done.13), channel_id=1, source_target_pairs={{4,8},{8,12},{5,9},{9,13},{6,10},{10,14},{7,11},{11,15},{20,24},{2... | collective-permute-start | bytes 1376264 | tf_op jit(solution)/shard_map/ppermute | solution.py:516
  36.0 76.4 %copy-start.12 = (bf16[112,2048]{1,0:T(8,128)(2,1)}, bf16[112,2048]{1,0:T(8,128)(2,1)S(1)}, u32[]{:S(2)}) copy-start(bf16[112,2048]{1,0:T(8,128)(2,1)S(1)} %collective-permute-done.12.refs_16_) | copy-start | bytes 1376260
  36.0 30.1 %collective-permute-start.17 = (bf16[112,2048]{1,0:T(8,128)(2,1)S(1)}, bf16[112,2048]{1,0:T(8,128)(2,1)S(1)}, u32[]{:S(2)}, u32[]{:S(2)}) collective-permute-start(bf16[112,2048]{1,0:T(8,128)(2,1)S(1)} %collective-permute-done.12.refs_16_), channel_id=1, source_target_pairs={{4,0},{8,4},{5,1},{9,5},{6,2},{10,6},{7,3},{11,7},{20,16},{24,20},... | collective-permute-start | bytes 1376264 | tf_op jit(solution)/shard_map/ppermute | solution.py:517
  37.3 76.6 %copy-start.9 = (bf16[144,2048]{1,0:T(8,128)(2,1)}, bf16[144,2048]{1,0:T(8,128)(2,1)S(1)}, u32[]{:S(2)}) copy-start(bf16[144,2048]{1,0:T(8,128)(2,1)S(1)} %collective-permute-done.8.refs_14_) | copy-start | bytes 1769476
  37.4 3.8 %copy-start.10 = (bf16[144,2048]{1,0:T(8,128)(2,1)}, bf16[144,2048]{1,0:T(8,128)(2,1)S(1)}, u32[]{:S(2)}) copy-start(bf16[144,2048]{1,0:T(8,128)(2,1)S(1)} %broadcast_select_fusion.refs_10_) | copy-start | bytes 1769476
  37.4 3.8 %collective-permute-start.11 = (bf16[144,2048]{1,0:T(8,128)(2,1)S(1)}, bf16[144,2048]{1,0:T(8,128)(2,1)S(1)}, u32[]{:S(2)}, u32[]{:S(2)}) collective-permute-start(bf16[144,2048]{1,0:T(8,128)(2,1)S(1)} %collective-permute-done.10), channel_id=1, source_target_pairs={{4,8},{8,12},{5,9},{9,13},{6,10},{10,14},{7,11},{11,15},{20,24},{2... | collective-permute-start | bytes 1769480 | tf_op jit(solution)/shard_map/ppermute | solution.py:516
  38.1 23.8 %collective-permute-start.9 = (bf16[144,2048]{1,0:T(8,128)(2,1)S(1)}, bf16[144,2048]{1,0:T(8,128)(2,1)S(1)}, u32[]{:S(2)}, u32[]{:S(2)}) collective-permute-start(bf16[144,2048]{1,0:T(8,128)(2,1)S(1)} %collective-permute-done.8.refs_14_), channel_id=1, source_target_pairs={{4,0},{8,4},{5,1},{9,5},{6,2},{10,6},{7,3},{11,7},{20,16},{24,20},... | collective-permute-start | bytes 1769480 | tf_op jit(solution)/shard_map/ppermute | solution.py:517
  39.5 28.2 %collective-permute-start.23 = (bf16[144,2048]{1,0:T(8,128)(2,1)S(1)}, bf16[144,2048]{1,0:T(8,128)(2,1)S(1)}, u32[]{:S(2)}, u32[]{:S(2)}) collective-permute-start(bf16[144,2048]{1,0:T(8,128)(2,1)S(1)} %broadcast_select_fusion.refs_10_), channel_id=1, source_target_pairs={{0,2},{1,3},{2,0},{3,1},{4,6},{5,7},{6,4},{7,5},{8,10},{9,11},{10,... | collective-permute-start | bytes 1769480 | tf_op jit(solution)/shard_map/ppermute | solution.py:538
  41.2 51.3 %copy-start.6 = (bf16[256,768]{1,0:T(8,128)(2,1)}, bf16[256,768]{1,0:T(8,128)(2,1)S(1)}, u32[]{:S(2)}) copy-start(bf16[256,768]{1,0:T(8,128)(2,1)S(1)} %get-tuple-element.34.refs_7_) | copy-start | bytes 1179652
  41.2 24.9 %collective-permute-start.24 = (bf16[112,2048]{1,0:T(8,128)(2,1)S(1)}, bf16[112,2048]{1,0:T(8,128)(2,1)S(1)}, u32[]{:S(2)}, u32[]{:S(2)}) collective-permute-start(bf16[112,2048]{1,0:T(8,128)(2,1)S(1)} %broadcast_select_fusion.3.refs_11_), channel_id=1, source_target_pairs={{0,2},{1,3},{2,0},{3,1},{4,6},{5,7},{6,4},{7,5},{8,10},{9,11},{10,... | collective-permute-start | bytes 1376264 | tf_op jit(solution)/shard_map/ppermute | solution.py:538
  61.9 22.6 %collective-permute-start.1 = (bf16[256,768]{1,0:T(8,128)(2,1)S(1)}, bf16[256,768]{1,0:T(8,128)(2,1)S(1)}, u32[]{:S(2)}, u32[]{:S(2)}) collective-permute-start(bf16[256,768]{1,0:T(8,128)(2,1)S(1)} %get-tuple-element.35), channel_id=1, source_target_pairs={{0,8},{4,12},{8,0},{12,4},{1,9},{5,13},{9,1},{13,5},{2,10},{6,14},... | collective-permute-start | bytes 1179656 | tf_op jit(solution)/shard_map/ppermute | solution.py:485
  63.1 27.7 %collective-permute-start.3 = (bf16[256,768]{1,0:T(8,128)(2,1)S(1)}, bf16[256,768]{1,0:T(8,128)(2,1)S(1)}, u32[]{:S(2)}, u32[]{:S(2)}) collective-permute-start(bf16[256,768]{1,0:T(8,128)(2,1)S(1)} %get-tuple-element.36), channel_id=1, source_target_pairs={{0,12},{4,0},{8,4},{12,8},{1,13},{5,1},{9,5},{13,9},{2,14},{6,2},{... | collective-permute-start | bytes 1179656 | tf_op jit(solution)/shard_map/ppermute | solution.py:485
  66.0 46.3 %copy-start.11 = (bf16[144,2048]{1,0:T(8,128)(2,1)}, bf16[144,2048]{1,0:T(8,128)(2,1)S(1)}, u32[]{:S(2)}) copy-start(bf16[144,2048]{1,0:T(8,128)(2,1)S(1)} %broadcast_select_fusion.1.refs_9_) | copy-start | bytes 1769476
  66.0 26.4 %collective-permute-start.5 = (bf16[256,768]{1,0:T(8,128)(2,1)S(1)}, bf16[256,768]{1,0:T(8,128)(2,1)}, u32[]{:S(2)}, u32[]{:S(2)}) collective-permute-start(bf16[256,768]{1,0:T(8,128)(2,1)S(1)} %get-tuple-element.37), channel_id=1, source_target_pairs={{0,4},{4,8},{8,12},{12,0},{1,5},{5,9},{9,13},{13,1},{2,6},{6,10},{... | collective-permute-start | bytes 1179656 | tf_op jit(solution)/shard_map/ppermute | solution.py:485
  66.1 24.6 %copy-start.22 = (bf16[112,2048]{1,0:T(8,128)(2,1)}, bf16[112,2048]{1,0:T(8,128)(2,1)S(1)}, u32[]{:S(2)}) copy-start(bf16[112,2048]{1,0:T(8,128)(2,1)S(1)} %collective-permute-done.24.refs_13_) | copy-start | bytes 1376260
  66.1 27.3 %collective-permute-start.7 = (bf16[256,768]{1,0:T(8,128)(2,1)S(1)}, bf16[256,768]{1,0:T(8,128)(2,1)S(1)}, u32[]{:S(2)}, u32[]{:S(2)}) collective-permute-start(bf16[256,768]{1,0:T(8,128)(2,1)S(1)} %get-tuple-element.34.refs_7_), channel_id=1, source_target_pairs={{0,16},{16,0},{1,17},{17,1},{2,18},{18,2},{3,19},{19,3},{4,20},{20... | collective-permute-start | bytes 1179656 | tf_op jit(solution)/shard_map/ppermute | solution.py:482
  67.7 51.0 %copy-start.21 = (bf16[144,2048]{1,0:T(8,128)(2,1)}, bf16[144,2048]{1,0:T(8,128)(2,1)S(1)}, u32[]{:S(2)}) copy-start(bf16[144,2048]{1,0:T(8,128)(2,1)S(1)} %collective-permute-done.23.refs_12_) | copy-start | bytes 1769476
  67.7 47.6 %collective-permute-start.14 = (bf16[144,2048]{1,0:T(8,128)(2,1)S(1)}, bf16[144,2048]{1,0:T(8,128)(2,1)}, u32[]{:S(2)}, u32[]{:S(2)}) collective-permute-start(bf16[144,2048]{1,0:T(8,128)(2,1)S(1)} %broadcast_select_fusion.1.refs_9_), channel_id=1, source_target_pairs={{8,12},{4,0},{9,13},{5,1},{10,14},{6,2},{11,15},{7,3},{24,28},{20,... | collective-permute-start | bytes 1769480 | tf_op jit(solution)/shard_map/ppermute | solution.py:546
  84.4 27.9 %copy-start.16 = (bf16[256,768]{1,0:T(8,128)(2,1)}, bf16[256,768]{1,0:T(8,128)(2,1)S(1)}, u32[]{:S(2)}) copy-start(bf16[256,768]{1,0:T(8,128)(2,1)S(1)} %collective-permute-done.1.refs_1_) | copy-start | bytes 1179652
  84.4 12.0 %collective-permute-start.2 = (bf16[256,768]{1,0:T(8,128)(2,1)S(1)}, bf16[256,768]{1,0:T(8,128)(2,1)S(1)}, u32[]{:S(2)}, u32[]{:S(2)}) collective-permute-start(bf16[256,768]{1,0:T(8,128)(2,1)S(1)} %collective-permute-done.1.refs_1_), channel_id=1, source_target_pairs={{0,16},{16,0},{1,17},{17,1},{2,18},{18,2},{3,19},{19,3},{4,20},{20... | collective-permute-start | bytes 1179656 | tf_op jit(solution)/shard_map/ppermute | solution.py:482
  90.8 7.2 %copy-start.17 = (bf16[256,768]{1,0:T(8,128)(2,1)}, bf16[256,768]{1,0:T(8,128)(2,1)S(1)}, u32[]{:S(2)}) copy-start(bf16[256,768]{1,0:T(8,128)(2,1)S(1)} %collective-permute-done.3.refs_3_) | copy-start | bytes 1179652
  90.8 13.4 %collective-permute-start.4 = (bf16[256,768]{1,0:T(8,128)(2,1)S(1)}, bf16[256,768]{1,0:T(8,128)(2,1)S(1)}, u32[]{:S(2)}, u32[]{:S(2)}) collective-permute-start(bf16[256,768]{1,0:T(8,128)(2,1)S(1)} %collective-permute-done.3.refs_3_), channel_id=1, source_target_pairs={{0,16},{16,0},{1,17},{17,1},{2,18},{18,2},{3,19},{19,3},{4,20},{20... | collective-permute-start | bytes 1179656 | tf_op jit(solution)/shard_map/ppermute | solution.py:482
  92.4 19.9 %copy-start.14 = (bf16[112,2048]{1,0:T(8,128)(2,1)}, bf16[112,2048]{1,0:T(8,128)(2,1)S(1)}, u32[]{:S(2)}) copy-start(bf16[112,2048]{1,0:T(8,128)(2,1)S(1)} %broadcast_select_fusion.2.refs_10_) | copy-start | bytes 1376260
  92.5 21.4 %collective-permute-start.27 = (bf16[112,2048]{1,0:T(8,128)(2,1)S(1)}, bf16[112,2048]{1,0:T(8,128)(2,1)}, u32[]{:S(2)}, u32[]{:S(2)}) collective-permute-start(bf16[112,2048]{1,0:T(8,128)(2,1)S(1)} %broadcast_select_fusion.2.refs_10_), channel_id=1, source_target_pairs={{0,2},{1,3},{2,0},{3,1},{4,6},{5,7},{6,4},{7,5},{8,10},{9,11},{10,... | collective-permute-start | bytes 1376264 | tf_op jit(solution)/shard_map/ppermute | solution.py:538
  93.5 10.7 %copy-start.18 = (bf16[256,768]{1,0:T(8,128)(2,1)}, bf16[256,768]{1,0:T(8,128)(2,1)S(1)}, u32[]{:S(2)}) copy-start(bf16[256,768]{1,0:T(8,128)(2,1)S(1)} %collective-permute-done.7.refs_8_) | copy-start | bytes 1179652
  93.5 18.9 %collective-permute-start.6 = (bf16[256,768]{1,0:T(8,128)(2,1)}, bf16[256,768]{1,0:T(8,128)(2,1)}, u32[]{:S(2)}, u32[]{:S(2)}) collective-permute-start(bf16[256,768]{1,0:T(8,128)(2,1)} %collective-permute-done.5.refs_5_), channel_id=1, source_target_pairs={{0,16},{16,0},{1,17},{17,1},{2,18},{18,2},{3,19},{19,3},{4,20},{20... | collective-permute-start | bytes 1179656 | tf_op jit(solution)/shard_map/ppermute | solution.py:482
  96.4 15.9 %copy-start.19 = (bf16[256,768]{1,0:T(8,128)(2,1)}, bf16[256,768]{1,0:T(8,128)(2,1)S(1)}, u32[]{:S(2)}) copy-start(bf16[256,768]{1,0:T(8,128)(2,1)S(1)} %collective-permute-done.2.refs_2_) | copy-start | bytes 1179652
  96.4 30.5 %collective-permute-start.26 = (bf16[144,2048]{1,0:T(8,128)(2,1)S(1)}, bf16[144,2048]{1,0:T(8,128)(2,1)}, u32[]{:S(2)}, u32[]{:S(2)}) collective-permute-start(bf16[144,2048]{1,0:T(8,128)(2,1)S(1)} %broadcast_select_fusion.1.refs_9_), channel_id=1, source_target_pairs={{0,2},{1,3},{2,0},{3,1},{4,6},{5,7},{6,4},{7,5},{8,10},{9,11},{10,... | collective-permute-start | bytes 1769480 | tf_op jit(solution)/shard_map/ppermute | solution.py:538
  104.9 21.9 %collective-permute-start.19 = (bf16[112,2048]{1,0:T(8,128)(2,1)S(1)}, bf16[112,2048]{1,0:T(8,128)(2,1)}, u32[]{:S(2)}, u32[]{:S(2)}) collective-permute-start(bf16[112,2048]{1,0:T(8,128)(2,1)S(1)} %broadcast_select_fusion.2.refs_10_), channel_id=1, source_target_pairs={{8,12},{4,0},{9,13},{5,1},{10,14},{6,2},{11,15},{7,3},{24,28},{20,... | collective-permute-start | bytes 1376264 | tf_op jit(solution)/shard_map/ppermute | solution.py:546
  112.4 23.9 %collective-permute-start.21 = (bf16[112,2048]{1,0:T(8,128)(2,1)S(1)}, bf16[112,2048]{1,0:T(8,128)(2,1)}, u32[]{:S(2)}, u32[]{:S(2)}) collective-permute-start(bf16[112,2048]{1,0:T(8,128)(2,1)S(1)} %collective-permute-done.12.refs_16_), channel_id=1, source_target_pairs={{4,6},{5,7},{6,4},{7,5},{8,10},{9,11},{10,8},{11,9},{20,22},{21,23... | collective-permute-start | bytes 1376264 | tf_op jit(solution)/shard_map/ppermute | solution.py:538
  113.9 22.7 %collective-permute-start.16 = (bf16[144,2048]{1,0:T(8,128)(2,1)S(1)}, bf16[144,2048]{1,0:T(8,128)(2,1)}, u32[]{:S(2)}, u32[]{:S(2)}) collective-permute-start(bf16[144,2048]{1,0:T(8,128)(2,1)S(1)} %collective-permute-done.8.refs_14_), channel_id=1, source_target_pairs={{4,6},{5,7},{6,4},{7,5},{8,10},{9,11},{10,8},{11,9},{20,22},{21,23... | collective-permute-start | bytes 1769480 | tf_op jit(solution)/shard_map/ppermute | solution.py:538
  115.3 26.6 %collective-permute-start.15 = (bf16[144,2048]{1,0:T(8,128)(2,1)}, bf16[144,2048]{1,0:T(8,128)(2,1)}, u32[]{:S(2)}, u32[]{:S(2)}) collective-permute-start(bf16[144,2048]{1,0:T(8,128)(2,1)} %collective-permute-done.14.refs_13_), channel_id=1, source_target_pairs={{0,2},{1,3},{2,0},{3,1},{12,14},{13,15},{14,12},{15,13},{16,18},{1... | collective-permute-start | bytes 1769480 | tf_op jit(solution)/shard_map/ppermute | solution.py:538
  126.8 34.4 %collective-permute-start.25 = (bf16[1024,384]{1,0:T(8,128)(2,1)}, bf16[1024,384]{1,0:T(8,128)(2,1)S(1)}, u32[]{:S(2)}, u32[]{:S(2)}) collective-permute-start(bf16[1024,384]{1,0:T(8,128)(2,1)} %get-tuple-element.31), channel_id=1, source_target_pairs={{0,1},{1,0},{2,3},{3,2},{4,5},{5,4},{6,7},{7,6},{8,9},{9,8},{10,11... | collective-permute-start | bytes 2359304 | tf_op jit(solution)/shard_map/ppermute | solution.py:479
  126.9 15.0 %collective-permute-start.20 = (bf16[112,2048]{1,0:T(8,128)(2,1)}, bf16[112,2048]{1,0:T(8,128)(2,1)S(1)}, u32[]{:S(2)}, u32[]{:S(2)}) collective-permute-start(bf16[112,2048]{1,0:T(8,128)(2,1)} %collective-permute-done.19.refs_15_), channel_id=1, source_target_pairs={{0,2},{1,3},{2,0},{3,1},{12,14},{13,15},{14,12},{15,13},{16,18},{1... | collective-permute-start | bytes 1376264 | tf_op jit(solution)/shard_map/ppermute | solution.py:538
  136.3 24.9 %collective-permute-start.28 = (bf16[768,384]{1,0:T(8,128)(2,1)}, bf16[768,384]{1,0:T(8,128)(2,1)S(1)}, u32[]{:S(2)}, u32[]{:S(2)}) collective-permute-start(bf16[768,384]{1,0:T(8,128)(2,1)} %get-tuple-element.33), channel_id=1, source_target_pairs={{0,1},{1,0},{2,3},{3,2},{4,5},{5,4},{6,7},{7,6},{8,9},{9,8},{10,11... | collective-permute-start | bytes 1769480 | tf_op jit(solution)/shard_map/ppermute | solution.py:479
  147.4 19.2 %collective-permute-start.22 = (bf16[256,384]{1,0:T(8,128)(2,1)}, bf16[256,384]{1,0:T(8,128)(2,1)S(1)}, u32[]{:S(2)}, u32[]{:S(2)}) collective-permute-start(bf16[256,384]{1,0:T(8,128)(2,1)} %get-tuple-element.28), channel_id=1, source_target_pairs={{0,1},{1,0},{2,3},{3,2},{4,5},{5,4},{6,7},{7,6},{8,9},{9,8},{10,11... | collective-permute-start | bytes 589832 | tf_op jit(solution)/shard_map/ppermute | solution.py:479
  147.5 13.3 %all-to-all-start = ((s32[4,1,512]{2,1,0:T(1,128)}), s32[4,1,512]{2,1,0:T(1,128)S(1)}, u32[]{:S(2)}, u32[]{:S(2)}) async-start(s32[4,1,512]{2,1,0:T(1,128)} %bitcast.29), calls=%async_computation | async-start | bytes 16384 | tf_op jit(solution)/shard_map/all_to_all | solution.py:507
  162.3 4.3 %copy-start.3 = (f32[256,384]{1,0:T(8,128)S(1)}, f32[256,384]{1,0:T(8,128)}, u32[]{:S(2)}) copy-start(f32[256,384]{1,0:T(8,128)} %get-tuple-element.27.kept_ref) | copy-start | bytes 1179652
  178.5 13.1 %copy-start.4 = (f32[4,64,128]{2,1,0:T(8,128)S(1)}, f32[4,64,128]{2,1,0:T(8,128)}, u32[]{:S(2)}) copy-start(f32[4,64,128]{2,1,0:T(8,128)} %refs_5_.1) | copy-start | bytes 393220
  178.5 8.6 %collective-permute-start.29 = (bf16[576,128]{1,0:T(8,128)(2,1)S(1)}, bf16[576,128]{1,0:T(8,128)(2,1)S(1)}, u32[]{:S(2)}, u32[]{:S(2)}) collective-permute-start(bf16[576,128]{1,0:T(8,128)(2,1)S(1)} %attend.5), channel_id=1, source_target_pairs={{0,4},{4,8},{8,12},{12,0},{1,5},{5,9},{9,13},{13,1},{2,6},{6,10},{... | collective-permute-start | bytes 442376 | tf_op jit(solution)/shard_map/ppermute | solution.py:485
  178.5 13.0 %collective-permute-start.30 = (bf16[576,128]{1,0:T(8,128)(2,1)S(1)}, bf16[576,128]{1,0:T(8,128)(2,1)S(1)}, u32[]{:S(2)}, u32[]{:S(2)}) collective-permute-start(bf16[576,128]{1,0:T(8,128)(2,1)S(1)} %attend.6), channel_id=1, source_target_pairs={{0,8},{4,12},{8,0},{12,4},{1,9},{5,13},{9,1},{13,5},{2,10},{6,14},... | collective-permute-start | bytes 442376 | tf_op jit(solution)/shard_map/ppermute | solution.py:485
  178.6 12.9 %collective-permute-start.31 = (bf16[576,128]{1,0:T(8,128)(2,1)S(1)}, bf16[576,128]{1,0:T(8,128)(2,1)S(1)}, u32[]{:S(2)}, u32[]{:S(2)}) collective-permute-start(bf16[576,128]{1,0:T(8,128)(2,1)S(1)} %attend.7), channel_id=1, source_target_pairs={{0,12},{4,0},{8,4},{12,8},{1,13},{5,1},{9,5},{13,9},{2,14},{6,2},{... | collective-permute-start | bytes 442376 | tf_op jit(solution)/shard_map/ppermute | solution.py:485
  (8 other events, 9.2 us)
